TPU v7x, 32 devices: a whole 2x2x4 slice. The times are simulated.
32 devices in a mesh: ctx: 8 (over y, x, core), fsdp: 4 (over z).
Axes of the slice: x: 2, y: 2, z: 4, core: 2. Of those that a mesh axis runs over, the one named last changes fastest.
Arguments:
- tokens: bfloat16 [4096, 1600], P(('fsdp', 'ctx')), may hold values from -6 to 6
- block_table: int32 [8, 2], replicated, may hold values from 0 to 15, as said below
- ln1_gain: bfloat16 [1600], P('fsdp'), may hold values from 0.099609375 to 1.8984375
- ln1_bias: bfloat16 [1600], P('fsdp'), may hold values from -1.75 to 1.75
- qkv_weight: bfloat16 [1600, 4800], P('fsdp'), may hold values from -0.15625 to 0.15625
- query_bias: bfloat16 [1600], P('fsdp'), may hold values from -3 to 3
- value_bias: bfloat16 [1600], P('fsdp'), may hold values from -0.875 to 0.875
- proj_weight: bfloat16 [1600, 1600], P('fsdp'), may hold values from -1.25 to 1.25
- proj_bias: bfloat16 [1600], P('fsdp'), may hold values from -1.75 to 1.75
- ln2_gain: bfloat16 [1600], P('fsdp'), may hold values from 0.099609375 to 1.8984375
- ln2_bias: bfloat16 [1600], P('fsdp'), may hold values from -1.75 to 1.75
- fc_weight: bfloat16 [1600, 6400], P('fsdp'), may hold values from -0.15625 to 0.15625
- fc_bias: bfloat16 [6400], P('fsdp'), may hold values from -3 to 3
- out_weight: bfloat16 [6400, 1600], P('fsdp'), may hold values from -0.078125 to 0.078125
- out_bias: bfloat16 [1600], P('fsdp'), may hold values from -1.75 to 1.75
- cotangent: bfloat16 [4096, 1600], P(('fsdp', 'ctx')), may hold values from -6 to 6
Outputs:
- layer_out: bfloat16 [4096, 1600], P(('fsdp', 'ctx'))
- grad_tokens: bfloat16 [4096, 1600], P(('fsdp', 'ctx'))
- grad_ln1_gain: float32 [1600], P('fsdp')
- grad_ln1_bias: float32 [1600], P('fsdp')
- grad_qkv_weight: float32 [1600, 4800], P('fsdp')
- grad_query_bias: float32 [1600], P('fsdp')
- grad_value_bias: float32 [1600], P('fsdp')
- grad_proj_weight: float32 [1600, 1600], P('fsdp')
- grad_proj_bias: float32 [1600], P('fsdp')
- grad_ln2_gain: float32 [1600], P('fsdp')
- grad_ln2_bias: float32 [1600], P('fsdp')
- grad_fc_weight: float32 [1600, 6400], P('fsdp')
- grad_fc_bias: float32 [6400], P('fsdp')
- grad_out_weight: float32 [6400, 1600], P('fsdp')
- grad_out_bias: float32 [1600], P('fsdp')
Inputs may be any that keep to these rules, and one draw needn't show every extreme that they name: `block_table`: row i is (p_i, 15 - p_i) with p_i below 8; every block number appears exactly once.
All inputs are finite; a program needn't handle non-finite values.
Results may differ from a plain program's by a relative error of at most 0.02.
Values may be sent and summed in bfloat16 or wider, within the bound.
A program may use at most 256 MiB of HBM per device.

v0:
```python
import math

import jax
import jax.numpy as jnp
from jax import lax
from jax.sharding import PartitionSpec as P

HEADS = 25


def layer_norm(values, gain_vec, shift_vec):
    centre = values - jnp.mean(values, axis=-1, keepdims=True)
    spread = jnp.mean(centre * centre, axis=-1, keepdims=True)
    return centre * lax.rsqrt(spread + 1e-05) * gain_vec + shift_vec


def gelu_tanh(values):
    return jax.nn.gelu(values, approximate=True)


def body(
    tokens,
    block_table,
    ln1_gain,
    ln1_bias,
    qkv_weight,
    query_bias,
    value_bias,
    proj_weight,
    proj_bias,
    ln2_gain,
    ln2_bias,
    fc_weight,
    fc_bias,
    out_weight,
    out_bias,
    cotangent,
):
    row_count = tokens.shape[0]
    model_width = tokens.shape[1]
    block_rows = row_count // 2
    head_dim = model_width // HEADS
    score_scale = head_dim ** (-0.5)
    ctx_index = lax.axis_index("ctx")
    own_blocks = lax.dynamic_slice_in_dim(block_table, ctx_index, 1, 0).reshape(-1)
    offsets = jnp.arange(block_rows, dtype=jnp.int32)
    query_pos = (own_blocks[:, None] * block_rows + offsets[None, :]).reshape(-1)
    key_pos = (block_table.reshape(-1)[:, None] * block_rows + offsets[None, :]).reshape(-1)
    seq_len = key_pos.shape[0]
    key_block = math.gcd(seq_len, 512)
    block_count = seq_len // key_block
    pos_blocks = key_pos.reshape(block_count, key_block)
    gain_one, shift_one, qkv_full, q_bias, v_bias, proj_full, proj_b = (
        lax.all_gather(ln1_gain, "fsdp", axis=0, tiled=True),
        lax.all_gather(ln1_bias, "fsdp", axis=0, tiled=True),
        lax.all_gather(qkv_weight, "fsdp", axis=0, tiled=True),
        lax.all_gather(query_bias, "fsdp", axis=0, tiled=True),
        lax.all_gather(value_bias, "fsdp", axis=0, tiled=True),
        lax.all_gather(proj_weight, "fsdp", axis=0, tiled=True),
        lax.all_gather(proj_bias, "fsdp", axis=0, tiled=True),
    )
    inputs = tokens.astype(jnp.float32)
    gain_one_f = gain_one.astype(jnp.float32)
    shift_one_f = shift_one.astype(jnp.float32)
    normed_one = layer_norm(inputs, gain_one_f, shift_one_f).astype(jnp.bfloat16)
    bias_row = jnp.concatenate([q_bias, jnp.zeros_like(q_bias), v_bias]).astype(jnp.float32)
    joined = jnp.dot(normed_one, qkv_full, preferred_element_type=jnp.float32) + bias_row
    query_rows = joined[:, :model_width].astype(jnp.bfloat16).reshape(row_count, HEADS, head_dim)
    key_local = joined[:, model_width : 2 * model_width].astype(jnp.bfloat16)
    value_local = joined[:, 2 * model_width :].astype(jnp.bfloat16)
    key_all, value_all = (
        lax.all_gather(key_local, "ctx", axis=0, tiled=True),
        lax.all_gather(value_local, "ctx", axis=0, tiled=True),
    )

    def scores_of(key_tile, pos_tile):
        raw_scores = jnp.einsum(
            "qhd,khd->hqk", query_rows, key_tile, preferred_element_type=jnp.float32
        )
        allowed = pos_tile[None, :] <= query_pos[:, None]
        return (jnp.where(allowed[None], raw_scores * score_scale, -1e30), allowed)

    key_tiles = key_all.reshape(block_count, key_block, HEADS, head_dim)
    value_tiles = value_all.reshape(block_count, key_block, HEADS, head_dim)

    def stat_step(carried, tile_set):
        top_prev, total_prev = carried
        scores, allowed = scores_of(tile_set[0], tile_set[1])
        top_new = jnp.maximum(top_prev, jnp.max(scores, axis=-1))
        total_new = total_prev * jnp.exp(top_prev - top_new) + jnp.sum(
            jnp.exp(scores - top_new[..., None]), axis=-1
        )
        return ((top_new, total_new), None)

    start_stats = (
        jnp.full((HEADS, row_count), -1e30, jnp.float32),
        jnp.zeros((HEADS, row_count), jnp.float32),
    )
    (top_all, total_all), _ = lax.scan(stat_step, start_stats, (key_tiles, pos_blocks))
    log_total = top_all + jnp.log(total_all)

    def out_step(summed, tile_set):
        scores, allowed = scores_of(tile_set[0], tile_set[2])
        soft_w = jnp.exp(scores - log_total[..., None]).astype(jnp.bfloat16)
        return (
            summed
            + jnp.einsum("hqk,khd->qhd", soft_w, tile_set[1], preferred_element_type=jnp.float32),
            None,
        )

    heads_f, _ = lax.scan(
        out_step,
        jnp.zeros((row_count, HEADS, head_dim), jnp.float32),
        (key_tiles, value_tiles, pos_blocks),
    )
    heads_low = heads_f.reshape(row_count, model_width).astype(jnp.bfloat16)
    middle = (
        inputs
        + jnp.dot(heads_low, proj_full, preferred_element_type=jnp.float32)
        + proj_b.astype(jnp.float32)
    )
    fsdp_count = lax.axis_size("fsdp")
    width_share = model_width // fsdp_count
    small_stack = jnp.stack([ln2_gain, ln2_bias, out_bias], axis=1)
    small_tiled = jnp.tile(small_stack, (1, fsdp_count))
    fc_cols, small_full = (
        lax.all_to_all(fc_weight, "fsdp", split_axis=1, concat_axis=0, tiled=True),
        lax.all_to_all(small_tiled, "fsdp", split_axis=1, concat_axis=0, tiled=True),
    )
    gain_two_f = small_full[:, 0].astype(jnp.float32)
    shift_two_f = small_full[:, 1].astype(jnp.float32)
    out_b_f = small_full[:, 2].astype(jnp.float32)
    normed_two = layer_norm(middle, gain_two_f, shift_two_f).astype(jnp.bfloat16)
    group_normed, group_upstream = (
        lax.all_gather(normed_two, "fsdp", axis=0, tiled=True),
        lax.all_gather(cotangent, "fsdp", axis=0, tiled=True),
    )
    hidden_pre = jnp.dot(
        group_normed, fc_cols, preferred_element_type=jnp.float32
    ) + fc_bias.astype(jnp.float32)
    hidden = gelu_tanh(hidden_pre).astype(jnp.bfloat16)
    rows = hidden
    summed_out = lax.psum_scatter(
        jnp.dot(rows, out_weight, preferred_element_type=jnp.float32).astype(jnp.bfloat16),
        "fsdp",
        scatter_dimension=0,
        tiled=True,
    ).astype(jnp.float32)
    output = middle + summed_out + out_b_f
    out_rows = output.astype(jnp.bfloat16)
    owned_ow = jnp.einsum("tf,td->fd", hidden, group_upstream, preferred_element_type=jnp.float32)
    full_out_b = jnp.sum(group_upstream.astype(jnp.float32), axis=0)
    owned_ob = lax.dynamic_slice_in_dim(
        full_out_b, lax.axis_index("fsdp") * width_share, width_share, 0
    )
    grad_hidden = jnp.einsum(
        "td,fd->tf", group_upstream, out_weight, preferred_element_type=jnp.float32
    )
    _, gelu_pull = jax.vjp(gelu_tanh, hidden_pre)
    grad_pre = gelu_pull(grad_hidden)[0].astype(jnp.bfloat16)
    grad_fc_cols = jnp.einsum(
        "tc,tf->cf", group_normed, grad_pre, preferred_element_type=jnp.float32
    )
    owned_fcb = jnp.sum(grad_pre.astype(jnp.float32), axis=0)
    rows = grad_pre
    grad_normed_two = lax.psum_scatter(
        jnp.einsum("tf,cf->tc", rows, fc_cols, preferred_element_type=jnp.float32).astype(
            jnp.bfloat16
        ),
        "fsdp",
        scatter_dimension=0,
        tiled=True,
    ).astype(jnp.float32)
    _, norm_pull_two = jax.vjp(layer_norm, middle, gain_two_f, shift_two_f)
    grad_mid_norm, grad_gain_two, grad_shift_two = norm_pull_two(grad_normed_two)
    grad_middle = cotangent.astype(jnp.float32) + grad_mid_norm
    norm_pair = jnp.stack([grad_gain_two, grad_shift_two], axis=1)
    owned_fcw, norm_parts = (
        lax.all_to_all(
            grad_fc_cols.astype(jnp.bfloat16), "fsdp", split_axis=0, concat_axis=1, tiled=True
        ).astype(grad_fc_cols.dtype),
        lax.all_to_all(
            norm_pair.astype(jnp.bfloat16), "fsdp", split_axis=0, concat_axis=1, tiled=True
        ).astype(norm_pair.dtype),
    )
    norm_sums = jnp.sum(norm_parts.reshape(width_share, fsdp_count, 2), axis=1)
    owned_g2 = norm_sums[:, 0]
    owned_b2 = norm_sums[:, 1]
    total_g2, total_b2, total_fcw, total_fcb, total_ow, total_ob = (
        lax.psum(owned_g2.astype(jnp.bfloat16), "ctx").astype(jnp.float32),
        lax.psum(owned_b2.astype(jnp.bfloat16), "ctx").astype(jnp.float32),
        lax.psum(owned_fcw.astype(jnp.bfloat16), "ctx").astype(jnp.float32),
        lax.psum(owned_fcb.astype(jnp.bfloat16), "ctx").astype(jnp.float32),
        lax.psum(owned_ow.astype(jnp.bfloat16), "ctx").astype(jnp.float32),
        lax.psum(owned_ob.astype(jnp.bfloat16), "ctx").astype(jnp.float32),
    )
    grad_branch = grad_middle.astype(jnp.bfloat16)
    grad_proj_w = jnp.einsum(
        "tc,td->cd", heads_low, grad_branch, preferred_element_type=jnp.float32
    )
    grad_proj_b = jnp.sum(grad_branch.astype(jnp.float32), axis=0)
    grad_heads = jnp.einsum(
        "td,cd->tc", grad_branch, proj_full, preferred_element_type=jnp.float32
    ).astype(jnp.bfloat16)
    grad_heads_split = grad_heads.reshape(row_count, HEADS, head_dim)
    delta_rows = jnp.sum(grad_heads_split.astype(jnp.float32) * heads_f, axis=-1).T

    def grad_step(grad_query, tile_set):
        key_tile, value_tile, pos_tile = tile_set
        scores, allowed = scores_of(key_tile, pos_tile)
        soft_w = jnp.exp(scores - log_total[..., None])
        grad_soft = jnp.einsum(
            "qhd,khd->hqk", grad_heads_split, value_tile, preferred_element_type=jnp.float32
        )
        grad_raw = jnp.where(
            allowed[None], soft_w * (grad_soft - delta_rows[..., None]) * score_scale, 0.0
        ).astype(jnp.bfloat16)
        grad_query = grad_query + jnp.einsum(
            "hqk,khd->qhd", grad_raw, key_tile, preferred_element_type=jnp.float32
        )
        grad_key = jnp.einsum(
            "hqk,qhd->khd", grad_raw, query_rows, preferred_element_type=jnp.float32
        )
        grad_value = jnp.einsum(
            "hqk,qhd->khd",
            soft_w.astype(jnp.bfloat16),
            grad_heads_split,
            preferred_element_type=jnp.float32,
        )
        return (grad_query, (grad_key, grad_value))

    grad_query, (key_grads, value_grads) = lax.scan(
        grad_step,
        jnp.zeros((row_count, HEADS, head_dim), jnp.float32),
        (key_tiles, value_tiles, pos_blocks),
    )
    key_terms = key_grads.reshape(seq_len, model_width)
    value_terms = value_grads.reshape(seq_len, model_width)
    key_mine, value_mine = (
        lax.psum_scatter(
            key_terms.astype(jnp.bfloat16), "ctx", scatter_dimension=0, tiled=True
        ).astype(jnp.float32),
        lax.psum_scatter(
            value_terms.astype(jnp.bfloat16), "ctx", scatter_dimension=0, tiled=True
        ).astype(jnp.float32),
    )
    grad_joined = jnp.concatenate(
        [grad_query.reshape(row_count, model_width), key_mine, value_mine], axis=1
    ).astype(jnp.bfloat16)
    grad_q_bias = jnp.sum(grad_joined[:, :model_width].astype(jnp.float32), axis=0)
    grad_v_bias = jnp.sum(grad_joined[:, 2 * model_width :].astype(jnp.float32), axis=0)
    grad_qkv_w = jnp.einsum(
        "tc,tk->ck", normed_one, grad_joined, preferred_element_type=jnp.float32
    )
    grad_normed_one = jnp.einsum(
        "tk,ck->tc", grad_joined, qkv_full, preferred_element_type=jnp.float32
    )
    _, norm_pull_one = jax.vjp(layer_norm, inputs, gain_one_f, shift_one_f)
    grad_in_norm, grad_gain_one, grad_shift_one = norm_pull_one(grad_normed_one)
    grad_inputs = (grad_middle + grad_in_norm).astype(jnp.bfloat16)
    owned_g1, owned_b1, owned_qkv, owned_qb, owned_vb, owned_pw, owned_pb = (
        lax.psum_scatter(
            grad_gain_one.astype(jnp.bfloat16), "fsdp", scatter_dimension=0, tiled=True
        ).astype(jnp.float32),
        lax.psum_scatter(
            grad_shift_one.astype(jnp.bfloat16), "fsdp", scatter_dimension=0, tiled=True
        ).astype(jnp.float32),
        lax.psum_scatter(
            grad_qkv_w.astype(jnp.bfloat16), "fsdp", scatter_dimension=0, tiled=True
        ).astype(jnp.float32),
        lax.psum_scatter(
            grad_q_bias.astype(jnp.bfloat16), "fsdp", scatter_dimension=0, tiled=True
        ).astype(jnp.float32),
        lax.psum_scatter(
            grad_v_bias.astype(jnp.bfloat16), "fsdp", scatter_dimension=0, tiled=True
        ).astype(jnp.float32),
        lax.psum_scatter(
            grad_proj_w.astype(jnp.bfloat16), "fsdp", scatter_dimension=0, tiled=True
        ).astype(jnp.float32),
        lax.psum_scatter(
            grad_proj_b.astype(jnp.bfloat16), "fsdp", scatter_dimension=0, tiled=True
        ).astype(jnp.float32),
    )
    total_g1, total_b1, total_qkv, total_qb, total_vb, total_pw, total_pb = (
        lax.psum(owned_g1.astype(jnp.bfloat16), "ctx").astype(jnp.float32),
        lax.psum(owned_b1.astype(jnp.bfloat16), "ctx").astype(jnp.float32),
        lax.psum(owned_qkv.astype(jnp.bfloat16), "ctx").astype(jnp.float32),
        lax.psum(owned_qb.astype(jnp.bfloat16), "ctx").astype(jnp.float32),
        lax.psum(owned_vb.astype(jnp.bfloat16), "ctx").astype(jnp.float32),
        lax.psum(owned_pw.astype(jnp.bfloat16), "ctx").astype(jnp.float32),
        lax.psum(owned_pb.astype(jnp.bfloat16), "ctx").astype(jnp.float32),
    )
    return (
        out_rows,
        grad_inputs,
        total_g1,
        total_b1,
        total_qkv,
        total_qb,
        total_vb,
        total_pw,
        total_pb,
        total_g2,
        total_b2,
        total_fcw,
        total_fcb,
        total_ow,
        total_ob,
    )


def solution(mesh):
    placed = (
        P(("fsdp", "ctx"), None),
        P(),
        P("fsdp"),
        P("fsdp"),
        P("fsdp", None),
        P("fsdp"),
        P("fsdp"),
        P("fsdp", None),
        P("fsdp"),
        P("fsdp"),
        P("fsdp"),
        P("fsdp", None),
        P("fsdp"),
        P("fsdp", None),
        P("fsdp"),
        P(("fsdp", "ctx"), None),
    )
    return jax.shard_map(
        body,
        mesh=mesh,
        in_specs=placed,
        out_specs=(
            P(("fsdp", "ctx"), None),
            P(("fsdp", "ctx"), None),
            P("fsdp"),
            P("fsdp"),
            P("fsdp", None),
            P("fsdp"),
            P("fsdp"),
            P("fsdp", None),
            P("fsdp"),
            P("fsdp"),
            P("fsdp"),
            P("fsdp", None),
            P("fsdp"),
            P("fsdp", None),
            P("fsdp"),
        ),
        check_vma=False,
    )
```

profile of v0, /device:TPU:0, one launch (start us, length us, event | category | flops | bytes accessed | tf_op | source)
XLA Modules:
  0.0 1569.6 jit_solution(5104515425968146760)
XLA Ops:
  10.6 21.1 %all-reduce.13 = (bf16[1600]{0:T(1024)(128)(2,1)S(1)}, bf16[1600]{0:T(1024)(128)(2,1)S(1)}, bf16[1600]{0:T(1024)(128)(2,1)S(1)}, bf16[1600]{0:T(1024)(128)(2,1)S(1)}, bf16[1600]{0:T(1024)(128)(2,1)S(1)}) all-reduce(bf16[1600]{0:T(1024)(128)(2,1)S(1)} %dynamic-update-slice.2, ...), channel_id=1, replica_groups=mesh['ctx'=8,'fsdp'=4] {'fsdp'}, use_global_device_ids=true, to_apply=%add.2 | all-reduce | flops 8000 | bytes 32000
  32.8 246.5 %all-gather.7.cloned.1.call-done = bf16[1600,4800]{1,0:T(8,128)(2,1)} async-done(((bf16[400,4800]{1,0:T(8,128)(2,1)}), bf16[1600,4800]{1,0:T(8,128)(2,1)}) %all-gather.7.cloned.1.call-update) | async-done | bytes 15360016 | tf_op jit(solution)/shard_map/all_gather | solution.py:56
  279.4 12.1 fusion.80
  299.0 11.7 all_to_all.51
  310.7 5.9 copy.78
  316.8 5.1 all-to-all-start.1
  324.4 8.5 reshape.304
  335.8 19.6 %while.39 = (s32[]{:T(128)}, f32[25,128]{1,0:T(8,128)S(1)}, f32[25,128]{1,0:T(8,128)S(1)}, s32[2,512]{1,0:T(2,128)S(1)}, bf16[2,512,25,64]{1,3,2,0:T(8,128)(2,1)...) while((s32[]{:T(128)}, f32[25,128]{1,0:T(8,128)S(1)}, ...), condition=%wide.region_5.6_spmd.clone, body=%wide.region_2.5_spmd.clone.sunk | while | flops 221265664 | bytes 15526528 | solution.py:99
  336.1 5.2 fusion.175
  345.9 5.2 fusion.175
  355.3 4.9 all-gather.9.cloned.1.call-done
  360.2 8.5 reshape.303
  368.7 4.8 copy.75
  373.5 21.0 %while.40 = (s32[]{:T(128)}, f32[128,25,64]{0,2,1:T(8,128)}, bf16[2,512,25,64]{1,3,2,0:T(8,128)(2,1)}, s32[2,512]{1,0:T(2,128)S(1)}, bf16[2,512,25,64]{1,3,2,0:T...) while((s32[]{:T(128)}, f32[128,25,64]{0,2,1:T(8,128)}, ...), condition=%wide.region_7.8_spmd.clone, body=%wide.region_6.7_spmd.clone.sunk | while | flops 426459264 | bytes 5482114 | solution.py:111
  373.8 4.7 fusion.181
  378.8 5.0 fusion.181
  396.5 129.3 %all-gather.13.cloned.1.call-done = bf16[1600,1600]{1,0:T(8,128)(2,1)} async-done(((bf16[400,1600]{1,0:T(8,128)(2,1)}), bf16[1600,1600]{1,0:T(8,128)(2,1)}) %all-gather.13.cloned.1.call-update) | async-done | bytes 5120016 | tf_op jit(solution)/shard_map/all_gather | solution.py:59
  525.8 5.0 fusion.125
  533.0 31.9 %all-gather.17.cloned.1.call-done = bf16[512,1600]{0,1:T(8,128)(2,1)} async-done(((bf16[128,1600]{0,1:T(8,128)(2,1)}), bf16[512,1600]{0,1:T(8,128)(2,1)}) %all-gather.17.cloned.1.call-update) | async-done | bytes 1638416 | tf_op jit(solution)/shard_map/all_gather | solution.py:136
  564.9 7.9 fusion.126
  572.8 31.1 %all-gather.15.cloned.1.call-done = bf16[512,1600]{0,1:T(8,128)(2,1)} async-done(((bf16[128,1600]{0,1:T(8,128)(2,1)}), bf16[512,1600]{0,1:T(8,128)(2,1)}) %all-gather.15.cloned.1.call-update) | async-done | bytes 1638416 | tf_op jit(solution)/shard_map/all_gather | solution.py:135
  603.9 11.7 fusion.118
  616.8 6.7 convolution_convert_fusion.4
  627.1 35.8 %reduce-scatter.21.cloned.1.call-done = bf16[128,1600]{1,0:T(8,128)(2,1)} async-done(((bf16[512,1600]{1,0:T(8,128)(2,1)}), bf16[128,1600]{1,0:T(8,128)(2,1)}) %reduce-scatter.21.cloned.1.call-update) | async-done | bytes 409616
  675.4 49.1 %while.41 = (s32[]{:T(128)}, f32[128,25,64]{0,2,1:T(8,128)}, bf16[2,512,25,64]{1,3,2,0:T(8,128)(2,1)}, bf16[2,512,25,64]{1,3,2,0:T(8,128)(2,1)}, bf16[2,512,25,6...) while((s32[]{:T(128)}, f32[128,25,64]{0,2,1:T(8,128)}, ...), condition=%wide.region_16.17_spmd.clone, body=%wide.region_15.16_spmd.clone.sunk | while | flops 1068712064 | bytes 150980000 | solution.py:232
  675.8 5.2 fusion.192
  681.3 6.4 fusion.193
  700.1 5.1 fusion.192
  705.5 6.4 fusion.193
  724.5 5.3 copy.82
  750.5 30.1 %reduce-scatter.25.cloned.1.call-done = bf16[128,1600]{1,0:T(8,128)(2,1)} async-done(((bf16[1024,1600]{1,0:T(8,128)(2,1)}), bf16[128,1600]{1,0:T(8,128)(2,1)}) %reduce-scatter.25.cloned.1.call-update) | async-done | bytes 409616
  781.9 50.1 %reduce-scatter.23.cloned.1.call-done = bf16[128,1600]{1,0:T(8,128)(2,1)} async-done(((bf16[1024,1600]{1,0:T(8,128)(2,1)}), bf16[128,1600]{1,0:T(8,128)(2,1)}) %reduce-scatter.23.cloned.1.call-update) | async-done | bytes 409616
  833.4 8.5 convolution_convert_fusion
  843.3 6.3 convolution_convert_fusion.2
  849.6 5.1 all-to-all-start.3
  855.0 8.0 convolution_convert_fusion.5
  866.8 8.1 convolution_convert_fusion.1
  874.9 176.1 %all-to-all-done.3 = bf16[4,400,1600]{2,1,0:T(8,128)(2,1)} async-done(((bf16[4,400,1600]{2,1,0:T(8,128)(2,1)}), bf16[4,400,1600]{2,1,0:T(8,128)(2,1)}, u32[]{:S(2)}, u32[]{:S(2)}) %all-to-all-start.3) | async-done | bytes 5120032 | tf_op jit(solution)/shard_map/all_to_all | solution.py:179
  1051.0 6.9 copy.84
  1057.9 9.8 all_to_all.59
  1067.8 228.2 %reduce-scatter.15.cloned.1.call-done = bf16[400,4800]{1,0:T(8,128)(2,1)} async-done(((bf16[1600,4800]{1,0:T(8,128)(2,1)}), bf16[400,4800]{1,0:T(8,128)(2,1)}) %reduce-scatter.15.cloned.1.call-update) | async-done | bytes 3840016 | tf_op jit(solution)/shard_map/reduce_scatter | solution.py:268
  1301.9 33.4 %reduce-scatter.19.cloned.1.call-done = bf16[128,1600]{1,0:T(8,128)(2,1)} async-done(((bf16[512,1600]{1,0:T(8,128)(2,1)}), bf16[128,1600]{1,0:T(8,128)(2,1)}) %reduce-scatter.19.cloned.1.call-update) | async-done | bytes 409616
  1336.7 9.3 fusion.117
  1346.6 16.9 %all-reduce.12 = (bf16[1600]{0:T(1024)(128)(2,1)S(1)}, bf16[1600]{0:T(1024)(128)(2,1)S(1)}, bf16[1600]{0:T(1024)(128)(2,1)S(1)}, bf16[1600]{0:T(1024)(128)(2,1)S(1)}, bf16[1600]{0:T(1024)(128)(2,1)S(1)}) all-reduce(bf16[1600]{0:T(1024)(128)(2,1)S(1)} %get-tuple-element.374, ...), channel_id=6, replica_groups=mesh['ctx'=8,'fsdp'=4] {'fsdp'}, use_global_device_ids=true, to_apply=%region_22.23.clone | all-reduce | flops 8000 | bytes 32000
  1363.9 24.1 %all-reduce.10 = (bf16[400]{0:T(512)(128)(2,1)S(1)}, bf16[400]{0:T(512)(128)(2,1)S(1)}, bf16[400]{0:T(512)(128)(2,1)S(1)}, bf16[400]{0:T(512)(128)(2,1)S(1)}, bf...) all-reduce(bf16[400]{0:T(512)(128)(2,1)S(1)} %dynamic-slice.6, ...), channel_id=1, replica_groups=mesh['ctx'=8,'fsdp'=4] {'ctx'}, use_global_device_ids=true, to_apply=%region_23.24 | all-reduce | flops 4800 | bytes 19200 | tf_op jit(solution)/shard_map/psum | solution.py:285
  1395.2 150.3 %all-reduce.16.cloned.1.call-done = (bf16[400,4800]{1,0:T(8,128)(2,1)}, bf16[400,1600]{1,0:T(8,128)(2,1)}, bf16[400,6400]{1,0:T(8,128)(2,1)}, bf16[1600,1600]{1,0:T(8,128)(2,1)}) async-done(((bf16[400,4800]{1,0:T(8,128)(2,1)}, bf16[400,1600]{1,0:T(8,128)(2,1)}, bf16[400,6400]{1,0:T(8,128)(2,1)}, bf16[1600,1600]{1,0:T(8,128)(2,1)}), (bf16[400,4800]{1,0:T(8,128)(2,1)}, bf16[400,1600]{1,0:T(8,128)(2,1)}, ...) | async-done | bytes 15360016 | tf_op jit(solution)/shard_map/psum | solution.py:287
  1545.5 6.0 convert_element_type.266
  1557.9 4.8 convert_element_type.281
  (307 shorter events, 122.6 us)
Async XLA Ops:
  7.2 24.6 %copy-start.7 = (bf16[128,1600]{0,1:T(8,128)(2,1)S(1)}, bf16[128,1600]{0,1:T(8,128)(2,1)}, u32[]{:S(2)}) copy-start(bf16[128,1600]{0,1:T(8,128)(2,1)} %param.22) | copy-start | bytes 1228804
  7.3 272.1 %all-gather.7.cloned.1.call-start = ((), (), s32[]{:S(2)}) async-start(), calls=%async_computation.10 | async-start | bytes 19456000 | tf_op jit(solution)/shard_map/all_gather | solution.py:56
  8.0 316.4 %all-gather.11.cloned.1.call-start = ((), (), s32[]{:S(2)}) async-start(), calls=%async_computation.12 | async-start | bytes 3686400 | tf_op jit(solution)/shard_map/all_gather | solution.py:72
  31.7 259.8 %copy-start.28 = (f32[1600]{0:T(1024)}, f32[1600]{0:T(1024)S(1)}, u32[]{:S(2)}) copy-start(f32[1600]{0:T(1024)S(1)} %convert_element_type.230) | copy-start | bytes 19204
  31.8 259.7 %copy-start.30 = (f32[1600]{0:T(1024)}, f32[1600]{0:T(1024)S(1)}, u32[]{:S(2)}) copy-start(f32[1600]{0:T(1024)S(1)} %convert_element_type.231) | copy-start | bytes 19204
  32.1 259.4 %copy-start.33 = (f32[128]{0:T(128)}, f32[128]{0:T(128)S(1)}, u32[]{:S(2)}) copy-start(f32[128]{0:T(128)S(1)} %broadcast_multiply_fusion.2) | copy-start | bytes 1540
  32.8 258.7 %copy-start.35 = (f32[128]{0:T(128)}, f32[128]{0:T(128)S(1)}, u32[]{:S(2)}) copy-start(f32[128]{0:T(128)S(1)} %fusion.110) | copy-start | bytes 1540
  291.6 7.0 copy-start.39
  292.7 67.6 %all-gather.9.cloned.1.call-start = ((), (), s32[]{:S(2)}) async-start(), calls=%async_computation.11 | async-start | bytes 3686400 | tf_op jit(solution)/shard_map/all_gather | solution.py:73
  293.4 232.4 %all-gather.13.cloned.1.call-start = ((), (), s32[]{:S(2)}) async-start(), calls=%async_computation.13 | async-start | bytes 6656000 | tf_op jit(solution)/shard_map/all_gather | solution.py:59
  294.7 22.1 %all-to-all-start = ((bf16[400,4,3]{0,2,1:T(4,128)(2,1)}), bf16[400,4,3]{0,2,1:T(4,128)(2,1)S(1)}, u32[]{:S(2)}, u32[]{:S(2)}) async-start(bf16[400,4,3]{0,2,1:T(4,128)(2,1)} %tile.2), calls=%async_computation | async-start | bytes 32768 | tf_op jit(solution)/shard_map/all_to_all | solution.py:128
  297.9 267.0 %all-gather.17.cloned.1.call-start = ((), (), s32[]{:S(2)}) async-start(), calls=%async_computation.15 | async-start | bytes 2048000 | tf_op jit(solution)/shard_map/all_gather | solution.py:136
  316.8 256.0 %all-to-all-start.1 = ((bf16[400,4,1600]{2,0,1:T(8,128)(2,1)}), bf16[400,4,1600]{2,0,1:T(8,128)(2,1)}, u32[]{:S(2)}, u32[]{:S(2)}) async-start(bf16[400,4,1600]{2,0,1:T(8,128)(2,1)} %copy.78), calls=%async_computation.1 | async-start | bytes 10649600 | tf_op jit(solution)/shard_map/all_to_all | solution.py:127
  321.9 282.0 %all-gather.15.cloned.1.call-start = ((), (), s32[]{:S(2)}) async-start(), calls=%async_computation.14 | async-start | bytes 2048000 | tf_op jit(solution)/shard_map/all_gather | solution.py:135
  525.8 7.2 copy-start.37
  532.9 130.0 %reduce-scatter.21.cloned.1.call-start = ((), (), s32[]{:S(2)}) async-start(), calls=%async_computation.19 | async-start | bytes 2129920
  627.1 153.6 %reduce-scatter.25.cloned.1.call-start = ((), (), s32[]{:S(2)}) async-start(), calls=%async_computation.21 | async-start | bytes 3833856
  675.8 5.2 copy-start
  692.3 6.0 copy-start.13
  700.1 5.2 copy-start
  712.0 4.8 copy-start.15
  716.8 6.0 copy-start.13
  734.3 97.8 %reduce-scatter.23.cloned.1.call-start = ((), (), s32[]{:S(2)}) async-start(), calls=%async_computation.20 | async-start | bytes 3833856
  744.0 323.8 %reduce-scatter.17.cloned.1.call-start = ((), (), s32[]{:S(2)}) async-start(), calls=%async_computation.17 | async-start | bytes 6656000 | tf_op jit(solution)/shard_map/reduce_scatter | solution.py:277
  749.1 84.2 %copy-start.8 = (bf16[128,1600]{0,1:T(8,128)(2,1)S(1)}, bf16[128,1600]{0,1:T(8,128)(2,1)}, u32[]{:S(2)}) copy-start(bf16[128,1600]{0,1:T(8,128)(2,1)} %param.22) | copy-start | bytes 1228804
  749.1 84.2 %copy-start.29 = (f32[1600]{0:T(1024)S(1)}, f32[1600]{0:T(1024)}, u32[]{:S(2)}) copy-start(f32[1600]{0:T(1024)} %copy-done.28) | copy-start | bytes 19204
  749.1 84.2 %copy-start.31 = (f32[1600]{0:T(1024)S(1)}, f32[1600]{0:T(1024)}, u32[]{:S(2)}) copy-start(f32[1600]{0:T(1024)} %copy-done.30) | copy-start | bytes 19204
  749.1 84.2 %copy-start.34 = (f32[128]{0:T(128)S(1)}, f32[128]{0:T(128)}, u32[]{:S(2)}) copy-start(f32[128]{0:T(128)} %copy-done.33) | copy-start | bytes 1540
  749.1 84.2 %copy-start.36 = (f32[128]{0:T(128)S(1)}, f32[128]{0:T(128)}, u32[]{:S(2)}) copy-start(f32[128]{0:T(128)} %copy-done.35) | copy-start | bytes 1540
  749.1 546.8 %reduce-scatter.15.cloned.1.call-start = ((), (), s32[]{:S(2)}) async-start(), calls=%async_computation.16 | async-start | bytes 19456000 | tf_op jit(solution)/shard_map/reduce_scatter | solution.py:268
  750.5 91.3 %copy-start.21 = (bf16[128,25,64]{0,2,1:T(8,128)(2,1)}, bf16[128,25,64]{0,2,1:T(8,128)(2,1)S(1)}, u32[]{:S(2)}) copy-start(bf16[128,25,64]{0,2,1:T(8,128)(2,1)S(1)} %get-tuple-element.465) | copy-start | bytes 1228804
  781.9 59.9 %copy-start.22 = (bf16[128,1600]{0,1:T(8,128)(2,1)}, bf16[128,1600]{0,1:T(8,128)(2,1)S(1)}, u32[]{:S(2)}) copy-start(bf16[128,1600]{0,1:T(8,128)(2,1)S(1)} %copy.96) | copy-start | bytes 1228804
  833.3 8.5 copy-start.23
  849.6 201.4 %all-to-all-start.3 = ((bf16[4,400,1600]{2,1,0:T(8,128)(2,1)}), bf16[4,400,1600]{2,1,0:T(8,128)(2,1)}, u32[]{:S(2)}, u32[]{:S(2)}) async-start(bf16[4,400,1600]{2,1,0:T(8,128)(2,1)} %bitcast.213), calls=%async_computation.5 | async-start | bytes 10649600 | tf_op jit(solution)/shard_map/all_to_all | solution.py:179
  854.7 480.5 %reduce-scatter.19.cloned.1.call-start = ((), (), s32[]{:S(2)}) async-start(), calls=%async_computation.18 | async-start | bytes 2129920
  866.7 678.8 %all-reduce.16.cloned.1.call-start = ((), (), s32[]{:S(2)}) async-start(), calls=%async_computation.22 | async-start | bytes 31334400 | tf_op jit(solution)/shard_map/psum | solution.py:287
  1296.0 40.5 %copy-start.19 = (bf16[128,1600]{1,0:T(8,128)(2,1)S(1)}, bf16[128,1600]{1,0:T(8,128)(2,1)}, u32[]{:S(2)}) copy-start(bf16[128,1600]{1,0:T(8,128)(2,1)} %reduce-scatter.25.cloned.1.call-done) | copy-start | bytes 1228804
  1297.9 38.6 %all-to-all-start.2 = ((bf16[4,400,2]{1,2,0:T(2,128)(2,1)}), bf16[4,400,2]{1,2,0:T(2,128)(2,1)S(1)}, u32[]{:S(2)}, u32[]{:S(2)}) async-start(bf16[4,400,2]{1,2,0:T(2,128)(2,1)} %copy.83), calls=%async_computation.4 | async-start | bytes 16384 | tf_op jit(solution)/shard_map/all_to_all | solution.py:182
  1336.6 9.4 copy-start.50
  1336.6 27.3 %copy-start.38 = (bf16[1600]{0:T(1024)(128)(2,1)S(1)}, bf16[1600]{0:T(1024)(128)(2,1)}, u32[]{:S(2)}) copy-start(bf16[1600]{0:T(1024)(128)(2,1)} %get-tuple-element.460) | copy-start | bytes 9604
  1336.6 56.7 %copy-start.5 = (f32[128,1600]{0,1:T(8,128)S(1)}, f32[128,1600]{0,1:T(8,128)}, u32[]{:S(2)}) copy-start(f32[128,1600]{0,1:T(8,128)} %copy-done.4) | copy-start | bytes 2457604
  1336.6 56.7 %copy-start.9 = (bf16[128,1600]{0,1:T(8,128)(2,1)S(1)}, bf16[128,1600]{0,1:T(8,128)(2,1)}, u32[]{:S(2)}) copy-start(bf16[128,1600]{0,1:T(8,128)(2,1)} %copy.92) | copy-start | bytes 1228804
  1336.7 56.7 %copy-start.11 = (bf16[128,1600]{0,1:T(8,128)(2,1)S(1)}, bf16[128,1600]{0,1:T(8,128)(2,1)}, u32[]{:S(2)}) copy-start(bf16[128,1600]{0,1:T(8,128)(2,1)} %param.37) | copy-start | bytes 1228804
  1336.7 56.6 %copy-start.32 = (f32[1600]{0:T(1024)S(1)}, f32[1600]{0:T(1024)}, u32[]{:S(2)}) copy-start(f32[1600]{0:T(1024)} %get-tuple-element.378) | copy-start | bytes 19204
  1545.5 7.6 slice-start.2
  1545.5 6.0 copy-start.26
  1545.5 7.6 slice-start.3
  1551.5 6.4 slice-start
  (34 other events, 89.3 us)
Sparse Core Ops, SparseCore 0:
  9.6 269.6 all-gather.6
  292.8 31.6 all-gather.10
  326.9 33.2 all-gather.8
  361.7 164.0 all-gather.12
  527.2 37.6 all-gather.16
  566.9 36.9 all-gather.14
  627.2 35.6 reduce-scatter.20
  734.4 46.2 reduce-scatter.24
  784.7 47.3 reduce-scatter.22
  834.8 164.3 reduce-scatter.16
  1001.5 294.3 reduce-scatter.14
  1298.7 36.4 reduce-scatter.18
  1339.8 205.6 all-reduce.15
where the time goes:
time: 1580 us; the launch traced here: 1570 us
  waiting for transfers between devices  1150 us (73%)
  matrix products  151 us (10%)
  local copies, waits for them, and re-layouts  113 us (7%)
  blocking collectives  62.2 us (4%)
  other arithmetic  45.8 us (3%)
  starting transfers between devices  18.1 us (1%)
  between operations  16.5 us (1%)
    all_gather x1, waiting for transfers between devices, body(): lax.all_gather(qkv_weight, 'fsdp', axis=0, tiled=True)  247 us
    reduce_scatter x1, waiting for transfers between devices, body(): lax.psum_scatter(grad_qkv_w.astype(jnp.bfloat16), 'fsdp', scatter_dimensi...  228 us
    all_to_all x1, waiting for transfers between devices, body(): lax.all_to_all(grad_fc_cols.astype(jnp.bfloat16), 'fsdp', split_axis=0, c...  176 us
    unnamed x17, waiting for transfers between devices  152 us
    psum x1, waiting for transfers between devices, body(): lax.psum(owned_qkv.astype(jnp.bfloat16), 'ctx').astype(jnp.float32)  150 us
    all_gather x1, waiting for transfers between devices, body(): lax.all_gather(proj_weight, 'fsdp', axis=0, tiled=True)  129 us
    unnamed x127, local copies, waits for them, and re-layouts  40.2 us
    unnamed x2, blocking collectives  38 us
  transfers between devices with their start and end apart: 17, of which 13 were waited for; matrix products, arithmetic and copies ran while one was open for 10% of the time, Pallas kernels for 0%

commit v1 on v0

v1 whole, which is shorter than its diff:
```python
import functools

import jax
import jax.numpy as jnp
from jax import lax
from jax.experimental import pallas as pl
from jax.experimental.pallas import tpu as pltpu
from jax.sharding import PartitionSpec as P

HEADS = 25
BF = jnp.bfloat16
F32 = jnp.float32
MESH = pl.DeviceIdType.MESH
ANY = pl.BlockSpec(memory_space=pl.ANY)
VMEM = pl.BlockSpec(memory_space=pltpu.VMEM)
NT = (((1,), (1,)), ((), ()))


def dot(a, b, dims=(((1,), (0,)), ((), ()))):
    return lax.dot_general(a, b, dims, preferred_element_type=F32)


def places(n):
    me = lax.axis_index("ctx")
    core = lax.rem(me, 2)
    chip = me // 2
    sib = me + 1 - 2 * core
    if n == 8:
        across = chip + 1 - 2 * lax.rem(chip, 2)
        along = lax.rem(chip + 2, 4)
        first = across * (1 - core) + along * core
        second = along * (1 - core) + across * core
        others = [first, second, 3 - chip]
    else:
        half = n // 2
        others = [lax.rem(chip + d, half) for d in range(1, half)]
    return me, core, chip, sib, others


def twin(square, k):
    return 1 - k if square and k < 2 else k


def greet(devices):
    barrier = pltpu.get_barrier_semaphore()
    for device in devices:
        pl.semaphore_signal(barrier, inc=1, device_id={"ctx": device}, device_id_type=MESH)
    pl.semaphore_wait(barrier, len(devices))


def send(src, dst, ssem, rsem, device):
    return pltpu.make_async_remote_copy(
        src_ref=src,
        dst_ref=dst,
        send_sem=ssem,
        recv_sem=rsem,
        device_id={"ctx": device},
        device_id_type=MESH,
    )


def gather_kernel(n, count, parts, *refs):
    ins, outs = refs[:count], refs[count : 2 * count]
    own_sem, sib_s, sib_r, far_s, far_r = refs[2 * count :]
    me, core, chip, sib, others = places(n)
    square = n == 8
    peers = others[:2] if square else others
    half = n // 2
    if square:
        froms = others
    else:
        froms = [lax.rem(chip + half - d, half) for d in range(1, half)]
    greet([sib] + [2 * p + core for p in peers])
    rows = ins[0].shape[0] // parts
    started = []
    locals_ = []
    for j in range(count):
        own = pltpu.make_async_copy(ins[j], outs[j].at[me], own_sem.at[j])
        own.start()
        locals_.append(own)
    for j in range(count):
        for c in range(parts):
            win = pl.ds(c * rows, rows)
            for d, p in enumerate(peers):
                cp = send(
                    ins[j].at[win],
                    outs[j].at[me, win],
                    far_s.at[j, d, c],
                    far_r.at[j, d, c],
                    2 * p + core,
                )
                cp.start()
                started.append(cp)
            cp = send(
                ins[j].at[win],
                outs[j].at[me, win],
                sib_s.at[j, 0, c],
                sib_r.at[j, 0, c],
                sib,
            )
            cp.start()
            started.append(cp)

    def arrived(j, d, c):
        src = 2 * froms[d] + core
        win = pl.ds(c * rows, rows)
        piece = outs[j].at[src, win]
        send(piece, piece, far_s.at[j, d, c], far_r.at[j, d, c], sib).wait_recv()
        if square and d == 0:
            cp = send(
                piece, piece, far_s.at[j, 2, c], far_r.at[j, 2, c], 2 * others[1] + core
            )
            cp.start()
            started.append(cp)
        e = twin(square, d) + 1
        cp = send(piece, piece, sib_s.at[j, e, c], sib_r.at[j, e, c], sib)
        cp.start()
        started.append(cp)

    for j in range(count):
        for c in range(parts):
            for d in range(2 if square else len(others)):
                arrived(j, d, c)
        if square:
            for c in range(parts):
                arrived(j, 2, c)
    for own in locals_:
        own.wait()
    for j in range(count):
        for d in range(len(others) + 1):
            src = (me if d == 0 else 2 * froms[d - 1] + core) + sib - me
            for c in range(parts):
                piece = outs[j].at[src, pl.ds(c * rows, rows)]
                send(piece, piece, sib_s.at[j, d, c], sib_r.at[j, d, c], sib).wait_recv()
    for cp in started:
        cp.wait_send()


def plane_gather(n, cid, *arrays):
    count = len(arrays)
    rows, width = arrays[0].shape
    parts = 4 if n == 8 else 1
    far = n // 2 - 1
    outs = pl.pallas_call(
        functools.partial(gather_kernel, n, count, parts),
        out_shape=[jax.ShapeDtypeStruct((n,) + a.shape, a.dtype) for a in arrays],
        in_specs=[VMEM] * count,
        out_specs=[ANY] * count,
        scratch_shapes=[
            pltpu.SemaphoreType.DMA((count,)),
            pltpu.SemaphoreType.DMA((count, far + 1, parts)),
            pltpu.SemaphoreType.DMA((count, far + 1, parts)),
            pltpu.SemaphoreType.DMA((count, far, parts)),
            pltpu.SemaphoreType.DMA((count, far, parts)),
        ],
        compiler_params=pltpu.CompilerParams(collective_id=cid, has_side_effects=True),
        name=f"plane_gather_{cid}",
    )(*arrays)
    return [o.reshape(n * rows, width) for o in outs]


def scatter_kernel(n, parts, part_ref, out_ref, mine, theirs, sums, inbox, own_s, sib_s, sib_r, far_s, far_r):
    me, core, chip, sib, others = places(n)
    square = n == 8
    half = n // 2
    peers = others[:2] if square else others
    greet([sib] + [2 * p + core for p in peers])
    rows = part_ref.shape[1] // parts
    order = ([2, 0, 1, 3] if square else list(range(half)))
    chips = others + [chip]
    started = []
    loads = {}
    for c in range(parts):
        win = pl.ds(c * rows, rows)
        for k in order:
            e = twin(square, k)
            cp = send(
                part_ref.at[2 * chips[k] + 1 - core, win],
                theirs.at[e, win],
                sib_s.at[e, c],
                sib_r.at[e, c],
                sib,
            )
            cp.start()
            started.append(cp)
            ld = pltpu.make_async_copy(
                part_ref.at[2 * chips[k] + core, win], mine.at[k, win], own_s.at[k, c]
            )
            ld.start()
            loads[k, c] = ld

    def chip_sum(k, c):
        win = pl.ds(c * rows, rows)
        loads[k, c].wait()
        send(
            theirs.at[k, win], theirs.at[k, win], sib_s.at[k, c], sib_r.at[k, c], sib
        ).wait_recv()
        return mine[k, win, :].astype(F32) + theirs[k, win, :].astype(F32)

    def pass_on(k, c, slot, peer):
        win = pl.ds(c * rows, rows)
        cp = send(
            sums.at[k, win], inbox.at[slot, win], far_s.at[slot, c], far_r.at[slot, c], peer
        )
        cp.start()
        started.append(cp)

    def wait_in(slot, c):
        win = pl.ds(c * rows, rows)
        send(
            inbox.at[slot, win], inbox.at[slot, win], far_s.at[slot, c], far_r.at[slot, c], sib
        ).wait_recv()
        return inbox[slot, win, :].astype(F32)

    if square:
        a, b = 2 * others[0] + core, 2 * others[1] + core
        for c in range(parts):
            win = pl.ds(c * rows, rows)
            for k, slot in ((2, 0), (0, 1)):
                sums[k, win, :] = chip_sum(k, c).astype(BF)
                pass_on(k, c, slot, a)
        for c in range(parts):
            win = pl.ds(c * rows, rows)
            sums[1, win, :] = (chip_sum(1, c) + wait_in(0, c)).astype(BF)
            pass_on(1, c, 2, b)
        for c in range(parts):
            win = pl.ds(c * rows, rows)
            out_ref[win, :] = chip_sum(3, c) + wait_in(1, c)
        for c in range(parts):
            win = pl.ds(c * rows, rows)
            out_ref[win, :] += wait_in(2, c)
    else:
        for c in range(parts):
            win = pl.ds(c * rows, rows)
            for k in range(half - 1):
                sums[k, win, :] = chip_sum(k, c).astype(BF)
                pass_on(k, c, k, 2 * others[k] + core)
        for c in range(parts):
            win = pl.ds(c * rows, rows)
            out_ref[win, :] = chip_sum(half - 1, c)
            for k in range(half - 1):
                out_ref[win, :] += wait_in(k, c)
    for cp in started:
        cp.wait_send()


def plane_scatter(n, cid, partial):
    half = n // 2
    rows, width = partial.shape[0] // n, partial.shape[1]
    parts = 4 if n == 8 else 1
    return pl.pallas_call(
        functools.partial(scatter_kernel, n, parts),
        out_shape=jax.ShapeDtypeStruct((rows, width), F32),
        in_specs=[ANY],
        out_specs=VMEM,
        scratch_shapes=[
            pltpu.VMEM((half, rows, width), BF),
            pltpu.VMEM((half, rows, width), BF),
            pltpu.VMEM((half - 1, rows, width), BF),
            pltpu.VMEM((half - 1, rows, width), BF),
            pltpu.SemaphoreType.DMA((half, parts)),
            pltpu.SemaphoreType.DMA((half, parts)),
            pltpu.SemaphoreType.DMA((half, parts)),
            pltpu.SemaphoreType.DMA((half - 1, parts)),
            pltpu.SemaphoreType.DMA((half - 1, parts)),
        ],
        compiler_params=pltpu.CompilerParams(collective_id=cid, has_side_effects=True),
        name=f"plane_scatter_{cid}",
    )(partial.reshape(n, rows, width))


def attend_kernel(blocks, blk, tile, inv_ref, q_ref, k_ref, v_ref, o_ref, p_ref, qn, kn, vn, ot):
    length = blocks * blk
    for i in range(blocks):
        src, dst = pl.ds(pl.multiple_of(inv_ref[i] * blk, blk), blk), pl.ds(i * blk, blk)
        qn[dst, :] = q_ref[src, :]
        kn[dst, :] = k_ref[src, :]
        vn[dst, :] = v_ref[src, :]
    v_turned = vn[...].astype(F32).T.astype(BF)
    lane = lax.broadcasted_iota(jnp.int32, (1, 128), 1)
    above = lax.broadcasted_iota(jnp.int32, (tile, tile), 0) > lax.broadcasted_iota(
        jnp.int32, (tile, tile), 1
    )
    for i in range(length // tile):
        cols = pl.ds(i * tile, tile)
        keys = (i + 1) * tile
        for h in range(2):
            here = (lane // 64) == h
            q = jnp.where(here, qn[cols, :].astype(F32) * 0.125, 0.0).astype(BF)
            last = jnp.where(above, -1e30, dot(kn[pl.ds(i * tile, tile), :], q, NT))
            top = jnp.max(last, axis=0, keepdims=True)
            if i:
                early = dot(kn[pl.ds(0, i * tile), :], q, NT)
                top = jnp.maximum(top, jnp.max(early, axis=0, keepdims=True))
            last = jnp.exp(last - top)
            total = jnp.sum(last, axis=0, keepdims=True)
            if i:
                early = jnp.exp(early - top)
                total = total + jnp.sum(early, axis=0, keepdims=True)
            scale = 1.0 / total
            last = (last * scale).astype(BF)
            p_ref[h, pl.ds(i * tile, tile), cols] = last
            half = slice(64 * h, 64 * h + 64)
            o = dot(v_turned[half, i * tile : keys], last)
            if i:
                early = (early * scale).astype(BF)
                p_ref[h, pl.ds(0, i * tile), cols] = early
                o = o + dot(v_turned[half, : i * tile], early)
            ot[half, cols] = o
    o_nat = ot[...].T
    for i in range(blocks):
        o_ref[pl.ds(pl.multiple_of(inv_ref[i] * blk, blk), blk), :] = o_nat[
            i * blk : (i + 1) * blk, :
        ].astype(BF)


def attend(qkv, inv, blk):
    length = qkv.shape[0]
    cols = qkv.shape[1] // 3
    pairs = cols // 128
    blocks = inv.shape[0]
    tile = 256
    piece = lambda off: pl.BlockSpec((length, 128), lambda p, s: (0, off * pairs + p))
    return pl.pallas_call(
        functools.partial(attend_kernel, blocks, blk, tile),
        out_shape=[
            jax.ShapeDtypeStruct((length, cols), BF),
            jax.ShapeDtypeStruct((2 * pairs, length, length), BF),
        ],
        grid_spec=pltpu.PrefetchScalarGridSpec(
            num_scalar_prefetch=1,
            grid=(pairs,),
            in_specs=[piece(0), piece(1), piece(2)],
            out_specs=[
                pl.BlockSpec((length, 128), lambda p, s: (0, p)),
                pl.BlockSpec((2, length, length), lambda p, s: (p, 0, 0)),
            ],
            scratch_shapes=[
                pltpu.VMEM((length, 128), BF),
                pltpu.VMEM((length, 128), BF),
                pltpu.VMEM((length, 128), BF),
                pltpu.VMEM((128, length), F32),
            ],
        ),
        compiler_params=pltpu.CompilerParams(vmem_limit_bytes=60 * 1024 * 1024),
        name="attend",
    )(inv, qkv, qkv, qkv)


def attend_back_kernel(
    blocks, blk, tile, pairs, inv_ref, q_ref, k_ref, v_ref, g_ref, o_ref, p_ref, out_ref,
    qn, kn, vn, gn, on, dqt, dk, dv,
):
    length = blocks * blk
    for i in range(blocks):
        src, dst = pl.ds(pl.multiple_of(inv_ref[i] * blk, blk), blk), pl.ds(i * blk, blk)
        qn[dst, :] = q_ref[src, :]
        kn[dst, :] = k_ref[src, :]
        vn[dst, :] = v_ref[src, :]
        gn[dst, :] = g_ref[src, :]
        on[dst, :] = o_ref[src, :]
    k_turned = kn[...].astype(F32).T.astype(BF)
    prod = (gn[...].astype(F32) * on[...].astype(F32)).T
    deltas = [jnp.sum(prod[64 * h : 64 * h + 64, :], axis=0, keepdims=True) for h in range(2)]
    lane = lax.broadcasted_iota(jnp.int32, (1, 128), 1)
    dk[...] = jnp.zeros_like(dk)
    dv[...] = jnp.zeros_like(dv)
    for i in range(length // tile):
        cols = pl.ds(i * tile, tile)
        keys = (i + 1) * tile
        for h in range(2):
            here = (lane // 64) == h
            q = jnp.where(here, qn[cols, :].astype(F32), 0.0).astype(BF)
            g = jnp.where(here, gn[cols, :].astype(F32), 0.0).astype(BF)
            p = p_ref[h, pl.ds(0, keys), cols]
            dp = dot(vn[pl.ds(0, keys), :], g, NT)
            ds = (
                p.astype(F32) * (dp - deltas[h][:, i * tile : (i + 1) * tile]) * 0.125
            ).astype(BF)
            half = slice(64 * h, 64 * h + 64)
            dqt[half, cols] = dot(k_turned[half, :keys], ds)
            dk[pl.ds(0, keys), :] += dot(ds, q)
            dv[pl.ds(0, keys), :] += dot(p, g)
    dq = dqt[...].T
    pair = pl.program_id(0)
    for i in range(blocks):
        dst = pl.ds(pl.multiple_of(inv_ref[i] * blk, blk), blk)
        src = slice(i * blk, (i + 1) * blk)
        for t, val in enumerate((dq, dk, dv)):
            at = pl.ds(pl.multiple_of((t * pairs + pair) * 128, 128), 128)
            out_ref[dst, at] = val[src, :].astype(BF)


def attend_back(qkv, grad, o, p, inv, blk):
    length = qkv.shape[0]
    cols = qkv.shape[1] // 3
    pairs = cols // 128
    blocks = inv.shape[0]
    tile = 256
    piece = lambda off: pl.BlockSpec((length, 128), lambda i, s: (0, off * pairs + i))
    return pl.pallas_call(
        functools.partial(attend_back_kernel, blocks, blk, tile, pairs),
        out_shape=jax.ShapeDtypeStruct((length, 3 * cols), BF),
        grid_spec=pltpu.PrefetchScalarGridSpec(
            num_scalar_prefetch=1,
            grid=(pairs,),
            in_specs=[
                piece(0),
                piece(1),
                piece(2),
                piece(0),
                piece(0),
                pl.BlockSpec((2, length, length), lambda i, s: (i, 0, 0)),
            ],
            out_specs=pl.BlockSpec((length, 3 * cols), lambda i, s: (0, 0)),
            scratch_shapes=[pltpu.VMEM((length, 128), BF)] * 5
            + [
                pltpu.VMEM((128, length), F32),
                pltpu.VMEM((length, 128), F32),
                pltpu.VMEM((length, 128), F32),
            ],
        ),
        compiler_params=pltpu.CompilerParams(vmem_limit_bytes=60 * 1024 * 1024),
        name="attend_back",
    )(inv, qkv, qkv, qkv, grad, o, p)


def norm(values):
    centre = values - jnp.mean(values, axis=-1, keepdims=True)
    rstd = lax.rsqrt(jnp.mean(centre * centre, axis=-1, keepdims=True) + 1e-05)
    return centre * rstd, rstd


def norm_back(grad, unit, rstd, gain):
    inner = grad * gain
    return rstd * (
        inner
        - jnp.mean(inner, axis=-1, keepdims=True)
        - unit * jnp.mean(inner * unit, axis=-1, keepdims=True)
    )


def gelu(u):
    return jax.nn.gelu(u, approximate=True)


def make_body(n, nz):
    def body(
        tokens, block_table, ln1_gain, ln1_bias, qkv_weight, query_bias, value_bias,
        proj_weight, proj_bias, ln2_gain, ln2_bias, fc_weight, fc_bias, out_weight,
        out_bias, cotangent,
    ):
        ctx = lax.axis_index("ctx")
        z = lax.axis_index("fsdp")
        rows, width = tokens.shape
        blk = rows // 2
        wz = width // nz
        slots = -(-HEADS // n)
        hw = slots * (width // HEADS)
        unit_z = out_weight.shape[0]
        uw = unit_z // n
        units = uw * nz
        table = block_table.reshape(-1)
        inv = jnp.argmax(
            table[None, :] == jnp.arange(table.shape[0], dtype=table.dtype)[:, None], axis=1
        ).astype(jnp.int32)

        along_z = lambda a, axis=0: lax.all_gather(a, "fsdp", axis=axis, tiled=True)
        small = jnp.stack(
            [ln1_gain, ln1_bias, query_bias, value_bias, proj_bias, ln2_gain, ln2_bias, out_bias]
        )
        small = lax.all_gather(small, "fsdp", axis=0)
        small = small.transpose(1, 0, 2).reshape(8, width).astype(F32)
        g1, b1, qb, vb, pb, g2, b2, ob = [small[i] for i in range(8)]
        fb = along_z(lax.dynamic_slice_in_dim(fc_bias, ctx * uw, uw)).astype(F32)
        pad_cols = lambda v: lax.dynamic_slice_in_dim(jnp.pad(v, (0, n * hw - width)), ctx * hw, hw)
        qkv_bias = jnp.concatenate([pad_cols(qb), jnp.zeros((hw,), F32), pad_cols(vb)])

        padded = jnp.pad(qkv_weight, ((0, 0), (0, n * hw - width)))
        w_qkv = along_z(
            jnp.concatenate(
                [lax.dynamic_slice_in_dim(padded, t * width + ctx * hw, hw, 1) for t in range(3)],
                axis=1,
            )
        )
        w_proj = lax.psum(
            lax.dynamic_slice_in_dim(
                jnp.pad(proj_weight, ((hw, hw), (0, 0))),
                jnp.clip(ctx * hw - z * wz + hw, 0, wz + hw),
                hw,
                0,
            ),
            "fsdp",
        )
        w_fc = along_z(
            jnp.concatenate(
                [
                    lax.dynamic_slice_in_dim(fc_weight, t * unit_z + ctx * uw, uw, 1)
                    for t in range(nz)
                ],
                axis=1,
            )
        )
        w_out = along_z(lax.dynamic_slice_in_dim(out_weight, ctx * uw, uw, 0))

        x = tokens.astype(F32)
        unit1, rstd1 = norm(x)
        h1_own = (unit1 * g1 + b1).astype(BF)
        h1, cot = plane_gather(n, 1, h1_own, cotangent)
        qkv = (dot(h1, w_qkv) + qkv_bias).astype(BF)
        o, p = attend(qkv, inv, blk)
        mid = x + plane_scatter(n, 2, dot(o, w_proj).astype(BF)) + pb
        unit2, rstd2 = norm(mid)
        (h2,) = plane_gather(n, 3, (unit2 * g2 + b2).astype(BF))
        u = dot(h2, w_fc) + fb
        hidden, pull = jax.vjp(gelu, u)
        hidden = hidden.astype(BF)
        dz = dot(cot, w_out, NT)
        du = pull(dz)[0].astype(BF)
        dh2 = plane_scatter(n, 4, dot(du, w_fc, NT).astype(BF))
        dmid = cotangent.astype(F32) + norm_back(dh2, unit2, rstd2, g2)
        da_own = dmid.astype(BF)
        (da,) = plane_gather(n, 5, da_own)
        layer_out = (mid + plane_scatter(n, 6, dot(hidden, w_out).astype(BF)) + ob).astype(BF)
        TN = (((0,), (0,)), ((), ()))
        to_owner = lambda a: lax.psum_scatter(
            a.astype(BF), "fsdp", scatter_dimension=0, tiled=True
        )
        over_ctx = lambda a: lax.all_gather(a, "ctx", axis=0)
        part_out = over_ctx(to_owner(dot(hidden, cot, TN)))
        part_fc = over_ctx(to_owner(dot(h2, du, TN)))
        do = dot(da, w_proj, NT).astype(BF)
        dqkv = attend_back(qkv, do, o, p, inv, blk)
        part_qkv = over_ctx(to_owner(dot(h1, dqkv, TN)))
        part_proj = over_ctx(lax.psum(dot(o, da, TN).astype(BF), "fsdp"))
        dh1 = plane_scatter(n, 7, dot(dqkv, w_qkv, NT).astype(BF))
        grad_tokens = (dmid + norm_back(dh1, unit1, rstd1, g1)).astype(BF)

        grad_out = part_out.reshape(unit_z, width).astype(F32)
        grad_fc = (
            part_fc.reshape(n, wz, nz, uw)
            .transpose(1, 2, 0, 3)
            .reshape(wz, nz * unit_z)
            .astype(F32)
        )
        grad_qkv = (
            part_qkv.reshape(n, wz, 3, hw)
            .transpose(1, 2, 0, 3)
            .reshape(wz, 3, n * hw)[:, :, :width]
            .reshape(wz, 3 * width)
            .astype(F32)
        )
        grad_proj = lax.dynamic_slice_in_dim(
            part_proj.reshape(n * hw, width), z * wz, wz, 0
        ).astype(F32)

        put = lambda v, at, size: lax.dynamic_update_slice_in_dim(
            jnp.zeros((size,), F32), v, at, 0
        )
        col_sum = lambda a: jnp.sum(a.astype(F32), axis=0)
        bias_cols = col_sum(dqkv)
        dfb = col_sum(du).reshape(nz, uw)
        packed = jnp.concatenate(
            [
                col_sum(dh1 * unit1),
                col_sum(dh1),
                col_sum(da_own),
                col_sum(dh2 * unit2),
                col_sum(dh2),
                col_sum(cotangent),
                put(bias_cols[:hw], ctx * hw, n * hw),
                put(bias_cols[2 * hw :], ctx * hw, n * hw),
                lax.dynamic_update_slice_in_dim(
                    jnp.zeros((nz, unit_z), F32), dfb, ctx * uw, 1
                ).reshape(-1),
            ]
        )
        packed = lax.psum(packed, ("fsdp", "ctx"))
        mine = lambda i: lax.dynamic_slice_in_dim(packed, i + z * wz, wz, 0)
        base = 6 * width
        gfb = lax.dynamic_slice_in_dim(packed, base + 2 * n * hw + z * unit_z, unit_z, 0)
        return (
            layer_out,
            grad_tokens,
            mine(0),
            mine(width),
            grad_qkv,
            mine(base),
            mine(base + n * hw),
            grad_proj,
            mine(2 * width),
            mine(3 * width),
            mine(4 * width),
            grad_fc,
            gfb,
            grad_out,
            mine(5 * width),
        )

    return body


def solution(mesh):
    both = P(("fsdp", "ctx"), None)
    vec, mat = P("fsdp"), P("fsdp", None)
    placed = (both, P(), vec, vec, mat, vec, vec, mat, vec, vec, vec, mat, vec, mat, vec, both)
    outs = (both, both, vec, vec, mat, vec, vec, mat, vec, vec, vec, mat, vec, mat, vec)
    return jax.shard_map(
        make_body(mesh.shape["ctx"], mesh.shape["fsdp"]),
        mesh=mesh,
        in_specs=placed,
        out_specs=outs,
        check_vma=False,
    )
```

time: 1580 us -> 918 us (0.58)
  waiting for transfers between devices: 1150 us -> 396 us
  Pallas kernels: 0 us -> 189 us
  matrix products: 151 us -> 77.9 us
  local copies, waits for them, and re-layouts: 113 us -> 171 us
  blocking collectives: 62.2 us -> 27.9 us
  starting transfers between devices: 18.1 us -> 0.53 us
  other arithmetic: 45.8 us -> 28.8 us
    all_gather x6 -> x7, waiting for transfers between devices: 445 us -> 135 us  [the longest x4 81.6 us: body(): over_ctx = lambda a: lax.all_gather(a, 'ctx', axis=0)]
    pallas_call x0 -> x9, Pallas kernels: none -> 189 us  [the longest x4 87.3 us: plane_scatter(): pl.pallas_call(functools.partial(scatter_kernel, n, parts), out_shape=jax...]
    all_to_all x4 -> x0, waiting for transfers between devices: 176 us -> none  [the longest x1 176 us: body(): lax.all_to_all(grad_fc_cols.astype(jnp.bfloat16), 'fsdp', split_axis=0, c...]
    reduce_scatter x2, waiting for transfers between devices: 228 us -> 74.7 us  [body(): lax.psum_scatter(a.astype(BF), 'fsdp', scatter_dimension=0, tiled=True)]
    unnamed x17 -> x14, waiting for transfers between devices: 152 us -> 55.7 us
    convert_element_type x2 -> x9, local copies, waits for them, and re-layouts: 8.71 us -> 96.3 us  [the longest x3 49 us: body(): grad_fc = part_fc.reshape(n, wz, nz, uw).transpose(1, 2, 0, 3).reshape(wz...]
    dot_general x26 -> x12, matrix products: 151 us -> 77.9 us  [dot(): return lax.dot_general(a, b, dims, preferred_element_type=F32)]
    all_to_all x6 -> x0, local copies, waits for them, and re-layouts: 34.5 us -> none  [the longest x2 17.6 us: body(): lax.all_to_all(fc_weight, 'fsdp', split_axis=1, concat_axis=0, tiled=True)]
  transfers between devices with their start and end apart: 17 -> 13, of which waited for: 13 -> 9; matrix products, arithmetic and copies ran while one was open for 10% -> 25% of each run, Pallas kernels for 0% -> 14%
where the time goes in v1:
time: 918 us; the launch traced here: 907 us
  waiting for transfers between devices  396 us (43%)
  Pallas kernels  189 us (21%)
  local copies, waits for them, and re-layouts  171 us (19%)
  matrix products  77.9 us (8%)
  other arithmetic  28.8 us (3%)
  blocking collectives  27.9 us (3%)
  between operations  15.5 us (2%)
    psum x1, waiting for transfers between devices, body(): packed = lax.psum(packed, ('fsdp', 'ctx'))  126 us
    pallas_call x4, Pallas kernels, plane_scatter(): pl.pallas_call(functools.partial(scatter_kernel, n, parts), out_shape=jax...  87.3 us
    all_gather x4, waiting for transfers between devices, body(): over_ctx = lambda a: lax.all_gather(a, 'ctx', axis=0)  81.6 us
    dot_general x12, matrix products, dot(): return lax.dot_general(a, b, dims, preferred_element_type=F32)  77.9 us
    pallas_call x3, Pallas kernels, plane_gather(): pl.pallas_call(functools.partial(gather_kernel, n, count, parts), out_sha...  75.8 us
    reduce_scatter x2, waiting for transfers between devices, body(): lax.psum_scatter(a.astype(BF), 'fsdp', scatter_dimension=0, tiled=True)  74.7 us
    unnamed x14, waiting for transfers between devices  55.7 us
    all_gather x3, waiting for transfers between devices, body(): along_z = lambda a, axis=0: lax.all_gather(a, 'fsdp', axis=axis, tiled=True)  53.2 us
  transfers between devices with their start and end apart: 13, of which 9 were waited for; matrix products, arithmetic and copies ran while one was open for 25% of the time, Pallas kernels for 14%

profile of v1, /device:TPU:0, one launch (start us, length us, event | category | flops | bytes accessed | tf_op | source)
XLA Modules:
  0.0 906.7 jit_solution(11074737162694589159)
XLA Ops:
  16.4 15.3 %all-gather = bf16[32,400]{1,0:T(8,128)(2,1)S(1)} all-gather(bf16[8,400]{1,0:T(8,128)(2,1)S(1)} %stack.35), channel_id=2, replica_groups=mesh['ctx'=8,'fsdp'=4] {'fsdp'}, dimensions={0}, use_global_device_ids=true | all-gather | bytes 32000 | tf_op jit(solution)/shard_map/all_gather | solution.py:472
  37.6 12.6 %all-reduce.4 = bf16[800]{0:T(1024)(128)(2,1)S(1)} all-reduce(bf16[800]{0:T(1024)(128)(2,1)S(1)} %dynamic-update-slice), channel_id=1, replica_groups=mesh['ctx'=8,'fsdp'=4] {'fsdp'}, use_global_device_ids=true, to_apply=%add.4 | all-reduce | flops 800 | bytes 3200
  50.9 36.2 %plane_gather_1.1 = (bf16[8,128,1600]{2,1,0:T(8,128)(2,1)}, bf16[8,128,1600]{2,1,0:T(8,128)(2,1)}) custom-call(bf16[128,1600]{1,0:T(8,128)(2,1)} %fusion.15.refs_0_, bf16[128,1600]{1,0:T(8,128)(2,1)} %copy.128.refs_1_), custom_call_target="tpu_custom_call" | custom-call | tf_op jit(solution)/shard_map/plane_gather_1/pallas_call | solution.py:144
  87.8 6.9 add_convert_fusion.q_ref.k_ref.v_ref
  94.8 12.3 %attend.1 = (bf16[1024,256]{1,0:T(8,128)(2,1)}, bf16[4,1024,1024]{2,1,0:T(8,128)(2,1)}) custom-call(s32[16]{0:T(128)} %get-tuple-element.20.inv_ref, bf16[1024,768]{1,0:T(8,128)(2,1)} %add_convert_fusion.q_ref.k_ref.v_ref, bf16[1024,768]{1,0:T(8,128)(2,1)} %add_convert_fusion.q_ref.k_ref.v_ref, bf16[1024,768]{1,0:T(8,128)(2,1)} %add_convert_fusion.q_ref.k_ref.v_ref), custom_call_target="tpu_custom_call" | custom-call | tf_op jit(solution)/shard_map/attend/pallas_call | solution.py:324
  107.1 5.7 all-reduce.10.cloned.1.call-done
  112.8 4.1 convolution_convert_fusion.3
  116.9 5.6 copy.129
  122.5 20.7 %plane_scatter_2.1 = f32[128,1600]{1,0:T(8,128)} custom-call(bf16[8,128,1600]{2,1,0:T(8,128)(2,1)} %bitcast.56), custom_call_target="tpu_custom_call" | custom-call | tf_op jit(solution)/shard_map/plane_scatter_2/pallas_call | solution.py:251
  145.8 21.1 %plane_gather_3.1 = bf16[8,128,1600]{2,1,0:T(8,128)(2,1)} custom-call(bf16[128,1600]{1,0:T(8,128)(2,1)} %add_convert_fusion.2.refs_0_), custom_call_target="tpu_custom_call" | custom-call | tf_op jit(solution)/shard_map/plane_gather_3/pallas_call | solution.py:144
  166.9 5.4 all-gather.14.cloned.1.call-done
  172.3 7.7 fusion.28
  180.0 47.8 %all-gather.16.cloned.1.call-done = bf16[800,1600]{1,0:T(8,128)(2,1)} async-done(((bf16[200,1600]{1,0:T(8,128)(2,1)}), bf16[800,1600]{1,0:T(8,128)(2,1)}) %all-gather.16.cloned.1.call-update) | async-done | bytes 2560016 | tf_op jit(solution)/shard_map/all_gather | solution.py:468
  227.9 8.9 convert_reduce_fusion
  236.7 5.0 convolution_convert_fusion
  241.8 5.8 copy.132
  247.6 20.7 %plane_scatter_4.1 = f32[128,1600]{1,0:T(8,128)} custom-call(bf16[8,128,1600]{2,1,0:T(8,128)(2,1)} %bitcast.57), custom_call_target="tpu_custom_call" | custom-call | tf_op jit(solution)/shard_map/plane_scatter_4/pallas_call | solution.py:251
  270.9 8.8 convolution_convert_fusion.2
  279.7 5.4 copy.130
  285.1 23.3 %plane_scatter_6.1 = f32[128,1600]{1,0:T(8,128)} custom-call(bf16[8,128,1600]{2,1,0:T(8,128)(2,1)} %bitcast.58), custom_call_target="tpu_custom_call" | custom-call | tf_op jit(solution)/shard_map/plane_scatter_6/pallas_call | solution.py:251
  311.4 18.6 %plane_gather_5.1 = bf16[8,128,1600]{2,1,0:T(8,128)(2,1)} custom-call(bf16[128,1600]{1,0:T(8,128)(2,1)} %get-tuple-element.149.refs_0_), custom_call_target="tpu_custom_call" | custom-call | tf_op jit(solution)/shard_map/plane_gather_5/pallas_call | solution.py:144
  330.0 4.4 fusion.7
  334.5 3.9 convolution_convert_fusion.8.g_ref
  338.4 13.1 %attend_back.1 = bf16[1024,768]{1,0:T(8,128)(2,1)} custom-call(s32[16]{0:T(128)} %get-tuple-element.20.inv_ref, bf16[1024,768]{1,0:T(8,128)(2,1)} %add_convert_fusion.q_ref.k_ref.v_ref, bf16[1024,768]{1,0:T(8,128)(2,1)} %add_convert_fusion.q_ref.k_ref.v_ref, bf16[1024,768]{1,0:T(8,128)(2,1)} %add_convert_fusion.q_ref.k_ref.v_ref, ...), custom_call_target="tpu_custom_call" | custom-call | tf_op jit(solution)/shard_map/attend_back/pallas_call | solution.py:401
  351.5 6.8 convolution_convert_fusion.6
  358.4 7.1 convolution_convert_fusion.4
  365.6 8.5 convolution_convert_fusion.5
  374.1 5.8 convolution_convert_fusion.1
  380.0 5.4 copy.133
  385.4 22.6 %plane_scatter_7.1 = f32[128,1600]{1,0:T(8,128)} custom-call(bf16[8,128,1600]{2,1,0:T(8,128)(2,1)} %bitcast.59), custom_call_target="tpu_custom_call" | custom-call | tf_op jit(solution)/shard_map/plane_scatter_7/pallas_call | solution.py:251
  412.0 16.7 %reduce-scatter.8.cloned.1.call-done = bf16[400,768]{1,0:T(8,128)(2,1)} async-done(((bf16[1600,768]{1,0:T(8,128)(2,1)}), bf16[400,768]{1,0:T(8,128)(2,1)}) %reduce-scatter.8.cloned.1.call-update) | async-done | bytes 614416 | tf_op jit(solution)/shard_map/reduce_scatter | solution.py:526
  428.8 58.0 %reduce-scatter.10.cloned.1.call-done = bf16[400,800]{1,0:T(8,128)(2,1)} async-done(((bf16[1600,800]{1,0:T(8,128)(2,1)}), bf16[400,800]{1,0:T(8,128)(2,1)}) %reduce-scatter.10.cloned.1.call-update) | async-done | bytes 640016 | tf_op jit(solution)/shard_map/reduce_scatter | solution.py:526
  486.8 55.0 %reduce-scatter.12.cloned.1.call-done = bf16[200,1600]{1,0:T(8,128)(2,1)} async-done(((bf16[800,1600]{1,0:T(8,128)(2,1)}), bf16[200,1600]{1,0:T(8,128)(2,1)}) %reduce-scatter.12.cloned.1.call-update) | async-done | bytes 640016
  544.1 125.6 %all-reduce.12.cloned.1.call-done = f32[20096]{0:T(1024)} async-done(((f32[20096]{0:T(1024)}), f32[20096]{0:T(1024)}) %all-reduce.12.cloned.1.call-update) | async-done | bytes 80400 | tf_op jit(solution)/shard_map/psum | solution.py:578
  672.6 47.5 %all-gather.18.cloned.1.call-done = bf16[8,256,1600]{1,2,0:T(8,128)(2,1)} async-done(((bf16[1,256,1600]{1,2,0:T(8,128)(2,1)}), bf16[8,256,1600]{1,2,0:T(8,128)(2,1)}) %all-gather.18.cloned.1.call-update) | async-done | bytes 6553616 | tf_op jit(solution)/shard_map/all_gather | solution.py:529
  727.5 34.1 %all-gather.20.cloned.1.call-done = bf16[3200,768]{1,0:T(8,128)(2,1)} async-done(((bf16[400,768]{1,0:T(8,128)(2,1)}), bf16[3200,768]{1,0:T(8,128)(2,1)}) %all-gather.20.cloned.1.call-update) | async-done | bytes 4915216 | tf_op jit(solution)/shard_map/all_gather | solution.py:529
  761.6 7.4 copy.134
  769.0 17.0 %reshape.152 = bf16[8,400,3,256]{1,0,3,2:T(8,128)(2,1)} reshape(bf16[3200,768]{0,1:T(8,128)(2,1)} %copy.134) | data formatting | bytes 9830400 | tf_op jit(solution)/shard_map/reshape | solution.py:547
  786.1 9.3 %copy.135 = bf16[400,3,8,256]{3,2,0,1:T(8,128)(2,1)} copy(bf16[400,3,8,256]{0,2,3,1:T(8,128)(2,1)} %bitcast.55) | data formatting | bytes 9830400 | tf_op jit(solution)/shard_map/transpose | solution.py:548
  795.4 8.5 reshape.153
  803.9 6.0 slice_convert_fusion
  809.9 11.6 %copy.136 = f32[400,3,1600]{2,1,0:T(4,128)} copy(f32[400,3,1600]{2,0,1:T(8,128)} %slice_convert_fusion) | data formatting | bytes 15360000 | tf_op jit(solution)/shard_map/convert_element_type | solution.py:551
  821.5 13.4 %reshape.155 = f32[400,4800]{1,0:T(8,128)} reshape(f32[400,3,1600]{2,1,0:T(4,128)} %copy.136) | data formatting | bytes 15360000 | tf_op jit(solution)/shard_map/convert_element_type | solution.py:551
  834.9 8.5 copy.140
  843.5 17.2 %reshape.158 = f32[8,400,4,200]{1,0,3,2:T(8,128)} reshape(bf16[3200,800]{0,1:T(8,128)(2,1)} %copy.140) | data formatting | bytes 15360000 | tf_op jit(solution)/shard_map/convert_element_type | solution.py:544
  860.6 17.8 %copy.141 = f32[400,4,8,200]{3,2,1,0:T(8,128)} copy(f32[400,4,8,200]{0,2,3,1:T(8,128)} %bitcast.54) | data formatting | bytes 20480000 | tf_op jit(solution)/shard_map/convert_element_type | solution.py:544
  878.5 14.0 %reshape.156 = f32[400,6400]{1,0:T(8,128)} reshape(f32[400,4,8,200]{3,2,1,0:T(8,128)} %copy.141) | data formatting | bytes 20480000 | tf_op jit(solution)/shard_map/convert_element_type | solution.py:544
  892.5 7.3 convert_element_type.152
  (167 shorter events, 40.7 us)
Async XLA Ops:
  7.2 2.5 copy-start.6
  7.2 80.7 %all-gather.12.cloned.1.call-start = ((), (), s32[]{:S(2)}) async-start(), calls=%async_computation.3 | async-start | bytes 3072000 | tf_op jit(solution)/shard_map/all_gather | solution.py:468
  9.6 103.2 %all-reduce.10.cloned.1.call-start = ((), (), s32[]{:S(2)}) async-start(), calls=%async_computation.4 | async-start | bytes 1703936 | tf_op jit(solution)/shard_map/psum | solution.py:486
  10.9 5.3 copy-start.19
  10.9 5.3 copy-start.20
  10.9 5.3 copy-start.21
  10.9 5.3 copy-start.22
  10.9 5.3 copy-start.23
  10.9 5.3 copy-start.24
  11.0 5.4 copy-start.25
  11.0 5.4 copy-start.26
  11.0 20.9 %copy-start.8 = (bf16[128,1600]{0,1:T(8,128)(2,1)S(1)}, bf16[128,1600]{0,1:T(8,128)(2,1)}, u32[]{:S(2)}) copy-start(bf16[128,1600]{0,1:T(8,128)(2,1)} %param.16) | copy-start | bytes 1228804
  11.0 161.3 %all-gather.14.cloned.1.call-start = ((), (), s32[]{:S(2)}) async-start(), calls=%async_computation.5 | async-start | bytes 3584000 | tf_op jit(solution)/shard_map/all_gather | solution.py:468
  12.8 21.1 %copy-start.27 = (s32[8,2]{0,1:T(2,128)S(1)}, s32[8,2]{0,1:T(2,128)}, u32[]{:S(2)}) copy-start(s32[8,2]{0,1:T(2,128)} %param.17) | copy-start | bytes 196
  12.8 21.3 %copy-start.9 = (bf16[128,1600]{0,1:T(8,128)(2,1)S(1)}, bf16[128,1600]{0,1:T(8,128)(2,1)}, u32[]{:S(2)}) copy-start(bf16[128,1600]{0,1:T(8,128)(2,1)} %param.31) | copy-start | bytes 1228804
  14.0 22.1 %copy-start.29 = (u32[32]{0:T(128)S(1)}, u32[32]{0:T(128)}, u32[]{:S(2)}) copy-start(u32[32]{0:T(128)} %constant.114) | copy-start | bytes 388
  14.1 213.8 %all-gather.16.cloned.1.call-start = ((), (), s32[]{:S(2)}) async-start(), calls=%async_computation.6 | async-start | bytes 3328000 | tf_op jit(solution)/shard_map/all_gather | solution.py:468
  16.1 395.3 %all-reduce.14.cloned.1.call-start = ((), (), s32[]{:S(2)}) async-start(), calls=%async_computation.9 | async-start | bytes 1638400 | tf_op jit(solution)/shard_map/psum | solution.py:535
  32.4 1.4 copy-start.10
  32.7 1.1 copy-start.13
  50.2 220.7 %copy-start.16 = (f32[800]{0:T(1024)}, f32[800]{0:T(1024)S(1)}, u32[]{:S(2)}) copy-start(f32[800]{0:T(1024)S(1)} %convert_element_type.118) | copy-start | bytes 9604
  144.6 123.8 %copy-start.12 = (f32[128]{0:T(128)}, f32[128]{0:T(128)S(1)}, u32[]{:S(2)}) copy-start(f32[128]{0:T(128)S(1)} %broadcast_multiply_fusion.4) | copy-start | bytes 1540
  144.8 123.5 %copy-start.15 = (f32[128]{0:T(128)}, f32[128]{0:T(128)S(1)}, u32[]{:S(2)}) copy-start(f32[128]{0:T(128)S(1)} %add_rsqrt_fusion) | copy-start | bytes 1540
  227.8 8.9 copy-start.28
  236.7 5.0 copy-start.30
  285.1 23.3 %copy-start.1 = (f32[128,1600]{1,0:T(8,128)S(1)}, f32[128,1600]{1,0:T(8,128)}, u32[]{:S(2)}) copy-start(f32[128,1600]{1,0:T(8,128)} %plane_scatter_4.1) | copy-start | bytes 2457604
  285.1 23.3 %copy-start.3 = (bf16[128,1600]{1,0:T(8,128)(2,1)S(1)}, bf16[128,1600]{1,0:T(8,128)(2,1)}, u32[]{:S(2)}) copy-start(bf16[128,1600]{1,0:T(8,128)(2,1)} %copy.128.refs_1_) | copy-start | bytes 1228804
  308.4 21.6 %copy-start.5 = (bf16[1024,256]{1,0:T(8,128)(2,1)S(1)}, bf16[1024,256]{1,0:T(8,128)(2,1)}, u32[]{:S(2)}) copy-start(bf16[1024,256]{1,0:T(8,128)(2,1)} %get-tuple-element.22.o_ref) | copy-start | bytes 1572868
  330.0 4.5 copy-start.7
  334.4 94.3 %reduce-scatter.8.cloned.1.call-start = ((), (), s32[]{:S(2)}) async-start(), calls=%async_computation.8 | async-start | bytes 3072000 | tf_op jit(solution)/shard_map/reduce_scatter | solution.py:526
  351.5 6.9 copy-start.31
  358.3 7.2 copy-start.17
  358.3 128.4 %reduce-scatter.10.cloned.1.call-start = ((), (), s32[]{:S(2)}) async-start(), calls=%async_computation.14 | async-start | bytes 3584000 | tf_op jit(solution)/shard_map/reduce_scatter | solution.py:526
  365.5 8.6 copy-start.2
  365.5 176.3 %reduce-scatter.12.cloned.1.call-start = ((), (), s32[]{:S(2)}) async-start(), calls=%async_computation.15 | async-start | bytes 3328000
  374.1 295.6 %all-reduce.12.cloned.1.call-start = ((), (), s32[]{:S(2)}) async-start(), calls=%async_computation.7 | async-start | bytes 163840 | tf_op jit(solution)/shard_map/psum | solution.py:578
  385.4 22.6 %copy-start.18 = (f32[800]{0:T(1024)S(1)}, f32[800]{0:T(1024)}, u32[]{:S(2)}) copy-start(f32[800]{0:T(1024)} %get-tuple-element.146) | copy-start | bytes 9604
  385.4 23.4 %copy-start.11 = (f32[128]{0:T(128)S(1)}, f32[128]{0:T(128)}, u32[]{:S(2)}) copy-start(f32[128]{0:T(128)} %copy-done.10) | copy-start | bytes 1540
  385.4 23.4 %copy-start.14 = (f32[128]{0:T(128)S(1)}, f32[128]{0:T(128)}, u32[]{:S(2)}) copy-start(f32[128]{0:T(128)} %copy-done.13) | copy-start | bytes 1540
  408.4 134.3 %copy-start = (f32[128,1600]{1,0:T(8,128)S(1)}, f32[128,1600]{1,0:T(8,128)}, u32[]{:S(2)}) copy-start(f32[128,1600]{1,0:T(8,128)} %plane_scatter_7.1) | copy-start | bytes 2457604
  408.7 134.0 %copy-start.4 = (f32[128,1600]{1,0:T(8,128)S(1)}, f32[128,1600]{1,0:T(8,128)}, u32[]{:S(2)}) copy-start(f32[128,1600]{1,0:T(8,128)} %get-tuple-element.150) | copy-start | bytes 2457604
  411.4 308.7 %all-gather.18.cloned.1.call-start = ((), (), s32[]{:S(2)}) async-start(), calls=%async_computation.10 | async-start | bytes 7372800 | tf_op jit(solution)/shard_map/all_gather | solution.py:529
  412.0 349.6 %all-gather.20.cloned.1.call-start = ((), (), s32[]{:S(2)}) async-start(), calls=%async_computation.11 | async-start | bytes 5529600 | tf_op jit(solution)/shard_map/all_gather | solution.py:529
  428.7 406.2 %all-gather.22.cloned.1.call-start = ((), (), s32[]{:S(2)}) async-start(), calls=%async_computation.12 | async-start | bytes 6451200 | tf_op jit(solution)/shard_map/all_gather | solution.py:529
  486.8 405.7 %all-gather.24.cloned.1.call-start = ((), (), s32[]{:S(2)}) async-start(), calls=%async_computation.13 | async-start | bytes 5990400 | tf_op jit(solution)/shard_map/all_gather | solution.py:529
Sparse Core Ops, SparseCore 0:
  10.1 55.1 all-gather.11
  68.3 44.4 all-reduce.9
  114.4 57.8 all-gather.13
  173.7 54.0 all-gather.15
  334.6 43.1 all-reduce.13
  380.0 48.6 reduce-scatter.7
  431.0 55.6 reduce-scatter.9
  489.6 52.0 reduce-scatter.11
  547.9 121.7 all-reduce.11
  671.4 48.5 all-gather.17
  722.0 39.5 all-gather.19
  763.3 43.0 all-gather.21
  808.3 41.3 all-gather.23

commit v2 on v1

v2 whole, which is shorter than its diff:
```python
import functools

import jax
import jax.numpy as jnp
from jax import lax
from jax.experimental import pallas as pl
from jax.experimental.pallas import tpu as pltpu
from jax.sharding import PartitionSpec as P

HEADS = 25
BF = jnp.bfloat16
F32 = jnp.float32
MESH = pl.DeviceIdType.MESH
ANY = pl.BlockSpec(memory_space=pl.ANY)
VMEM = pl.BlockSpec(memory_space=pltpu.VMEM)
NN = (((1,), (0,)), ((), ()))
NT = (((1,), (1,)), ((), ()))
TN = (((0,), (0,)), ((), ()))


def dot(a, b, dims=NN):
    return lax.dot_general(a, b, dims, preferred_element_type=F32)


def places(n):
    me = lax.axis_index("ctx")
    core = lax.rem(me, 2)
    chip = me // 2
    sib = me + 1 - 2 * core
    if n == 8:
        across = chip + 1 - 2 * lax.rem(chip, 2)
        along = lax.rem(chip + 2, 4)
        first = across * (1 - core) + along * core
        second = along * (1 - core) + across * core
        others = [first, second, 3 - chip]
    else:
        half = n // 2
        others = [lax.rem(chip + d, half) for d in range(1, half)]
    return me, core, chip, sib, others


def twin(square, k):
    return 1 - k if square and k < 2 else k


def signal(sem, **device):
    pl.semaphore_signal(sem, inc=1, device_id=device, device_id_type=MESH)


def greet(devices, planes=()):
    barrier = pltpu.get_barrier_semaphore()
    for device in devices:
        signal(barrier, ctx=device)
    for plane in planes:
        signal(barrier, fsdp=plane)
    pl.semaphore_wait(barrier, len(devices) + len(planes))


def send(src, dst, ssem, rsem, **device):
    return pltpu.make_async_remote_copy(
        src_ref=src,
        dst_ref=dst,
        send_sem=ssem,
        recv_sem=rsem,
        device_id=device,
        device_id_type=MESH,
    )


def merge(*lists):
    keyed = []
    for t, steps in enumerate(lists):
        keyed += [((i + 0.5) / len(steps), t, i, step) for i, step in enumerate(steps)]
    for item in sorted(keyed, key=lambda k: k[:3]):
        item[3]()


class Gather:
    def __init__(self, n, src, out, sems):
        self.n, self.src, self.out = n, src, out
        self.own_s, self.sib_s, self.sib_r, self.far_s, self.far_r = sems
        self.parts = src.shape[0]
        self.square = n == 8
        self.me, self.core, self.chip, self.sib, self.others = places(n)
        half = n // 2
        if self.square:
            self.froms = self.others
        else:
            self.froms = [lax.rem(self.chip + half - d, half) for d in range(1, half)]
        self.peers = self.others[:2] if self.square else self.others
        self.started = []

    @staticmethod
    def sems(n, parts):
        dma = pltpu.SemaphoreType.DMA
        far = n // 2 - 1
        return [dma((parts,)), dma((far + 1, parts)), dma((far + 1, parts)), dma((far, parts)), dma((far, parts))]

    def go(self, copy):
        copy.start()
        self.started.append(copy)

    def start(self):
        self.locals = []
        for c in range(self.parts):
            piece = self.src.at[c]
            for d, p in enumerate(self.peers):
                self.go(
                    send(
                        piece,
                        self.out.at[self.me, c],
                        self.far_s.at[d, c],
                        self.far_r.at[d, c],
                        ctx=2 * p + self.core,
                    )
                )
            self.go(
                send(
                    piece, self.out.at[self.me, c], self.sib_s.at[0, c], self.sib_r.at[0, c], ctx=self.sib
                )
            )
            own = pltpu.make_async_copy(piece, self.out.at[self.me, c], self.own_s.at[c])
            own.start()
            self.locals.append(own)

    def arrived(self, d, c):
        piece = self.out.at[2 * self.froms[d] + self.core, c]
        send(piece, piece, self.far_s.at[d, c], self.far_r.at[d, c], ctx=self.sib).wait_recv()
        if self.square and d == 0:
            self.go(
                send(
                    piece,
                    piece,
                    self.far_s.at[2, c],
                    self.far_r.at[2, c],
                    ctx=2 * self.others[1] + self.core,
                )
            )
        e = twin(self.square, d) + 1
        self.go(send(piece, piece, self.sib_s.at[e, c], self.sib_r.at[e, c], ctx=self.sib))

    def steps(self):
        todo = []
        for c in range(self.parts):
            for d in range(2 if self.square else len(self.others)):
                todo.append(functools.partial(self.arrived, d, c))
            if self.square and c:
                todo.append(functools.partial(self.arrived, 2, c - 1))
        if self.square:
            todo.append(functools.partial(self.arrived, 2, self.parts - 1))
        return todo

    def finish(self):
        for own in self.locals:
            own.wait()
        for d in range(len(self.others) + 1):
            chip = self.chip if d == 0 else self.froms[d - 1]
            for c in range(self.parts):
                piece = self.out.at[2 * chip + 1 - self.core, c]
                send(
                    piece, piece, self.sib_s.at[d, c], self.sib_r.at[d, c], ctx=self.sib
                ).wait_recv()
        for copy in self.started:
            copy.wait_send()


class Relay:
    def __init__(self, nz, z, lo, hi, count, src, out, sems, lead):
        self.nz, self.z, self.lo, self.hi, self.count = nz, z, lo, hi, count
        self.src, self.out, self.lead = src, out, lead
        self.own_s, self.up_s, self.down_s, self.recv = sems

    @staticmethod
    def sems(blocks):
        return [pltpu.SemaphoreType.DMA((blocks,)) for _ in range(4)]

    def up(self, src, b):
        return send(src, self.out.at[b], self.up_s.at[b], self.recv.at[b], fsdp=self.z + 1)

    def down(self, src, b):
        return send(src, self.out.at[b], self.down_s.at[b], self.recv.at[b], fsdp=self.z - 1)

    def own(self, b):
        return pltpu.make_async_copy(self.src.at[b - self.lead], self.out.at[b], self.own_s.at[b])

    def start(self):
        lo, hi = self.lo, self.hi

        def body(i, carry):
            u, d = hi - 1 - i, lo + i

            @pl.when(self.z < self.nz - 1)
            def _():
                self.up(self.src.at[u - self.lead], u).start()

            @pl.when(self.z > 0)
            def _():
                self.down(self.src.at[d - self.lead], d).start()

            self.own(d).start()
            return carry

        lax.fori_loop(0, hi - lo, body, 0)

    def step(self, i):
        b = self.lo - 1 - i

        @pl.when(b >= 0)
        def _():
            self.up(self.out.at[b], b).wait_recv()

            @pl.when(self.z < self.nz - 1)
            def _():
                self.up(self.out.at[b], b).start()

        e = self.hi + i

        @pl.when(e < self.count)
        def _():
            self.down(self.out.at[e], e).wait_recv()

            @pl.when(self.z > 0)
            def _():
                self.down(self.out.at[e], e).start()

    def steps(self, most):
        return [functools.partial(self.step, i) for i in range(most)]

    def finish(self):
        def sent(b, carry):
            @pl.when((self.z < self.nz - 1) & (b < self.hi))
            def _():
                self.up(self.out.at[b], b).wait_send()

            @pl.when((self.z > 0) & (b >= self.lo))
            def _():
                self.down(self.out.at[b], b).wait_send()

            @pl.when((b >= self.lo) & (b < self.hi))
            def _():
                self.own(b).wait()

            return carry

        lax.fori_loop(0, self.count, sent, 0)


def others_of(z, nz):
    return [lax.rem(z + d, nz) for d in range(1, nz)]


def entry_kernel(n, nz, tok, cot, small, wq, wp, h1_all, cot_all, vec, wq_all, wp_all, *scratch):
    h1, inbox, zeros, small_s, small_r, zero_s = scratch[:6]
    g_h, g_c = scratch[6:11], scratch[11:16]
    r_q, r_p = scratch[16:20], scratch[20:24]
    me, core, chip, sib, others = places(n)
    z = lax.axis_index("fsdp")
    planes = others_of(z, nz)
    greet([sib] + [2 * p + core for p in (others[:2] if n == 8 else others)], planes)
    width = tok.shape[1]
    wz = small.shape[1]
    for d, plane in enumerate(planes):
        send(small, inbox.at[z], small_s.at[d], small_r.at[d], fsdp=plane).start()
    inbox[z] = small[...]
    gather_c = Gather(n, cot, cot_all, g_c)
    gather_c.start()
    k = wq.shape[0]
    relay_q = Relay(nz, z, z * k, (z + 1) * k, nz * k, wq, wq_all, r_q, z * k)
    relay_q.start()
    share, blocks = wp.shape[0], wp_all.shape[0]
    base = me * blocks
    valid = jnp.clip(nz * share - base, 0, blocks)
    lo = jnp.clip(z * share - base, 0, valid)
    hi = jnp.clip((z + 1) * share - base, 0, valid)
    relay_p = Relay(nz, z, lo, hi, valid, wp, wp_all, r_p, z * share - base)
    relay_p.start()
    zeros[...] = jnp.zeros_like(zeros)

    def clear(b, carry):
        pltpu.make_async_copy(zeros, wp_all.at[b], zero_s.at[b]).start()
        return carry

    lax.fori_loop(valid, blocks, clear, 0)
    for d in range(nz - 1):
        came = lax.rem(z + nz - 1 - d, nz)
        send(small, inbox.at[came], small_s.at[d], small_r.at[d], fsdp=planes[d]).wait_recv()
    for p in range(nz):
        vec[:, p * wz : (p + 1) * wz] = inbox[p].astype(F32)
    gain, shift = vec[0:1, :], vec[1:2, :]
    parts, rows = h1.shape[0], h1.shape[1]
    for c in range(parts):
        unit, _ = norm(tok[c * rows : (c + 1) * rows, :].astype(F32))
        h1[c] = (unit * gain + shift).astype(BF)
    gather_h = Gather(n, h1, h1_all, g_h)
    gather_h.start()
    merge(
        gather_c.steps() + gather_h.steps(),
        relay_q.steps(nz * k - k) + relay_p.steps(blocks),
    )
    gather_c.finish()
    gather_h.finish()
    relay_q.finish()
    relay_p.finish()

    def cleared(b, carry):
        pltpu.make_async_copy(zeros, wp_all.at[b], zero_s.at[b]).wait()
        return carry

    lax.fori_loop(valid, blocks, cleared, 0)
    for d, plane in enumerate(planes):
        send(small, inbox.at[z], small_s.at[d], small_r.at[d], fsdp=plane).wait_send()


def entry(n, nz, tokens, cot, small, wq, wp, hw):
    rows, width = tokens.shape
    parts = 4 if n == 8 else 1
    dma = pltpu.SemaphoreType.DMA
    k, blocks = wq.shape[0], hw // 8
    shape = jax.ShapeDtypeStruct
    piece = (parts, rows // parts, width)
    return pl.pallas_call(
        functools.partial(entry_kernel, n, nz),
        out_shape=[
            shape((n,) + piece, BF),
            shape((n,) + piece, BF),
            shape((small.shape[0], width), F32),
            shape((nz * k,) + wq.shape[1:], BF),
            shape((blocks, 8, width), BF),
        ],
        in_specs=[VMEM] * 5,
        out_specs=[ANY, ANY, VMEM, ANY, ANY],
        scratch_shapes=[
            pltpu.VMEM(piece, BF),
            pltpu.VMEM((nz,) + small.shape, BF),
            pltpu.VMEM((8, width), BF),
            dma((nz - 1,)),
            dma((nz - 1,)),
            dma((blocks,)),
        ]
        + Gather.sems(n, parts)
        + Gather.sems(n, parts)
        + Relay.sems(nz * k)
        + Relay.sems(blocks),
        compiler_params=pltpu.CompilerParams(collective_id=1, has_side_effects=True),
        name="entry",
    )(tokens, cot.reshape(piece), small, wq, wp)


def gather_kernel(n, count, *refs):
    ins, outs, sems = refs[:count], refs[count : 2 * count], refs[2 * count :]
    me, core, chip, sib, others = places(n)
    greet([sib] + [2 * p + core for p in (others[:2] if n == 8 else others)])
    gathers = [Gather(n, ins[j], outs[j], sems[5 * j : 5 * j + 5]) for j in range(count)]
    for g in gathers:
        g.start()
    for g in gathers:
        for step in g.steps():
            step()
    for g in gathers:
        g.finish()


def plane_gather(n, cid, *arrays):
    count = len(arrays)
    sems = []
    for a in arrays:
        sems += Gather.sems(n, a.shape[0])
    return pl.pallas_call(
        functools.partial(gather_kernel, n, count),
        out_shape=[jax.ShapeDtypeStruct((n,) + a.shape, a.dtype) for a in arrays],
        in_specs=[VMEM] * count,
        out_specs=[ANY] * count,
        scratch_shapes=sems,
        compiler_params=pltpu.CompilerParams(collective_id=cid, has_side_effects=True),
        name=f"plane_gather_{cid}",
    )(*arrays)


class Scatter:
    def __init__(self, n, dims, a, w, out, scratch):
        self.n, self.dims, self.a, self.w, self.out = n, dims, a, w, out
        self.part, self.theirs, self.sums, self.inbox = scratch[:4]
        self.sib_s, self.sib_r, self.far_s, self.far_r = scratch[4:]
        self.me, self.core, self.chip, self.sib, self.others = places(n)
        self.square = n == 8
        self.half = n // 2
        self.parts = self.sib_s.shape[1]
        self.full = self.part.shape[2]
        self.rows = self.full // self.parts
        if self.square:
            first, second = [2 * p + self.core for p in self.others[:2]]
            self.ends = [(0, 0, first), (1, 1, first), (2, 2, second)]
        else:
            self.ends = [(k, k, 2 * self.others[k] + self.core) for k in range(self.half - 1)]

    @staticmethod
    def scratch(n, rows, width):
        dma = pltpu.SemaphoreType.DMA
        half, parts = n // 2, 2 if n == 8 else 1
        return [
            pltpu.VMEM((half, 2, rows, width), BF),
            pltpu.VMEM((half, rows, width), BF),
            pltpu.VMEM((half - 1, rows, width), BF),
            pltpu.VMEM((half - 1, rows, width), BF),
            dma((half, parts)),
            dma((half, parts)),
            dma((half - 1, parts)),
            dma((half - 1, parts)),
        ]

    def chip_at(self, k):
        if not self.square:
            return lax.rem(self.chip + 1 + k, self.half)
        x, y = lax.rem(self.chip, 2), self.chip // 2
        first, second = 1 - lax.rem(k, 3) // 2, 1 - lax.rem(k, 2)
        dx = first * (1 - self.core) + second * self.core
        dy = second * (1 - self.core) + first * self.core
        far = (k < 3).astype(jnp.int32)
        dx, dy = dx * far, dy * far
        return (y + dy - 2 * y * dy) * 2 + x + dx - 2 * x * dx

    def twin_at(self, k):
        if not self.square:
            return k
        return k + jnp.where(k == 1, 1, 0) - jnp.where(k == 2, 1, 0)

    def win(self, c):
        return pl.ds(c * self.rows, self.rows)

    def to_sib(self, k, c):
        e = self.twin_at(k)
        return send(
            self.part.at[k, 1 - self.core, self.win(c)],
            self.theirs.at[e, self.win(c)],
            self.sib_s.at[e, c],
            self.sib_r.at[e, c],
            ctx=self.sib,
        )

    def chip_sum(self, k, c):
        win = self.win(c)
        piece = self.theirs.at[k, win]
        send(piece, piece, self.sib_s.at[k, c], self.sib_r.at[k, c], ctx=self.sib).wait_recv()
        return self.part[k, self.core, win, :].astype(F32) + self.theirs[k, win, :].astype(F32)

    def pass_on(self, k, slot, peer, c):
        return send(
            self.sums.at[k, self.win(c)],
            self.inbox.at[slot, self.win(c)],
            self.far_s.at[slot, c],
            self.far_r.at[slot, c],
            ctx=peer,
        )

    def wait_in(self, slot, c):
        piece = self.inbox.at[slot, self.win(c)]
        send(piece, piece, self.far_s.at[slot, c], self.far_r.at[slot, c], ctx=self.sib).wait_recv()
        return self.inbox[slot, self.win(c), :].astype(F32)

    def forward(self, end, c):
        k, slot, peer = self.ends[end]
        total = self.chip_sum(k, c)
        if self.square and end == 2:
            total = total + self.wait_in(0, c)
        self.sums[k, self.win(c), :] = total.astype(BF)
        self.pass_on(k, slot, peer, c).start()

    def products(self):
        def product(k, carry):
            full = self.full
            at = pl.ds(pl.multiple_of(self.chip_at(k) * 2 * full, 2 * full), 2 * full)
            val = dot(self.a[at, :], self.w[...], self.dims).astype(BF)
            self.part[k, 0] = val[:full]
            self.part[k, 1] = val[full:]
            for c in range(self.parts):
                self.to_sib(k, c).start()

            @pl.when(k == 1)
            def _():
                for c in range(self.parts):
                    self.forward(0, c)

            return carry

        lax.fori_loop(0, self.half, product, 0)

    def own(self, c):
        self.out[self.win(c), :] = self.chip_sum(self.half - 1, c)

    def add(self, slot, c):
        self.out[self.win(c), :] += self.wait_in(slot, c)

    def steps(self):
        each = range(self.parts)
        todo = [functools.partial(self.forward, e, c) for e in range(1, self.half - 1) for c in each]
        todo += [functools.partial(self.own, c) for c in each]
        slots = (1, 2) if self.square else range(self.half - 1)
        return todo + [functools.partial(self.add, s, c) for s in slots for c in each]

    def finish(self):
        for c in range(self.parts):
            for k, slot, peer in self.ends:
                self.pass_on(k, slot, peer, c).wait_send()

        def sent(k, carry):
            for c in range(self.parts):
                self.to_sib(k, c).wait_send()
            return carry

        lax.fori_loop(0, self.half, sent, 0)


def scatter_kernel(n, dims, *refs):
    count = len(dims)
    ins, outs, scratch = refs[: 2 * count], refs[2 * count : 3 * count], refs[3 * count :]
    me, core, chip, sib, others = places(n)
    greet([sib] + [2 * p + core for p in (others[:2] if n == 8 else others)])
    jobs = [
        Scatter(n, dims[j], ins[2 * j], ins[2 * j + 1], outs[j], scratch[8 * j : 8 * j + 8])
        for j in range(count)
    ]
    steps = []
    for job in jobs:
        job.products()
        todo = job.steps()
        for step in todo[: job.parts]:
            step()
        steps += todo[job.parts :]
    for step in steps:
        step()
    for job in jobs:
        job.finish()


def plane_scatter(n, cid, *jobs):
    rows = jobs[0][0].shape[0] // n
    widths = [w.shape[1] if dims is NN else w.shape[0] for _, w, dims in jobs]
    scratch = []
    for width in widths:
        scratch += Scatter.scratch(n, rows, width)
    return pl.pallas_call(
        functools.partial(scatter_kernel, n, [job[2] for job in jobs]),
        out_shape=[jax.ShapeDtypeStruct((rows, width), F32) for width in widths],
        in_specs=[VMEM] * (2 * len(jobs)),
        out_specs=[VMEM] * len(jobs),
        scratch_shapes=scratch,
        compiler_params=pltpu.CompilerParams(
            collective_id=cid, has_side_effects=True, vmem_limit_bytes=60 * 1024 * 1024
        ),
        name=f"plane_scatter_{cid}",
    )(*[x for a, w, _ in jobs for x in (a, w)])


class Line:
    def __init__(self, nz, z, src, out, scratch):
        self.nz, self.z, self.src, self.out = nz, z, src, out
        self.mine, self.above, self.below, self.up_s, self.down_s, self.recv = scratch
        self.parts = src.shape[1]

    @staticmethod
    def scratch(shape):
        dma, lead = pltpu.SemaphoreType.DMA, shape[:2]
        return [pltpu.VMEM(shape, BF)] * 3 + [dma(lead), dma(lead), dma((2,) + lead)]

    def up(self, src, d, c):
        return send(
            src.at[d, c], self.above.at[d, c], self.up_s.at[d, c], self.recv.at[0, d, c], fsdp=self.z + 1
        )

    def down(self, src, d, c):
        return send(
            src.at[d, c], self.below.at[d, c], self.down_s.at[d, c], self.recv.at[1, d, c], fsdp=self.z - 1
        )

    def start(self):
        for d in range(self.nz - 1, 0, -1):

            @pl.when(self.z == 0)
            def _():
                for c in range(self.parts):
                    self.up(self.src, d, c).start()

            @pl.when(self.z == self.nz - 1)
            def _():
                for c in range(self.parts):
                    self.down(self.src, self.nz - 1 - d, c).start()

    def step_up(self, d, c):
        @pl.when((self.z > 0) & (self.z < d))
        def _():
            copy = self.up(self.mine, d, c)
            copy.wait_recv()
            self.mine[d, c] = (self.src[d, c].astype(F32) + self.above[d, c].astype(F32)).astype(BF)
            copy.start()

    def step_down(self, d, c):
        @pl.when((self.z < self.nz - 1) & (self.z > d))
        def _():
            copy = self.down(self.mine, d, c)
            copy.wait_recv()
            self.mine[d, c] = (self.src[d, c].astype(F32) + self.below[d, c].astype(F32)).astype(BF)
            copy.start()

    def settle(self, c):
        z = self.z
        self.out[c] = self.src[z, c]

        @pl.when(z > 0)
        def _():
            self.up(self.mine, z, c).wait_recv()
            self.out[c] = (self.out[c].astype(F32) + self.above[z, c].astype(F32)).astype(BF)

        @pl.when(z < self.nz - 1)
        def _():
            self.down(self.mine, z, c).wait_recv()
            self.out[c] = (self.out[c].astype(F32) + self.below[z, c].astype(F32)).astype(BF)

    def steps(self):
        todo = []
        for d in range(self.nz - 1, 1, -1):
            for c in range(self.parts):
                todo.append(functools.partial(self.step_up, d, c))
                todo.append(functools.partial(self.step_down, self.nz - 1 - d, c))
        return todo + [functools.partial(self.settle, c) for c in range(self.parts)]

    def finish(self):
        for d in range(self.nz):

            @pl.when(self.z < d)
            def _():
                for c in range(self.parts):
                    self.up(self.mine, d, c).wait_send()

            @pl.when(self.z > d)
            def _():
                for c in range(self.parts):
                    self.down(self.mine, d, c).wait_send()


def reduce_kernel(n, nz, gcount, dims, *refs):
    g_in, refs = refs[:gcount], refs[gcount:]
    line_in, a_in, w_in = refs[:3]
    refs = refs[3:]
    g_out, refs = refs[:gcount], refs[gcount:]
    line_out, out = refs[:2]
    refs = refs[2:]
    me, core, chip, sib, others = places(n)
    z = lax.axis_index("fsdp")
    greet([sib] + [2 * p + core for p in (others[:2] if n == 8 else others)], others_of(z, nz))
    line = Line(nz, z, line_in, line_out, refs[:6])
    line.start()
    scatter = Scatter(n, dims, a_in, w_in, out, refs[6:14])
    scatter.products()
    gathers = [
        Gather(n, g_in[j], g_out[j], refs[14 + 5 * j : 19 + 5 * j]) for j in range(gcount)
    ]
    plane_steps = []
    for g in gathers:
        g.start()
        plane_steps += g.steps()
    merge(plane_steps, line.steps(), scatter.steps())
    for job in gathers + [line, scatter]:
        job.finish()


def reduce_all(n, nz, cid, ready, partial, a, w, dims):
    rows, width = a.shape[0] // n, w.shape[0]
    scratch = Line.scratch(partial.shape) + Scatter.scratch(n, rows, width)
    for r in ready:
        scratch += Gather.sems(n, r.shape[0])
    shape = jax.ShapeDtypeStruct
    return pl.pallas_call(
        functools.partial(reduce_kernel, n, nz, len(ready), dims),
        out_shape=[shape((n,) + r.shape, BF) for r in ready]
        + [shape(partial.shape[1:], BF), shape((rows, width), F32)],
        in_specs=[VMEM] * (len(ready) + 3),
        out_specs=[ANY] * len(ready) + [VMEM] * 2,
        scratch_shapes=scratch,
        compiler_params=pltpu.CompilerParams(
            collective_id=cid, has_side_effects=True, vmem_limit_bytes=60 * 1024 * 1024
        ),
        name="reduce_all",
    )(*ready, partial, a, w)


class Vectors:
    def __init__(self, n, nz, src, out, scratch):
        self.n, self.nz, self.src, self.out = n, nz, src, out
        self.from_sib, self.chips, self.line = scratch[:3]
        self.ss, self.sr, self.cs, self.cr, self.ls, self.lr = scratch[3:]
        self.me, self.core, self.chip, self.sib, self.others = places(n)
        self.z = lax.axis_index("fsdp")
        self.planes = others_of(self.z, nz)

    @staticmethod
    def scratch(n, nz, shape):
        dma = pltpu.SemaphoreType.DMA
        half = n // 2
        return [
            pltpu.VMEM(shape, F32),
            pltpu.VMEM((half,) + shape, F32),
            pltpu.VMEM((nz,) + shape, F32),
            dma((1,)),
            dma((1,)),
            dma((half - 1,)),
            dma((half - 1,)),
            dma((nz - 1,)),
            dma((nz - 1,)),
        ]

    def to_sib(self):
        return send(self.src, self.from_sib, self.ss.at[0], self.sr.at[0], ctx=self.sib)

    def to_chip(self, d):
        at = self.chips.at[self.chip]
        return send(at, at, self.cs.at[d], self.cr.at[d], ctx=2 * self.others[d] + self.core)

    def to_plane(self, d):
        at = self.line.at[self.z]
        return send(at, at, self.ls.at[d], self.lr.at[d], fsdp=self.planes[d])

    def start(self):
        self.to_sib().start()

    def first(self):
        self.to_sib().wait_recv()
        self.chips[self.chip] = self.src[...] + self.from_sib[...]
        for d in range(self.n // 2 - 1):
            self.to_chip(d).start()

    def second(self):
        for d in range(self.n // 2 - 1):
            self.to_chip(d).wait_recv()
        total = self.chips[0]
        for k in range(1, self.n // 2):
            total = total + self.chips[k]
        self.line[self.z] = total
        for d in range(self.nz - 1):
            self.to_plane(d).start()

    def third(self):
        for d in range(self.nz - 1):
            self.to_plane(d).wait_recv()
        total = self.line[0]
        for k in range(1, self.nz):
            total = total + self.line[k]
        self.out[...] = total

    def steps(self):
        return [self.first, self.second, self.third]

    def finish(self):
        self.to_sib().wait_send()
        for d in range(self.n // 2 - 1):
            self.to_chip(d).wait_send()
        for d in range(self.nz - 1):
            self.to_plane(d).wait_send()


def last_kernel(n, nz, src, vec, out, vec_out, *scratch):
    me, core, chip, sib, others = places(n)
    z = lax.axis_index("fsdp")
    greet([sib] + [2 * p + core for p in others], others_of(z, nz))
    vectors = Vectors(n, nz, vec, vec_out, scratch[:9])
    vectors.start()
    gather = Gather(n, src, out, scratch[9:])
    gather.start()
    merge(gather.steps(), vectors.steps())
    gather.finish()
    vectors.finish()


def last_gather(n, nz, cid, array, vectors):
    shape = jax.ShapeDtypeStruct
    return pl.pallas_call(
        functools.partial(last_kernel, n, nz),
        out_shape=[shape((n,) + array.shape, BF), shape(vectors.shape, F32)],
        in_specs=[VMEM, VMEM],
        out_specs=[ANY, VMEM],
        scratch_shapes=Vectors.scratch(n, nz, vectors.shape) + Gather.sems(n, array.shape[0]),
        compiler_params=pltpu.CompilerParams(collective_id=cid, has_side_effects=True),
        name="last_gather",
    )(array, vectors)


def hidden_kernel(h_ref, w_ref, b_ref, z_ref, s_ref):
    u = dot(h_ref[...], w_ref[...]) + b_ref[...]
    root = 0.7978845608028654
    square = u * u
    inner = jnp.tanh(root * u * (1.0 + 0.044715 * square))
    z_ref[...] = (0.5 * u * (1.0 + inner)).astype(BF)
    slope = 0.5 * (1.0 + inner) + 0.5 * u * (1.0 - inner * inner) * root * (1.0 + 3 * 0.044715 * square)
    s_ref[...] = slope.astype(BF)


def hidden_back_kernel(c_ref, w_ref, s_ref, d_ref, sum_ref):
    du = (dot(c_ref[...], w_ref[...], NT) * s_ref[...].astype(F32)).astype(BF)
    d_ref[...] = du

    @pl.when(pl.program_id(0) == 0)
    def _():
        sum_ref[...] = jnp.zeros_like(sum_ref)

    sum_ref[...] += jnp.sum(du.astype(F32), axis=0, keepdims=True)


def tiled(rows, cols):
    return pl.BlockSpec((rows, cols), lambda i: (i, 0))


def fixed(rows, cols):
    return pl.BlockSpec((rows, cols), lambda i: (0, 0))


def hidden_units(h2, w_fc, bias):
    rows, width = h2.shape
    units = w_fc.shape[1]
    tile = 256
    shape = jax.ShapeDtypeStruct((rows, units), BF)
    return pl.pallas_call(
        hidden_kernel,
        grid=(rows // tile,),
        out_shape=[shape, shape],
        in_specs=[tiled(tile, width), fixed(width, units), fixed(1, units)],
        out_specs=[tiled(tile, units), tiled(tile, units)],
        name="hidden",
    )(h2, w_fc, bias)


def hidden_back(cot, w_out, slope):
    rows, width = cot.shape
    units = w_out.shape[0]
    tile = 256
    return pl.pallas_call(
        hidden_back_kernel,
        grid=(rows // tile,),
        out_shape=[
            jax.ShapeDtypeStruct((rows, units), BF),
            jax.ShapeDtypeStruct((1, units), F32),
        ],
        in_specs=[tiled(tile, width), fixed(units, width), tiled(tile, units)],
        out_specs=[tiled(tile, units), fixed(1, units)],
        name="hidden_back",
    )(cot, w_out, slope)


def join_kernel(n, nz, hw, width, fc, qp, out, fc_o, qkv_o, proj_o, out_o):
    uw = fc.shape[-1] // nz
    pw = width // n
    for c in range(n):
        for b in range(nz):
            at = b * n * uw + c * uw
            fc_o[:, at : at + uw] = fc[c, 0, :, b * uw : (b + 1) * uw].astype(F32)
        proj_o[:, c * pw : (c + 1) * pw] = qp[c, 0, :, 3 * hw : 3 * hw + pw].astype(F32)
        size = min(hw, width - c * hw)
        if size > 0:
            for t in range(3):
                at = t * width + c * hw
                qkv_o[:, at : at + size] = qp[c, 0, :, t * hw : t * hw + size].astype(F32)
    out_o[...] = out[...].astype(F32)


def join(n, nz, hw, fc, qp, out):
    tiles = 25
    width = out.shape[1]
    wz = fc.shape[1]
    split = lambda a: a.reshape(n, tiles, wz // tiles, a.shape[-1])
    fc, qp = split(fc), split(qp)
    wide = lambda a: pl.BlockSpec((n, 1, wz // tiles, a.shape[-1]), lambda i: (0, i, 0, 0))
    t, ot = wz // tiles, out.shape[0] // tiles
    cols = (nz * out.shape[0], 3 * width, width)
    shape = jax.ShapeDtypeStruct
    return pl.pallas_call(
        functools.partial(join_kernel, n, nz, hw, width),
        grid=(tiles,),
        out_shape=[shape((wz, c), F32) for c in cols] + [shape(out.shape, F32)],
        in_specs=[wide(fc), wide(qp), tiled(ot, width)],
        out_specs=[tiled(t, c) for c in cols] + [tiled(ot, width)],
        name="join",
    )(fc, qp, out)


def attend_kernel(blocks, blk, tile, inv_ref, q_ref, k_ref, v_ref, o_ref, p_ref, qn, kn, vn, ot):
    length = blocks * blk
    for i in range(blocks):
        src, dst = pl.ds(pl.multiple_of(inv_ref[i] * blk, blk), blk), pl.ds(i * blk, blk)
        qn[dst, :] = q_ref[src, :]
        kn[dst, :] = k_ref[src, :]
        vn[dst, :] = v_ref[src, :]
    v_turned = vn[...].astype(F32).T.astype(BF)
    lane = lax.broadcasted_iota(jnp.int32, (1, 128), 1)
    above = lax.broadcasted_iota(jnp.int32, (tile, tile), 0) > lax.broadcasted_iota(
        jnp.int32, (tile, tile), 1
    )
    for i in range(length // tile):
        cols = pl.ds(i * tile, tile)
        keys = (i + 1) * tile
        for h in range(2):
            here = (lane // 64) == h
            q = jnp.where(here, qn[cols, :].astype(F32) * 0.125, 0.0).astype(BF)
            last = jnp.where(above, -1e30, dot(kn[pl.ds(i * tile, tile), :], q, NT))
            top = jnp.max(last, axis=0, keepdims=True)
            if i:
                early = dot(kn[pl.ds(0, i * tile), :], q, NT)
                top = jnp.maximum(top, jnp.max(early, axis=0, keepdims=True))
            last = jnp.exp(last - top)
            total = jnp.sum(last, axis=0, keepdims=True)
            if i:
                early = jnp.exp(early - top)
                total = total + jnp.sum(early, axis=0, keepdims=True)
            scale = 1.0 / total
            last = (last * scale).astype(BF)
            p_ref[h, pl.ds(i * tile, tile), cols] = last
            half = slice(64 * h, 64 * h + 64)
            o = dot(v_turned[half, i * tile : keys], last)
            if i:
                early = (early * scale).astype(BF)
                p_ref[h, pl.ds(0, i * tile), cols] = early
                o = o + dot(v_turned[half, : i * tile], early)
            ot[half, cols] = o
    o_nat = ot[...].T
    for i in range(blocks):
        o_ref[pl.ds(pl.multiple_of(inv_ref[i] * blk, blk), blk), :] = o_nat[
            i * blk : (i + 1) * blk, :
        ].astype(BF)


def attend(qkv, inv, blk):
    length = qkv.shape[0]
    cols = qkv.shape[1] // 3
    pairs = cols // 128
    blocks = inv.shape[0]
    tile = 256
    piece = lambda off: pl.BlockSpec((length, 128), lambda p, s: (0, off * pairs + p))
    return pl.pallas_call(
        functools.partial(attend_kernel, blocks, blk, tile),
        out_shape=[
            jax.ShapeDtypeStruct((length, cols), BF),
            jax.ShapeDtypeStruct((2 * pairs, length, length), BF),
        ],
        grid_spec=pltpu.PrefetchScalarGridSpec(
            num_scalar_prefetch=1,
            grid=(pairs,),
            in_specs=[piece(0), piece(1), piece(2)],
            out_specs=[
                pl.BlockSpec((length, 128), lambda p, s: (0, p)),
                pl.BlockSpec((2, length, length), lambda p, s: (p, 0, 0)),
            ],
            scratch_shapes=[
                pltpu.VMEM((length, 128), BF),
                pltpu.VMEM((length, 128), BF),
                pltpu.VMEM((length, 128), BF),
                pltpu.VMEM((128, length), F32),
            ],
        ),
        compiler_params=pltpu.CompilerParams(vmem_limit_bytes=60 * 1024 * 1024),
        name="attend",
    )(inv, qkv, qkv, qkv)


def attend_back_kernel(
    blocks, blk, tile, pairs, inv_ref, q_ref, k_ref, v_ref, g_ref, o_ref, p_ref, out_ref,
    qn, kn, vn, gn, on, dqt, dk, dv,
):
    length = blocks * blk
    for i in range(blocks):
        src, dst = pl.ds(pl.multiple_of(inv_ref[i] * blk, blk), blk), pl.ds(i * blk, blk)
        qn[dst, :] = q_ref[src, :]
        kn[dst, :] = k_ref[src, :]
        vn[dst, :] = v_ref[src, :]
        gn[dst, :] = g_ref[src, :]
        on[dst, :] = o_ref[src, :]
    k_turned = kn[...].astype(F32).T.astype(BF)
    prod = (gn[...].astype(F32) * on[...].astype(F32)).T
    deltas = [jnp.sum(prod[64 * h : 64 * h + 64, :], axis=0, keepdims=True) for h in range(2)]
    lane = lax.broadcasted_iota(jnp.int32, (1, 128), 1)
    dk[...] = jnp.zeros_like(dk)
    dv[...] = jnp.zeros_like(dv)
    for i in range(length // tile):
        cols = pl.ds(i * tile, tile)
        keys = (i + 1) * tile
        for h in range(2):
            here = (lane // 64) == h
            q = jnp.where(here, qn[cols, :].astype(F32), 0.0).astype(BF)
            g = jnp.where(here, gn[cols, :].astype(F32), 0.0).astype(BF)
            p = p_ref[h, pl.ds(0, keys), cols]
            dp = dot(vn[pl.ds(0, keys), :], g, NT)
            ds = (
                p.astype(F32) * (dp - deltas[h][:, i * tile : (i + 1) * tile]) * 0.125
            ).astype(BF)
            half = slice(64 * h, 64 * h + 64)
            dqt[half, cols] = dot(k_turned[half, :keys], ds)
            dk[pl.ds(0, keys), :] += dot(ds, q)
            dv[pl.ds(0, keys), :] += dot(p, g)
    dq = dqt[...].T
    pair = pl.program_id(0)
    for i in range(blocks):
        dst = pl.ds(pl.multiple_of(inv_ref[i] * blk, blk), blk)
        src = slice(i * blk, (i + 1) * blk)
        for t, val in enumerate((dq, dk, dv)):
            at = pl.ds(pl.multiple_of((t * pairs + pair) * 128, 128), 128)
            out_ref[dst, at] = val[src, :].astype(BF)


def attend_back(qkv, grad, o, p, inv, blk):
    length = qkv.shape[0]
    cols = qkv.shape[1] // 3
    pairs = cols // 128
    blocks = inv.shape[0]
    tile = 256
    piece = lambda off: pl.BlockSpec((length, 128), lambda i, s: (0, off * pairs + i))
    return pl.pallas_call(
        functools.partial(attend_back_kernel, blocks, blk, tile, pairs),
        out_shape=jax.ShapeDtypeStruct((length, 3 * cols), BF),
        grid_spec=pltpu.PrefetchScalarGridSpec(
            num_scalar_prefetch=1,
            grid=(pairs,),
            in_specs=[
                piece(0),
                piece(1),
                piece(2),
                piece(0),
                piece(0),
                pl.BlockSpec((2, length, length), lambda i, s: (i, 0, 0)),
            ],
            out_specs=pl.BlockSpec((length, 3 * cols), lambda i, s: (0, 0)),
            scratch_shapes=[pltpu.VMEM((length, 128), BF)] * 5
            + [
                pltpu.VMEM((128, length), F32),
                pltpu.VMEM((length, 128), F32),
                pltpu.VMEM((length, 128), F32),
            ],
        ),
        compiler_params=pltpu.CompilerParams(vmem_limit_bytes=60 * 1024 * 1024),
        name="attend_back",
    )(inv, qkv, qkv, qkv, grad, o, p)


def norm(values):
    centre = values - jnp.mean(values, axis=-1, keepdims=True)
    rstd = lax.rsqrt(jnp.mean(centre * centre, axis=-1, keepdims=True) + 1e-05)
    return centre * rstd, rstd


def norm_back(grad, unit, rstd, gain):
    inner = grad * gain
    return rstd * (
        inner
        - jnp.mean(inner, axis=-1, keepdims=True)
        - unit * jnp.mean(inner * unit, axis=-1, keepdims=True)
    )


def make_body(n, nz):
    def body(
        tokens, block_table, ln1_gain, ln1_bias, qkv_weight, query_bias, value_bias,
        proj_weight, proj_bias, ln2_gain, ln2_bias, fc_weight, fc_bias, out_weight,
        out_bias, cotangent,
    ):
        ctx = lax.axis_index("ctx")
        z = lax.axis_index("fsdp")
        rows, width = tokens.shape
        blk = rows // 2
        wz = width // nz
        slots = -(-HEADS // n)
        hw = slots * (width // HEADS)
        unit_z = out_weight.shape[0]
        uw = unit_z // n
        units = uw * nz
        table = block_table.reshape(-1)
        inv = jnp.argmax(
            table[None, :] == jnp.arange(table.shape[0], dtype=table.dtype)[:, None], axis=1
        ).astype(jnp.int32)

        take = lambda a, at, size, axis=0: lax.dynamic_slice_in_dim(a, at, size, axis)
        parts = 5
        padded = jnp.pad(qkv_weight, ((0, 0), (0, n * hw - width)))
        wq_own = jnp.concatenate(
            [take(padded, t * width + ctx * hw, hw, 1) for t in range(3)], axis=1
        ).reshape(parts, wz // parts, 3 * hw)
        wfc_own = jnp.concatenate(
            [take(fc_weight, t * unit_z + ctx * uw, uw, 1) for t in range(nz)], axis=1
        )
        wout_own = take(out_weight, ctx * uw, uw)
        small = jnp.stack(
            [ln1_gain, ln1_bias, query_bias, value_bias, proj_bias, ln2_gain, ln2_bias, out_bias]
            + [jnp.pad(take(fc_bias, ctx * uw, uw), (0, wz - uw))]
            + [jnp.zeros_like(ln1_gain)] * 7
        )
        h1, cot, small, w_qkv, w_proj = entry(
            n, nz, tokens, cotangent, small, wq_own, proj_weight.reshape(wz // 8, 8, width), hw
        )
        small, wfc_own, wout_own = lax.optimization_barrier((small, wfc_own, wout_own))
        w_fc = lax.all_gather(wfc_own, "fsdp", axis=0, tiled=True)
        w_out = lax.all_gather(wout_own, "fsdp", axis=0, tiled=True)
        length = n * rows
        h1, cot = h1.reshape(length, width), cot.reshape(length, width)
        w_qkv, w_proj = w_qkv.reshape(width, 3 * hw), w_proj.reshape(hw, width)
        g1, b1, qb, vb, pb, g2, b2, ob = [small[i] for i in range(8)]
        fb = small[8].reshape(nz, wz)[:, :uw].reshape(-1)
        pad_cols = lambda v: take(jnp.pad(v, (0, n * hw - width)), ctx * hw, hw)
        qkv_bias = jnp.concatenate([pad_cols(qb), jnp.zeros((hw,), F32), pad_cols(vb)])

        cut = 2 if n == 8 else 1
        pieces = lambda a: a.reshape(cut, a.shape[0] // cut, a.shape[1])
        x = tokens.astype(F32)
        unit1, rstd1 = norm(x)
        qkv = (dot(h1, w_qkv) + qkv_bias).astype(BF)
        o, p = attend(qkv, inv, blk)
        mid = x + plane_scatter(n, 5, (o, w_proj, NN))[0] + pb
        unit2, rstd2 = norm(mid)
        h2, o_all = plane_gather(n, 2, pieces((unit2 * g2 + b2).astype(BF)), pieces(o))
        h2 = h2.reshape(length, width)
        hidden, slope = hidden_units(h2, w_fc, fb.reshape(1, units))
        part_out = dot(hidden, cot, TN).astype(BF)
        du, dfb = hidden_back(cot, w_out, slope)
        part_fc = dot(h2, du, TN).astype(BF)
        du, hidden, part_out, part_fc = lax.optimization_barrier((du, hidden, part_out, part_fc))
        to_owner = lambda a: lax.psum_scatter(a, "fsdp", scatter_dimension=0, tiled=True)
        sum_out, sum_fc = to_owner(part_out), to_owner(part_fc)
        dh2, summed = plane_scatter(n, 6, (du, w_fc, NT), (hidden, w_out, NN))
        layer_out = (mid + summed + ob).astype(BF)
        dmid = cotangent.astype(F32) + norm_back(dh2, unit2, rstd2, g2)
        da_own = dmid.astype(BF)
        (da,) = plane_gather(n, 3, pieces(da_own))
        da = da.reshape(length, width)
        do = dot(da, w_proj, NT).astype(BF)
        dqkv = attend_back(qkv, do, o, p, inv, blk)
        part_qkv = dot(h1, dqkv, TN).astype(BF)
        pw = width // n
        part_proj = jnp.einsum(
            "ntk,td->nkd",
            o_all.reshape(n, length, hw),
            take(da, ctx * pw, pw, 1),
            preferred_element_type=F32,
        )
        part_proj = part_proj.reshape(n * hw, pw)[:width].astype(BF)
        spare = -(3 * hw + pw) % 128
        part_attn = jnp.concatenate(
            [part_qkv, part_proj, jnp.zeros((width, spare), BF)], axis=1
        ).reshape(nz, parts, wz // parts, 3 * hw + pw + spare)
        tail_parts = lambda a: a.reshape(parts, a.shape[0] // parts, a.shape[1])
        all_fc, all_out, sum_attn, dh1 = reduce_all(
            n, nz, 9, [tail_parts(sum_fc), tail_parts(sum_out)], part_attn, dqkv, w_qkv, NT
        )
        grad_tokens = (dmid + norm_back(dh1, unit1, rstd1, g1)).astype(BF)

        col_sum = lambda a: jnp.sum(a.astype(F32), axis=0)
        put = lambda v, size: lax.dynamic_update_slice_in_dim(
            jnp.zeros((size,), F32), v, ctx * v.shape[0], 0
        )
        bias_cols = col_sum(dqkv)
        dfb = dfb.reshape(nz, uw)
        rows_of = [
            col_sum(dh1 * unit1),
            col_sum(dh1),
            put(bias_cols[:hw], n * hw)[:width],
            put(bias_cols[2 * hw :], n * hw)[:width],
            col_sum(da_own),
            col_sum(dh2 * unit2),
            col_sum(dh2),
            col_sum(cotangent),
        ]
        wide_fb = lax.dynamic_update_slice_in_dim(jnp.zeros((nz, unit_z), F32), dfb, ctx * uw, 1)
        wide_fb = jnp.pad(wide_fb, ((0, 8 - nz % 8 if nz % 8 else 0), (0, width - unit_z)))
        vectors = jnp.concatenate([jnp.stack(rows_of), wide_fb])

        all_attn, vectors = last_gather(n, nz, 4, sum_attn, vectors)
        whole_rows = lambda a: a.reshape(n, a.shape[1] * a.shape[2], a.shape[3])
        grad_fc, grad_qkv, grad_proj, grad_out = join(
            n, nz, hw, whole_rows(all_fc), whole_rows(all_attn), all_out.reshape(unit_z, width)
        )
        mine = take(vectors[:8], z * wz, wz, 1)
        gfb = take(vectors[8 : 8 + nz], z, 1).reshape(-1)[:unit_z]
        return (
            layer_out,
            grad_tokens,
            mine[0],
            mine[1],
            grad_qkv,
            mine[2],
            mine[3],
            grad_proj,
            mine[4],
            mine[5],
            mine[6],
            grad_fc,
            gfb,
            grad_out,
            mine[7],
        )

    return body


def solution(mesh):
    both = P(("fsdp", "ctx"), None)
    vec, mat = P("fsdp"), P("fsdp", None)
    placed = (both, P(), vec, vec, mat, vec, vec, mat, vec, vec, vec, mat, vec, mat, vec, both)
    outs = (both, both, vec, vec, mat, vec, vec, mat, vec, vec, vec, mat, vec, mat, vec)
    return jax.shard_map(
        make_body(mesh.shape["ctx"], mesh.shape["fsdp"]),
        mesh=mesh,
        in_specs=placed,
        out_specs=outs,
        check_vma=False,
    )
```

time: 918 us -> 535 us (0.58)
  waiting for transfers between devices: 396 us -> 13 us
  Pallas kernels: 189 us -> 413 us
  local copies, waits for them, and re-layouts: 171 us -> 38.1 us
  matrix products: 77.9 us -> 32.7 us
  blocking collectives: 27.9 us -> 0 us
  other arithmetic: 28.8 us -> 17.3 us
    pallas_call x7 -> x10, Pallas kernels: 163 us -> 387 us  [the longest x1 84.5 us: reduce_all(): pl.pallas_call(functools.partial(reduce_kernel, n, nz, len(ready), dims),...]
    psum x3 -> x0, waiting for transfers between devices: 131 us -> none  [the longest x1 126 us: body(): packed = lax.psum(packed, ('fsdp', 'ctx'))]
    all_gather x7 -> x2, waiting for transfers between devices: 135 us -> 8.85 us  [the longest x1 8.83 us: body(): w_out = lax.all_gather(wout_own, 'fsdp', axis=0, tiled=True)]
    convert_element_type x9 -> x0, local copies, waits for them, and re-layouts: 96.3 us -> none  [the longest x3 49 us: body(): grad_fc = part_fc.reshape(n, wz, nz, uw).transpose(1, 2, 0, 3).reshape(wz...]
    reduce_scatter x2 -> x1, waiting for transfers between devices: 74.7 us -> 3.41 us  [body(): lax.psum_scatter(a, 'fsdp', scatter_dimension=0, tiled=True)]
    unnamed x14 -> x5, waiting for transfers between devices: 55.7 us -> 0.75 us
    dot_general x12 -> x5, matrix products: 77.9 us -> 28.6 us  [dot(): return lax.dot_general(a, b, dims, preferred_element_type=F32)]
    reshape x5 -> x2, local copies, waits for them, and re-layouts: 29.5 us -> 6.53 us  [the longest x1 6.45 us: body(): o_all.reshape(n, length, hw)]
  transfers between devices with their start and end apart: 13 -> 4, of which waited for: 9 -> 2; matrix products, arithmetic and copies ran while one was open for 25% -> 10% of each run, Pallas kernels for 14% -> 31%
where the time goes in v2:
time: 535 us; the launch traced here: 528 us
  Pallas kernels  413 us (77%)
  local copies, waits for them, and re-layouts  38.1 us (7%)
  matrix products  32.7 us (6%)
  other arithmetic  17.3 us (3%)
  between operations  14.3 us (3%)
  waiting for transfers between devices  13 us (2%)
    pallas_call x1, Pallas kernels, reduce_all(): pl.pallas_call(functools.partial(reduce_kernel, n, nz, len(ready), dims),...  84.5 us
    pallas_call x1, Pallas kernels, entry(): pl.pallas_call(functools.partial(entry_kernel, n, nz), out_shape=[shape((...  75.3 us
    pallas_call x2, Pallas kernels, plane_scatter(): pl.pallas_call(functools.partial(scatter_kernel, n, [job[2] for job in jo...  69.9 us
    pallas_call x2, Pallas kernels, plane_gather(): pl.pallas_call(functools.partial(gather_kernel, n, count), out_shape=[jax...  59.3 us
    pallas_call x1, Pallas kernels, last_gather(): pl.pallas_call(functools.partial(last_kernel, n, nz), out_shape=[shape((n...  55.8 us
    dot_general x5, matrix products, dot(): return lax.dot_general(a, b, dims, preferred_element_type=F32)  28.6 us
    pallas_call x1, Pallas kernels, join(): pl.pallas_call(functools.partial(join_kernel, n, nz, hw, width), grid=(ti...  25.1 us
    pallas_call x1, Pallas kernels, attend_back(): pl.pallas_call(functools.partial(attend_back_kernel, blocks, blk, tile, p...  13.1 us
  transfers between devices with their start and end apart: 4, of which 2 were waited for; matrix products, arithmetic and copies ran while one was open for 10% of the time, Pallas kernels for 31%

profile of v2, /device:TPU:0, one launch (start us, length us, event | category | flops | bytes accessed | tf_op | source)
XLA Modules:
  0.0 528.4 jit_solution(12998155324135161592)
XLA Ops:
  7.2 0.8 dynamic_slice.42
  8.0 0.7 stack.60
  13.5 2.0 copy.70.tok
  15.4 2.0 copy.72
  17.4 2.0 constant_dynamic-slice_fusion.1
  19.4 1.3 pad_dynamic-slice_fusion.2
  20.7 0.9 pad_maximum_fusion.1
  21.6 1.6 constant_dynamic-slice_fusion.5
  23.2 1.2 pad_maximum_fusion
  24.5 1.3 stack.71.small
  25.7 75.3 %entry.1 = (bf16[8,4,32,1600]{3,2,1,0:T(8,128)(2,1)}, bf16[8,4,32,1600]{3,2,1,0:T(8,128)(2,1)}, f32[16,1600]{1,0:T(8,128)}, bf16[20,80,768]{2,1,0:T(8,128)(2,1)}, bf16[32,8,1600]{2,1,0:T(8,128)(2,1)}) custom-call(bf16[128,1600]{1,0:T(8,128)(2,1)} %copy.70.tok, bf16[4,32,1600]{2,1,0:T(8,128)(2,1)} %bitcast.53, bf16[16,400]{1,0:T(8,128)(2,1)} %stack.71.small, ...), custom_call_target="tpu_custom_call" | custom-call | tf_op jit(solution)/shard_map/entry/pallas_call | solution.py:321
  101.1 0.7 all-gather.3.cloned.1.call-update
  102.2 1.3 slice_reduce_fusion
  105.1 7.0 %add_convert_fusion.q_ref.k_ref.v_ref = bf16[1024,768]{1,0:T(8,128)(2,1)} fusion(bf16[1024,1600]{1,0:T(8,128)(2,1)} %bitcast.79, bf16[1600,768]{1,0:T(8,128)(2,1)} %bitcast.60, f32[768]{0:T(1024)S(1)} %pad_maximum_fusion.2), kind=kOutput, calls=%fused_computation.8 | convolution fusion | flops 2518155264 | bytes 7310336 | tf_op jit(solution)/shard_map/dot_general | solution.py:22
  112.0 12.5 %attend.1 = (bf16[1024,256]{1,0:T(8,128)(2,1)}, bf16[4,1024,1024]{2,1,0:T(8,128)(2,1)}) custom-call(s32[16]{0:T(128)} %get-tuple-element.48.inv_ref, bf16[1024,768]{1,0:T(8,128)(2,1)} %add_convert_fusion.q_ref.k_ref.v_ref, bf16[1024,768]{1,0:T(8,128)(2,1)} %add_convert_fusion.q_ref.k_ref.v_ref, bf16[1024,768]{1,0:T(8,128)(2,1)} %add_convert_fusion.q_ref.k_ref.v_ref), custom_call_target="tpu_custom_call" | custom-call | tf_op jit(solution)/shard_map/attend/pallas_call | solution.py:935
  124.5 30.3 %plane_scatter_5.1 = f32[128,1600]{1,0:T(8,128)} custom-call(bf16[1024,256]{1,0:T(8,128)(2,1)} %get-tuple-element.53.refs_0_.o_ref, bf16[256,1600]{1,0:T(8,128)(2,1)} %bitcast.66), custom_call_target="tpu_custom_call" | custom-call | tf_op jit(solution)/shard_map/plane_scatter_5/pallas_call | solution.py:541
  155.0 1.5 fusion.17
  156.8 1.0 add_convert_fusion.2
  157.7 39.1 %plane_gather_2.1 = (bf16[8,2,64,1600]{3,2,1,0:T(8,128)(2,1)}, bf16[8,2,512,256]{3,2,1,0:T(8,128)(2,1)}) custom-call(bf16[2,64,1600]{2,1,0:T(8,128)(2,1)} %bitcast.64, bf16[2,512,256]{2,1,0:T(8,128)(2,1)} %bitcast.50), custom_call_target="tpu_custom_call" | custom-call | tf_op jit(solution)/shard_map/plane_gather_2/pallas_call | solution.py:368
  196.9 9.2 %hidden.1 = (bf16[1024,800]{1,0:T(8,128)(2,1)}, bf16[1024,800]{1,0:T(8,128)(2,1)}) custom-call(bf16[1024,1600]{1,0:T(8,128)(2,1)} %bitcast.56, bf16[1600,800]{1,0:T(8,128)(2,1)} %all-gather.5.cloned.1.call-done.w_ref.refs_1_, f32[1,800]{1,0:T(1,128)} %reshape_reshape.9.b_ref), custom_call_target="tpu_custom_call" | custom-call | tf_op jit(solution)/shard_map/hidden/pallas_call | solution.py:820
  206.1 7.2 %convolution_convert_fusion.1 = bf16[800,1600]{1,0:T(8,128)(2,1)} fusion(bf16[1024,800]{1,0:T(8,128)(2,1)} %get-tuple-element.63.refs_2_, bf16[1024,1600]{1,0:T(8,128)(2,1)} %bitcast.54), kind=kOutput, calls=%fused_computation.4 | convolution fusion | flops 2622720000 | bytes 7475200 | tf_op jit(solution)/shard_map/dot_general | solution.py:22
  213.3 8.8 %all-gather.3.cloned.1.call-done.w_ref.refs_3_ = bf16[800,1600]{1,0:T(8,128)(2,1)} async-done(((bf16[200,1600]{1,0:T(8,128)(2,1)}), bf16[800,1600]{1,0:T(8,128)(2,1)}) %all-gather.3.cloned.1.call-update) | async-done | bytes 2560016 | tf_op jit(solution)/shard_map/all_gather | solution.py:1095
  222.1 7.9 %hidden_back.1 = (bf16[1024,800]{1,0:T(8,128)(2,1)}, f32[1,800]{1,0:T(1,128)}) custom-call(bf16[1024,1600]{1,0:T(8,128)(2,1)} %bitcast.55, bf16[800,1600]{1,0:T(8,128)(2,1)} %all-gather.3.cloned.1.call-done.w_ref.refs_3_, bf16[1024,800]{1,0:T(8,128)(2,1)} %get-tuple-element.59.s_ref), custom_call_target="tpu_custom_call" | custom-call | tf_op jit(solution)/shard_map/hidden_back/pallas_call | solution.py:834
  230.1 7.2 %convolution_convert_fusion = bf16[1600,800]{0,1:T(8,128)(2,1)} fusion(bf16[1024,1600]{1,0:T(8,128)(2,1)} %bitcast.57, bf16[1024,800]{1,0:T(8,128)(2,1)} %get-tuple-element.62.refs_0_), kind=kOutput, calls=%fused_computation.3 | convolution fusion | flops 2622720000 | bytes 7475200 | tf_op jit(solution)/shard_map/dot_general | solution.py:22
  237.3 5.7 %copy.80 = bf16[1600,800]{1,0:T(8,128)(2,1)} copy(bf16[1600,800]{0,1:T(8,128)(2,1)} %convolution_convert_fusion) | data formatting | bytes 5120000
  243.0 6.5 %copy.76 = bf16[8,1024,256]{1,2,0:T(8,128)(2,1)} copy(bf16[8,1024,256]{2,1,0:T(8,128)(2,1)} %bitcast.51) | data formatting | bytes 8388608 | tf_op jit(solution)/shard_map/reshape | solution.py:1133
  249.7 39.6 %plane_scatter_6.1 = (f32[128,1600]{1,0:T(8,128)}, f32[128,1600]{1,0:T(8,128)}) custom-call(bf16[1024,800]{1,0:T(8,128)(2,1)} %get-tuple-element.62.refs_0_, bf16[1600,800]{1,0:T(8,128)(2,1)} %all-gather.5.cloned.1.call-done.w_ref.refs_1_, bf16[1024,800]{1,0:T(8,128)(2,1)} %get-tuple-element.63.refs_2_, ...), custom_call_target="tpu_custom_call" | custom-call | tf_op jit(solution)/shard_map/plane_scatter_6/pallas_call | solution.py:541
  289.3 1.5 multiply_reduce_fusion
  290.8 2.8 convert_reduce_fusion.3
  293.6 0.9 copy.78
  294.6 20.2 %plane_gather_3.1 = bf16[8,2,64,1600]{3,2,1,0:T(8,128)(2,1)} custom-call(bf16[2,64,1600]{2,1,0:T(8,128)(2,1)} %bitcast.63), custom_call_target="tpu_custom_call" | custom-call | tf_op jit(solution)/shard_map/plane_gather_3/pallas_call | solution.py:368
  314.8 4.1 fusion.13
  319.0 1.9 convolution_convert_fusion.3.g_ref
  320.9 13.1 %attend_back.1.refs_3_ = bf16[1024,768]{1,0:T(8,128)(2,1)} custom-call(s32[16]{0:T(128)} %get-tuple-element.48.inv_ref, bf16[1024,768]{1,0:T(8,128)(2,1)} %add_convert_fusion.q_ref.k_ref.v_ref, bf16[1024,768]{1,0:T(8,128)(2,1)} %add_convert_fusion.q_ref.k_ref.v_ref, bf16[1024,768]{1,0:T(8,128)(2,1)} %add_convert_fusion.q_ref.k_ref.v_ref, ...), custom_call_target="tpu_custom_call" | custom-call | tf_op jit(solution)/shard_map/attend_back/pallas_call | solution.py:1012
  334.0 1.7 convert_reduce_fusion
  336.7 5.2 convolution_convert_fusion.2
  341.9 2.6 maximum_maximum_fusion
  344.5 3.4 reduce-scatter.7.cloned.1.call-done
  347.9 84.5 %reduce_all.1 = (bf16[8,5,80,800]{3,2,1,0:T(8,128)(2,1)}, bf16[8,5,40,1600]{3,2,1,0:T(8,128)(2,1)}, bf16[5,80,1024]{2,1,0:T(8,128)(2,1)}, f32[128,1600]{1,0:T(8,128)}) custom-call(bf16[5,80,800]{2,1,0:T(8,128)(2,1)} %bitcast.67, bf16[5,40,1600]{2,1,0:T(8,128)(2,1)} %bitcast.68, bf16[4,5,80,1024]{3,2,1,0:T(8,128)(2,1)} %bitcast.46, ...), custom_call_target="tpu_custom_call" | custom-call | tf_op jit(solution)/shard_map/reduce_all/pallas_call | solution.py:672
  432.4 1.6 fusion.10
  434.0 1.3 concatenate.19.vec
  435.4 55.8 %last_gather.1 = (bf16[8,5,80,1024]{3,2,1,0:T(8,128)(2,1)}, f32[16,1600]{1,0:T(8,128)}) custom-call(bf16[5,80,1024]{2,1,0:T(8,128)(2,1)} %get-tuple-element.71.src, f32[16,1600]{1,0:T(8,128)} %concatenate.19.vec), custom_call_target="tpu_custom_call" | custom-call | tf_op jit(solution)/shard_map/last_gather/pallas_call | solution.py:775
  491.2 0.8 slice.95
  492.0 0.8 slice.87
  492.8 1.5 fusion.9
  494.4 0.9 copy.79
  495.9 25.1 %join.1 = (f32[400,6400]{1,0:T(8,128)}, f32[400,4800]{1,0:T(8,128)}, f32[400,1600]{1,0:T(8,128)}, f32[1600,1600]{1,0:T(8,128)}) custom-call(bf16[8,25,16,800]{3,2,1,0:T(8,128)(2,1)} %bitcast.48, bf16[8,25,16,1024]{3,2,1,0:T(8,128)(2,1)} %bitcast.47, bf16[1600,1600]{1,0:T(8,128)(2,1)} %bitcast.49), custom_call_target="tpu_custom_call" | custom-call | tf_op jit(solution)/shard_map/join/pallas_call | solution.py:873
  521.0 0.7 fusion.19
  (77 shorter events, 9.1 us)
Async XLA Ops:
  7.2 189.7 %all-gather.5.cloned.1.call-start = ((), (), s32[]{:S(2)}) async-start(), calls=%async_computation.3 | async-start | bytes 3584000 | tf_op jit(solution)/shard_map/all_gather | solution.py:1094
  23.2 78.9 %copy-start.6 = (s32[8,2]{0,1:T(2,128)S(1)}, s32[8,2]{0,1:T(2,128)}, u32[]{:S(2)}) copy-start(s32[8,2]{0,1:T(2,128)} %param.17) | copy-start | bytes 196
  101.1 121.0 %all-gather.3.cloned.1.call-start = ((), (), s32[]{:S(2)}) async-start(), calls=%async_computation.2 | async-start | bytes 3328000 | tf_op jit(solution)/shard_map/all_gather | solution.py:1095
  101.8 242.6 %reduce-scatter.9.cloned.1.call-start = ((), (), s32[]{:S(2)}) async-start(), calls=%async_computation.5 | async-start | bytes 3328000
  112.0 42.8 %copy-start = (bf16[128,1600]{1,0:T(8,128)(2,1)S(1)}, bf16[128,1600]{1,0:T(8,128)(2,1)}, u32[]{:S(2)}) copy-start(bf16[128,1600]{1,0:T(8,128)(2,1)} %copy.70.tok) | copy-start | bytes 1228804
  237.3 110.6 %reduce-scatter.7.cloned.1.call-start = ((), (), s32[]{:S(2)}) async-start(), calls=%async_computation.4 | async-start | bytes 3584000 | tf_op jit(solution)/shard_map/reduce_scatter | solution.py:1119
  243.0 6.6 %copy-start.5 = (f32[1,800]{1,0:T(1,128)S(1)}, f32[1,800]{1,0:T(1,128)}, u32[]{:S(2)}) copy-start(f32[1,800]{1,0:T(1,128)} %get-tuple-element.72) | copy-start | bytes 9604
  249.7 41.1 %copy-start.1 = (bf16[128,1600]{1,0:T(8,128)(2,1)S(1)}, bf16[128,1600]{1,0:T(8,128)(2,1)}, u32[]{:S(2)}) copy-start(bf16[128,1600]{1,0:T(8,128)(2,1)} %copy.72) | copy-start | bytes 1228804
  314.8 4.2 copy-start.2
  314.8 4.2 copy-start.4
  318.9 2.0 copy-start.3
  320.9 15.2 %slice-start = ((bf16[2048,200]{0,1:T(8,128)(2,1)}), bf16[1600,200]{0,1:T(8,128)(2,1)S(1)}, s32[]{:S(2)}) async-start(bf16[2048,200]{0,1:T(8,128)(2,1)} %copy-done.3), calls=%async_computation.6 | async-start | bytes 1331200 | tf_op jit(solution)/shard_map/slice | solution.py:1137
Sparse Core Ops, SparseCore 0:
  101.2 64.5 all-gather.4
  168.0 54.0 all-gather.2
  237.4 51.1 reduce-scatter.8
  291.3 56.5 reduce-scatter.6

commit v3 on v2

--- a/solution.py
+++ b/solution.py
@@ -1,4 +1,5 @@
 import functools
+import math
 
 import jax
 import jax.numpy as jnp
@@ -67,10 +68,11 @@
     )
 
 
-def merge(*lists):
+def merge(*lists, scales=None):
     keyed = []
     for t, steps in enumerate(lists):
-        keyed += [((i + 0.5) / len(steps), t, i, step) for i, step in enumerate(steps)]
+        scale = scales[t] if scales else 1.0
+        keyed += [((i + 0.5) * scale / len(steps), t, i, step) for i, step in enumerate(steps)]
     for item in sorted(keyed, key=lambda k: k[:3]):
         item[3]()
 
@@ -96,32 +98,26 @@
         far = n // 2 - 1
         return [dma((parts,)), dma((far + 1, parts)), dma((far + 1, parts)), dma((far, parts)), dma((far, parts))]
 
+    def own_sends(self, c):
+        piece, slot = self.src.at[c], self.out.at[self.me, c]
+        copies = [
+            send(piece, slot, self.far_s.at[d, c], self.far_r.at[d, c], ctx=2 * p + self.core)
+            for d, p in enumerate(self.peers)
+        ]
+        copies.append(send(piece, slot, self.sib_s.at[0, c], self.sib_r.at[0, c], ctx=self.sib))
+        return copies + [pltpu.make_async_copy(piece, slot, self.own_s.at[c])]
+
     def go(self, copy):
         copy.start()
         self.started.append(copy)
 
     def start(self):
-        self.locals = []
         for c in range(self.parts):
-            piece = self.src.at[c]
-            for d, p in enumerate(self.peers):
-                self.go(
-                    send(
-                        piece,
-                        self.out.at[self.me, c],
-                        self.far_s.at[d, c],
-                        self.far_r.at[d, c],
-                        ctx=2 * p + self.core,
-                    )
-                )
-            self.go(
-                send(
-                    piece, self.out.at[self.me, c], self.sib_s.at[0, c], self.sib_r.at[0, c], ctx=self.sib
-                )
-            )
-            own = pltpu.make_async_copy(piece, self.out.at[self.me, c], self.own_s.at[c])
-            own.start()
-            self.locals.append(own)
+            self.start_part(c)
+
+    def start_part(self, c):
+        for copy in self.own_sends(c):
+            copy.start()
 
     def arrived(self, d, c):
         piece = self.out.at[2 * self.froms[d] + self.core, c]
@@ -151,8 +147,11 @@
         return todo
 
     def finish(self):
-        for own in self.locals:
+        for c in range(self.parts):
+            *far, own = self.own_sends(c)
             own.wait()
+            for copy in far:
+                copy.wait_send()
         for d in range(len(self.others) + 1):
             chip = self.chip if d == 0 else self.froms[d - 1]
             for c in range(self.parts):
@@ -249,24 +248,31 @@
     return [lax.rem(z + d, nz) for d in range(1, nz)]
 
 
-def entry_kernel(n, nz, tok, cot, small, wq, wp, h1_all, cot_all, vec, wq_all, wp_all, *scratch):
-    h1, inbox, zeros, small_s, small_r, zero_s = scratch[:6]
-    g_h, g_c = scratch[6:11], scratch[11:16]
-    r_q, r_p = scratch[16:20], scratch[20:24]
+def entry_kernel(
+    n, nz, tok_t, cot_t, small, wq, wp, h1_all, cot_all, vec, wq_all, wp_all, tok, cot_own, *scratch
+):
+    cot, h1, inbox, zeros, small_s, small_r, zero_s = scratch[:7]
+    g_h, g_c = scratch[7:12], scratch[12:17]
+    r_q, r_p = scratch[17:21], scratch[21:25]
     me, core, chip, sib, others = places(n)
     z = lax.axis_index("fsdp")
     planes = others_of(z, nz)
     greet([sib] + [2 * p + core for p in (others[:2] if n == 8 else others)], planes)
-    width = tok.shape[1]
     wz = small.shape[1]
     for d, plane in enumerate(planes):
         send(small, inbox.at[z], small_s.at[d], small_r.at[d], fsdp=plane).start()
     inbox[z] = small[...]
-    gather_c = Gather(n, cot, cot_all, g_c)
-    gather_c.start()
     k = wq.shape[0]
     relay_q = Relay(nz, z, z * k, (z + 1) * k, nz * k, wq, wq_all, r_q, z * k)
     relay_q.start()
+    parts, rows = h1.shape[0], h1.shape[1]
+    turned = cot_t[...].astype(F32).T.astype(BF)
+    cot_own[...] = turned
+    for c in range(parts):
+        cot[c] = turned[c * rows : (c + 1) * rows, :]
+    gather_c = Gather(n, cot, cot_all, g_c)
+    gather_c.start()
+    tok[...] = tok_t[...].astype(F32).T.astype(BF)
     share, blocks = wp.shape[0], wp_all.shape[0]
     base = me * blocks
     valid = jnp.clip(nz * share - base, 0, blocks)
@@ -287,12 +293,11 @@
     for p in range(nz):
         vec[:, p * wz : (p + 1) * wz] = inbox[p].astype(F32)
     gain, shift = vec[0:1, :], vec[1:2, :]
-    parts, rows = h1.shape[0], h1.shape[1]
+    gather_h = Gather(n, h1, h1_all, g_h)
     for c in range(parts):
         unit, _ = norm(tok[c * rows : (c + 1) * rows, :].astype(F32))
         h1[c] = (unit * gain + shift).astype(BF)
-    gather_h = Gather(n, h1, h1_all, g_h)
-    gather_h.start()
+        gather_h.start_part(c)
     merge(
         gather_c.steps() + gather_h.steps(),
         relay_q.steps(nz * k - k) + relay_p.steps(blocks),
@@ -313,9 +318,10 @@
 
 def entry(n, nz, tokens, cot, small, wq, wp, hw):
     rows, width = tokens.shape
-    parts = 4 if n == 8 else 1
+    parts = 2 if n == 8 else 1
     dma = pltpu.SemaphoreType.DMA
-    k, blocks = wq.shape[0], hw // 8
+    k, tile = wq.shape[0], wp.shape[1]
+    blocks = hw // tile
     shape = jax.ShapeDtypeStruct
     piece = (parts, rows // parts, width)
     return pl.pallas_call(
@@ -325,14 +331,17 @@
             shape((n,) + piece, BF),
             shape((small.shape[0], width), F32),
             shape((nz * k,) + wq.shape[1:], BF),
-            shape((blocks, 8, width), BF),
+            shape((blocks, tile, width), BF),
+            shape((rows, width), BF),
+            shape((rows, width), BF),
         ],
         in_specs=[VMEM] * 5,
-        out_specs=[ANY, ANY, VMEM, ANY, ANY],
+        out_specs=[ANY, ANY, VMEM, ANY, ANY, VMEM, VMEM],
         scratch_shapes=[
             pltpu.VMEM(piece, BF),
+            pltpu.VMEM(piece, BF),
             pltpu.VMEM((nz,) + small.shape, BF),
-            pltpu.VMEM((8, width), BF),
+            pltpu.VMEM((tile, width), BF),
             dma((nz - 1,)),
             dma((nz - 1,)),
             dma((blocks,)),
@@ -343,42 +352,12 @@
         + Relay.sems(blocks),
         compiler_params=pltpu.CompilerParams(collective_id=1, has_side_effects=True),
         name="entry",
-    )(tokens, cot.reshape(piece), small, wq, wp)
-
-
-def gather_kernel(n, count, *refs):
-    ins, outs, sems = refs[:count], refs[count : 2 * count], refs[2 * count :]
-    me, core, chip, sib, others = places(n)
-    greet([sib] + [2 * p + core for p in (others[:2] if n == 8 else others)])
-    gathers = [Gather(n, ins[j], outs[j], sems[5 * j : 5 * j + 5]) for j in range(count)]
-    for g in gathers:
-        g.start()
-    for g in gathers:
-        for step in g.steps():
-            step()
-    for g in gathers:
-        g.finish()
-
-
-def plane_gather(n, cid, *arrays):
-    count = len(arrays)
-    sems = []
-    for a in arrays:
-        sems += Gather.sems(n, a.shape[0])
-    return pl.pallas_call(
-        functools.partial(gather_kernel, n, count),
-        out_shape=[jax.ShapeDtypeStruct((n,) + a.shape, a.dtype) for a in arrays],
-        in_specs=[VMEM] * count,
-        out_specs=[ANY] * count,
-        scratch_shapes=sems,
-        compiler_params=pltpu.CompilerParams(collective_id=cid, has_side_effects=True),
-        name=f"plane_gather_{cid}",
-    )(*arrays)
+    )(tokens.T, cot.T, small, wq, wp)
 
 
 class Scatter:
-    def __init__(self, n, dims, a, w, out, scratch):
-        self.n, self.dims, self.a, self.w, self.out = n, dims, a, w, out
+    def __init__(self, n, dims, a, w, scratch):
+        self.n, self.dims, self.a, self.w = n, dims, a, w
         self.part, self.theirs, self.sums, self.inbox = scratch[:4]
         self.sib_s, self.sib_r, self.far_s, self.far_r = scratch[4:]
         self.me, self.core, self.chip, self.sib, self.others = places(n)
@@ -396,7 +375,7 @@
     @staticmethod
     def scratch(n, rows, width):
         dma = pltpu.SemaphoreType.DMA
-        half, parts = n // 2, 2 if n == 8 else 1
+        half, parts = n // 2, 4 if n == 8 else 1
         return [
             pltpu.VMEM((half, 2, rows, width), BF),
             pltpu.VMEM((half, rows, width), BF),
@@ -484,18 +463,15 @@
 
         lax.fori_loop(0, self.half, product, 0)
 
-    def own(self, c):
-        self.out[self.win(c), :] = self.chip_sum(self.half - 1, c)
-
-    def add(self, slot, c):
-        self.out[self.win(c), :] += self.wait_in(slot, c)
-
-    def steps(self):
+    def forwards(self):
         each = range(self.parts)
-        todo = [functools.partial(self.forward, e, c) for e in range(1, self.half - 1) for c in each]
-        todo += [functools.partial(self.own, c) for c in each]
-        slots = (1, 2) if self.square else range(self.half - 1)
-        return todo + [functools.partial(self.add, s, c) for s in slots for c in each]
+        return [functools.partial(self.forward, e, c) for e in range(1, self.half - 1) for c in each]
+
+    def total(self, c):
+        val = self.chip_sum(self.half - 1, c)
+        for slot in (1, 2) if self.square else range(self.half - 1):
+            val = val + self.wait_in(slot, c)
+        return val
 
     def finish(self):
         for c in range(self.parts):
@@ -510,57 +486,16 @@
         lax.fori_loop(0, self.half, sent, 0)
 
 
-def scatter_kernel(n, dims, *refs):
-    count = len(dims)
-    ins, outs, scratch = refs[: 2 * count], refs[2 * count : 3 * count], refs[3 * count :]
-    me, core, chip, sib, others = places(n)
-    greet([sib] + [2 * p + core for p in (others[:2] if n == 8 else others)])
-    jobs = [
-        Scatter(n, dims[j], ins[2 * j], ins[2 * j + 1], outs[j], scratch[8 * j : 8 * j + 8])
-        for j in range(count)
-    ]
-    steps = []
-    for job in jobs:
-        job.products()
-        todo = job.steps()
-        for step in todo[: job.parts]:
-            step()
-        steps += todo[job.parts :]
-    for step in steps:
-        step()
-    for job in jobs:
-        job.finish()
-
-
-def plane_scatter(n, cid, *jobs):
-    rows = jobs[0][0].shape[0] // n
-    widths = [w.shape[1] if dims is NN else w.shape[0] for _, w, dims in jobs]
-    scratch = []
-    for width in widths:
-        scratch += Scatter.scratch(n, rows, width)
-    return pl.pallas_call(
-        functools.partial(scatter_kernel, n, [job[2] for job in jobs]),
-        out_shape=[jax.ShapeDtypeStruct((rows, width), F32) for width in widths],
-        in_specs=[VMEM] * (2 * len(jobs)),
-        out_specs=[VMEM] * len(jobs),
-        scratch_shapes=scratch,
-        compiler_params=pltpu.CompilerParams(
-            collective_id=cid, has_side_effects=True, vmem_limit_bytes=60 * 1024 * 1024
-        ),
-        name=f"plane_scatter_{cid}",
-    )(*[x for a, w, _ in jobs for x in (a, w)])
-
-
 class Line:
     def __init__(self, nz, z, src, out, scratch):
         self.nz, self.z, self.src, self.out = nz, z, src, out
-        self.mine, self.above, self.below, self.up_s, self.down_s, self.recv = scratch
+        self.mine, self.above, self.below, self.load_s, self.up_s, self.down_s, self.recv = scratch
         self.parts = src.shape[1]
 
     @staticmethod
     def scratch(shape):
         dma, lead = pltpu.SemaphoreType.DMA, shape[:2]
-        return [pltpu.VMEM(shape, BF)] * 3 + [dma(lead), dma(lead), dma((2,) + lead)]
+        return [pltpu.VMEM(shape, BF)] * 3 + [dma((1,)), dma(lead), dma(lead), dma((2,) + lead)]
 
     def up(self, src, d, c):
         return send(
@@ -585,43 +520,66 @@
                 for c in range(self.parts):
                     self.down(self.src, self.nz - 1 - d, c).start()
 
-    def step_up(self, d, c):
-        @pl.when((self.z > 0) & (self.z < d))
-        def _():
-            copy = self.up(self.mine, d, c)
-            copy.wait_recv()
-            self.mine[d, c] = (self.src[d, c].astype(F32) + self.above[d, c].astype(F32)).astype(BF)
-            copy.start()
-
-    def step_down(self, d, c):
-        @pl.when((self.z < self.nz - 1) & (self.z > d))
-        def _():
-            copy = self.down(self.mine, d, c)
-            copy.wait_recv()
-            self.mine[d, c] = (self.src[d, c].astype(F32) + self.below[d, c].astype(F32)).astype(BF)
-            copy.start()
-
-    def settle(self, c):
-        z = self.z
-        self.out[c] = self.src[z, c]
-
-        @pl.when(z > 0)
-        def _():
+        self.load = pltpu.make_async_copy(self.src, self.mine, self.load_s.at[0])
+        self.load.start()
+
+    def loaded(self):
+        self.load.wait()
+
+    def pass_up(self, d, c):
+        copy = self.up(self.mine, d, c)
+        copy.wait_recv()
+        self.mine[d, c] = self.mine[d, c] + self.above[d, c]
+        copy.start()
+
+    def pass_down(self, d, c):
+        copy = self.down(self.mine, d, c)
+        copy.wait_recv()
+        self.mine[d, c] = self.mine[d, c] + self.below[d, c]
+        copy.start()
+
+    def settle(self, place, c):
+        z, top = place, self.nz - 1
+        total = self.mine[z, c].astype(F32)
+        if z > 0:
             self.up(self.mine, z, c).wait_recv()
-            self.out[c] = (self.out[c].astype(F32) + self.above[z, c].astype(F32)).astype(BF)
-
-        @pl.when(z < self.nz - 1)
-        def _():
+            total = total + self.above[z, c].astype(F32)
+        if z < top:
             self.down(self.mine, z, c).wait_recv()
-            self.out[c] = (self.out[c].astype(F32) + self.below[z, c].astype(F32)).astype(BF)
-
-    def steps(self):
-        todo = []
-        for d in range(self.nz - 1, 1, -1):
-            for c in range(self.parts):
-                todo.append(functools.partial(self.step_up, d, c))
-                todo.append(functools.partial(self.step_down, self.nz - 1 - d, c))
-        return todo + [functools.partial(self.settle, c) for c in range(self.parts)]
+            total = total + self.below[z, c].astype(F32)
+        self.out[c] = total.astype(BF)
+
+    def steps(self, after=None):
+        top, parts = self.nz - 1, self.parts
+        slots = {}
+
+        def put(time, place, fn):
+            slots.setdefault(time, {}).setdefault(place, []).append(fn)
+
+        for place in range(self.nz):
+            for k in range(1, self.nz):
+                for c in range(parts):
+                    at = (k - 1) * parts + c
+                    if 0 < place < top - k + 1:
+                        put(at + place, place, functools.partial(self.pass_up, top - k + 1, c))
+                    if k - 1 < place < top:
+                        put(at + top - place, place, functools.partial(self.pass_down, k - 1, c))
+            for c in range(parts):
+                up = (top - place) * parts + c + place if place > 0 else 0
+                down = place * parts + c + top - place if place < top else 0
+                put(max(up, down), place, functools.partial(self.settle, place, c))
+                if after:
+                    put(max(up, down), place, functools.partial(after, c))
+
+        def run(work):
+            for place, fns in sorted(work.items()):
+
+                @pl.when(self.z == place)
+                def _():
+                    for fn in fns:
+                        fn()
+
+        return [self.loaded] + [functools.partial(run, slots[t]) for t in sorted(slots)]
 
     def finish(self):
         for d in range(self.nz):
@@ -635,52 +593,6 @@
             def _():
                 for c in range(self.parts):
                     self.down(self.mine, d, c).wait_send()
-
-
-def reduce_kernel(n, nz, gcount, dims, *refs):
-    g_in, refs = refs[:gcount], refs[gcount:]
-    line_in, a_in, w_in = refs[:3]
-    refs = refs[3:]
-    g_out, refs = refs[:gcount], refs[gcount:]
-    line_out, out = refs[:2]
-    refs = refs[2:]
-    me, core, chip, sib, others = places(n)
-    z = lax.axis_index("fsdp")
-    greet([sib] + [2 * p + core for p in (others[:2] if n == 8 else others)], others_of(z, nz))
-    line = Line(nz, z, line_in, line_out, refs[:6])
-    line.start()
-    scatter = Scatter(n, dims, a_in, w_in, out, refs[6:14])
-    scatter.products()
-    gathers = [
-        Gather(n, g_in[j], g_out[j], refs[14 + 5 * j : 19 + 5 * j]) for j in range(gcount)
-    ]
-    plane_steps = []
-    for g in gathers:
-        g.start()
-        plane_steps += g.steps()
-    merge(plane_steps, line.steps(), scatter.steps())
-    for job in gathers + [line, scatter]:
-        job.finish()
-
-
-def reduce_all(n, nz, cid, ready, partial, a, w, dims):
-    rows, width = a.shape[0] // n, w.shape[0]
-    scratch = Line.scratch(partial.shape) + Scatter.scratch(n, rows, width)
-    for r in ready:
-        scratch += Gather.sems(n, r.shape[0])
-    shape = jax.ShapeDtypeStruct
-    return pl.pallas_call(
-        functools.partial(reduce_kernel, n, nz, len(ready), dims),
-        out_shape=[shape((n,) + r.shape, BF) for r in ready]
-        + [shape(partial.shape[1:], BF), shape((rows, width), F32)],
-        in_specs=[VMEM] * (len(ready) + 3),
-        out_specs=[ANY] * len(ready) + [VMEM] * 2,
-        scratch_shapes=scratch,
-        compiler_params=pltpu.CompilerParams(
-            collective_id=cid, has_side_effects=True, vmem_limit_bytes=60 * 1024 * 1024
-        ),
-        name="reduce_all",
-    )(*ready, partial, a, w)
 
 
 class Vectors:
@@ -757,30 +669,240 @@
             self.to_plane(d).wait_send()
 
 
-def last_kernel(n, nz, src, vec, out, vec_out, *scratch):
+def beside(n):
     me, core, chip, sib, others = places(n)
+    return [sib] + [2 * p + core for p in (others[:2] if n == 8 else others)]
+
+
+def call(kernel, cid, name, ins, in_specs, outs, out_specs, scratch):
+    return pl.pallas_call(
+        kernel,
+        out_shape=[jax.ShapeDtypeStruct(*o) for o in outs],
+        in_specs=in_specs,
+        out_specs=out_specs,
+        scratch_shapes=scratch,
+        compiler_params=pltpu.CompilerParams(
+            collective_id=cid, has_side_effects=True, vmem_limit_bytes=60 * 1024 * 1024
+        ),
+        name=name,
+    )(*ins)
+
+
+def middle_kernel(n, o, w, tok, vec, mid, h2_all, h2, *scratch):
+    greet(beside(n))
+    scatter = Scatter(n, NN, o, w, scratch[:8])
+    gather = Gather(n, h2, h2_all, scratch[8:])
+    scatter.products()
+    for step in scatter.forwards():
+        step()
+    for c in range(gather.parts):
+        win = scatter.win(c)
+        val = tok[win, :].astype(F32) + scatter.total(c) + vec[4:5, :]
+        mid[win, :] = val
+        h2[c] = (norm(val)[0] * vec[5:6, :] + vec[6:7, :]).astype(BF)
+        gather.start_part(c)
+    for step in gather.steps():
+        step()
+    gather.finish()
+    scatter.finish()
+
+
+def middle(n, cid, o, w, tok, vec):
+    rows, width = tok.shape
+    parts = 4 if n == 8 else 1
+    piece = (parts, rows // parts, width)
+    return call(
+        functools.partial(middle_kernel, n),
+        cid,
+        "middle",
+        (o, w, tok, vec),
+        [VMEM] * 4,
+        [((rows, width), F32), ((n,) + piece, BF)],
+        [VMEM, ANY],
+        [pltpu.VMEM(piece, BF)] + Scatter.scratch(n, rows, width) + Gather.sems(n, parts),
+    )
+
+
+def spread_kernel(n, src, all_ref, *sems):
+    greet(beside(n))
+    gather = Gather(n, src, all_ref, sems)
+    gather.start()
+    for step in gather.steps():
+        step()
+    gather.finish()
+
+
+def spread(n, cid, array):
+    return call(
+        functools.partial(spread_kernel, n),
+        cid,
+        "spread",
+        (array,),
+        [VMEM],
+        [((n,) + array.shape, BF)],
+        [ANY],
+        Gather.sems(n, array.shape[0]),
+    )[0]
+
+
+def turn_kernel(n, du, w_fc, hid, w_out, mid, cot, vec, da_all, dmid, layer, sums, da, *scratch):
+    greet(beside(n))
+    back = Scatter(n, NT, du, w_fc, scratch[:8])
+    ahead = Scatter(n, NN, hid, w_out, scratch[8:16])
+    gather = Gather(n, da, da_all, scratch[16:])
+    back.products()
+    todo = back.forwards()
+    for step in todo[: back.parts]:
+        step()
+    ahead.products()
+    for step in todo[back.parts :]:
+        step()
+    sums[...] = jnp.zeros_like(sums)
+    for c in range(gather.parts):
+        win = back.win(c)
+        grad = back.total(c)
+        unit, rstd = norm(mid[win, :])
+        up = cot[win, :].astype(F32)
+        val = up + norm_back(grad, unit, rstd, vec[5:6, :])
+        dmid[win, :] = val
+        low = val.astype(BF)
+        da[c] = low
+        gather.start_part(c)
+        for row, term in ((4, low.astype(F32)), (5, grad * unit), (6, grad), (7, up)):
+            sums[row : row + 1, :] += jnp.sum(term, axis=0, keepdims=True)
+    merge(gather.steps(), ahead.forwards())
+    for c in range(gather.parts):
+        win = ahead.win(c)
+        layer[win, :] = (mid[win, :] + ahead.total(c) + vec[7:8, :]).astype(BF)
+    gather.finish()
+    back.finish()
+    ahead.finish()
+
+
+def turn(n, cid, du, w_fc, hidden, w_out, mid, cot, vec):
+    rows, width = mid.shape
+    parts = 4 if n == 8 else 1
+    piece = (parts, rows // parts, width)
+    return call(
+        functools.partial(turn_kernel, n),
+        cid,
+        "turn",
+        (du, w_fc, hidden, w_out, mid, cot, vec),
+        [VMEM] * 7,
+        [((n,) + piece, BF), ((rows, width), F32), ((rows, width), BF), ((8, width), F32)],
+        [ANY, VMEM, VMEM, VMEM],
+        [pltpu.VMEM(piece, BF)]
+        + Scatter.scratch(n, rows, width)
+        + Scatter.scratch(n, rows, width)
+        + Gather.sems(n, parts),
+    )
+
+
+def tail_kernel(
+    n, nz, fc, out, part, dqkv, w_qkv, tok, dmid, vec, v_in, fc_all, out_all, attn_all, g_tok, v_out,
+    v_own, attn, *scratch,
+):
     z = lax.axis_index("fsdp")
+    me, core, chip, sib, others = places(n)
     greet([sib] + [2 * p + core for p in others], others_of(z, nz))
-    vectors = Vectors(n, nz, vec, vec_out, scratch[:9])
-    vectors.start()
-    gather = Gather(n, src, out, scratch[9:])
-    gather.start()
-    merge(gather.steps(), vectors.steps())
-    gather.finish()
-    vectors.finish()
-
-
-def last_gather(n, nz, cid, array, vectors):
-    shape = jax.ShapeDtypeStruct
+    line = Line(nz, z, part, attn, scratch[:7])
+    line.start()
+    scatter = Scatter(n, NT, dqkv, w_qkv, scratch[7:15])
+    vectors = Vectors(n, nz, v_own, v_out, scratch[15:24])
+    fc_g = Gather(n, fc, fc_all, scratch[24:29])
+    out_g = Gather(n, out, out_all, scratch[29:34])
+    attn_g = Gather(n, attn, attn_all, scratch[34:39])
+    v_own[...] = v_in[...]
+    scatter.products()
+    todo = scatter.forwards()
+    for step in todo[: scatter.parts]:
+        step()
+    fc_g.start()
+
+    def rest(c):
+        win = scatter.win(c)
+        grad = scatter.total(c)
+        unit, rstd = norm(tok[win, :].astype(F32))
+        g_tok[win, :] = (dmid[win, :] + norm_back(grad, unit, rstd, vec[0:1, :])).astype(BF)
+        v_own[0:1, :] += jnp.sum(grad * unit, axis=0, keepdims=True)
+        v_own[1:2, :] += jnp.sum(grad, axis=0, keepdims=True)
+
+    first = todo[scatter.parts :] + [functools.partial(rest, c) for c in range(scatter.parts)]
+    first += [vectors.start, vectors.first, vectors.second]
+    fc_steps = fc_g.steps()
+    half = len(fc_steps) // 2
+    second = fc_steps[:half] + [out_g.start] + fc_steps[half:] + out_g.steps()
+    third = line.steps(attn_g.start_part)
+    merge(first, second, third, scales=(0.6, 1.0, 0.9))
+    for step in attn_g.steps() + [vectors.third]:
+        step()
+    for job in (fc_g, out_g, attn_g, scatter, line, vectors):
+        job.finish()
+
+
+def tail(n, nz, cid, fc, out, part, dqkv, w_qkv, tok, dmid, vec, v_in):
+    rows, width = tok.shape
+    attn = part.shape[1:]
+    return call(
+        functools.partial(tail_kernel, n, nz),
+        cid,
+        "tail",
+        (fc, out, part, dqkv, w_qkv, tok, dmid, vec, v_in),
+        [VMEM, VMEM, ANY] + [VMEM] * 6,
+        [((n,) + fc.shape, BF), ((n,) + out.shape, BF), ((n,) + attn, BF), (tok.shape, BF), (v_in.shape, F32)],
+        [ANY, ANY, ANY, VMEM, VMEM],
+        [pltpu.VMEM(v_in.shape, F32), pltpu.VMEM(attn, BF)]
+        + Line.scratch(part.shape)
+        + Scatter.scratch(n, rows, width)
+        + Vectors.scratch(n, nz, v_in.shape)
+        + Gather.sems(n, fc.shape[0])
+        + Gather.sems(n, out.shape[0])
+        + Gather.sems(n, attn[0]),
+    )
+
+
+def outer_kernel(x_ref, y_ref, out_ref):
+    out_ref[...] = dot(x_ref[...], y_ref[...], TN).astype(BF)
+
+
+def outer(x, y):
+    rows, m = x.shape
+    tile = 256
     return pl.pallas_call(
-        functools.partial(last_kernel, n, nz),
-        out_shape=[shape((n,) + array.shape, BF), shape(vectors.shape, F32)],
-        in_specs=[VMEM, VMEM],
-        out_specs=[ANY, VMEM],
-        scratch_shapes=Vectors.scratch(n, nz, vectors.shape) + Gather.sems(n, array.shape[0]),
-        compiler_params=pltpu.CompilerParams(collective_id=cid, has_side_effects=True),
-        name="last_gather",
-    )(array, vectors)
+        outer_kernel,
+        grid=(pl.cdiv(m, tile),),
+        out_shape=jax.ShapeDtypeStruct((m, y.shape[1]), BF),
+        in_specs=[pl.BlockSpec((rows, tile), lambda i: (0, i)), fixed(*y.shape)],
+        out_specs=tiled(tile, y.shape[1]),
+        name="outer",
+    )(x, y)
+
+
+def attn_outer_kernel(x_ref, y_ref, o_ref, a_ref, out_ref):
+    cols, pw = y_ref.shape[1], a_ref.shape[1]
+    out_ref[:, :cols] = dot(x_ref[...], y_ref[...], TN).astype(BF)
+    out_ref[:, cols : cols + pw] = dot(o_ref[0], a_ref[...], TN).astype(BF)
+    out_ref[:, cols + pw :] = jnp.zeros((out_ref.shape[0], out_ref.shape[1] - cols - pw), BF)
+
+
+def attn_outer(h1, dqkv, o_all, da_cols):
+    rows, m = h1.shape
+    tile = o_all.shape[2]
+    cols, pw = dqkv.shape[1], da_cols.shape[1]
+    total = -(-(cols + pw) // 128) * 128
+    return pl.pallas_call(
+        attn_outer_kernel,
+        grid=(pl.cdiv(m, tile),),
+        out_shape=jax.ShapeDtypeStruct((m, total), BF),
+        in_specs=[
+            pl.BlockSpec((rows, tile), lambda i: (0, i)),
+            fixed(rows, cols),
+            pl.BlockSpec((1, rows, tile), lambda i: (i, 0, 0)),
+            fixed(rows, pw),
+        ],
+        out_specs=tiled(tile, total),
+        name="attn_outer",
+    )(h1, dqkv, o_all, da_cols)
 
 
 def hidden_kernel(h_ref, w_ref, b_ref, z_ref, s_ref):
@@ -959,7 +1081,7 @@
 
 
 def attend_back_kernel(
-    blocks, blk, tile, pairs, inv_ref, q_ref, k_ref, v_ref, g_ref, o_ref, p_ref, out_ref,
+    blocks, blk, tile, pairs, inv_ref, q_ref, k_ref, v_ref, g_ref, o_ref, p_ref, out_ref, sum_ref,
     qn, kn, vn, gn, on, dqt, dk, dv,
 ):
     length = blocks * blk
@@ -994,6 +1116,9 @@
             dv[pl.ds(0, keys), :] += dot(p, g)
     dq = dqt[...].T
     pair = pl.program_id(0)
+    for t, val in enumerate((dq, dk[...], dv[...])):
+        at = pl.ds(pl.multiple_of((t * pairs + pair) * 128, 128), 128)
+        sum_ref[:, at] = jnp.sum(val.astype(BF).astype(F32), axis=0, keepdims=True)
     for i in range(blocks):
         dst = pl.ds(pl.multiple_of(inv_ref[i] * blk, blk), blk)
         src = slice(i * blk, (i + 1) * blk)
@@ -1011,7 +1136,10 @@
     piece = lambda off: pl.BlockSpec((length, 128), lambda i, s: (0, off * pairs + i))
     return pl.pallas_call(
         functools.partial(attend_back_kernel, blocks, blk, tile, pairs),
-        out_shape=jax.ShapeDtypeStruct((length, 3 * cols), BF),
+        out_shape=[
+            jax.ShapeDtypeStruct((length, 3 * cols), BF),
+            jax.ShapeDtypeStruct((1, 3 * cols), F32),
+        ],
         grid_spec=pltpu.PrefetchScalarGridSpec(
             num_scalar_prefetch=1,
             grid=(pairs,),
@@ -1023,7 +1151,10 @@
                 piece(0),
                 pl.BlockSpec((2, length, length), lambda i, s: (i, 0, 0)),
             ],
-            out_specs=pl.BlockSpec((length, 3 * cols), lambda i, s: (0, 0)),
+            out_specs=[
+                pl.BlockSpec((length, 3 * cols), lambda i, s: (0, 0)),
+                pl.BlockSpec((1, 3 * cols), lambda i, s: (0, 0)),
+            ],
             scratch_shapes=[pltpu.VMEM((length, 128), BF)] * 5
             + [
                 pltpu.VMEM((128, length), F32),
@@ -1078,94 +1209,80 @@
         wq_own = jnp.concatenate(
             [take(padded, t * width + ctx * hw, hw, 1) for t in range(3)], axis=1
         ).reshape(parts, wz // parts, 3 * hw)
+        row = lax.broadcasted_iota(jnp.int32, (16, wz), 0)
+        small = jnp.zeros((16, wz), BF)
+        for i, v in enumerate(
+            [ln1_gain, ln1_bias, query_bias, value_bias, proj_bias, ln2_gain, ln2_bias, out_bias]
+            + [jnp.pad(take(fc_bias, ctx * uw, uw), (0, wz - uw))]
+        ):
+            small = jnp.where(row == i, v[None, :], small)
+        tile = math.gcd(wz, hw)
+        h1, cot, small, w_qkv, w_proj, tok_own, cot_own = entry(
+            n, nz, tokens, cotangent, small, wq_own, proj_weight.reshape(wz // tile, tile, width), hw
+        )
+        small, fc_weight, out_weight = lax.optimization_barrier((small, fc_weight, out_weight))
         wfc_own = jnp.concatenate(
             [take(fc_weight, t * unit_z + ctx * uw, uw, 1) for t in range(nz)], axis=1
         )
-        wout_own = take(out_weight, ctx * uw, uw)
-        small = jnp.stack(
-            [ln1_gain, ln1_bias, query_bias, value_bias, proj_bias, ln2_gain, ln2_bias, out_bias]
-            + [jnp.pad(take(fc_bias, ctx * uw, uw), (0, wz - uw))]
-            + [jnp.zeros_like(ln1_gain)] * 7
-        )
-        h1, cot, small, w_qkv, w_proj = entry(
-            n, nz, tokens, cotangent, small, wq_own, proj_weight.reshape(wz // 8, 8, width), hw
-        )
-        small, wfc_own, wout_own = lax.optimization_barrier((small, wfc_own, wout_own))
         w_fc = lax.all_gather(wfc_own, "fsdp", axis=0, tiled=True)
-        w_out = lax.all_gather(wout_own, "fsdp", axis=0, tiled=True)
+        w_out = lax.all_gather(take(out_weight, ctx * uw, uw), "fsdp", axis=0, tiled=True)
         length = n * rows
-        h1, cot = h1.reshape(length, width), cot.reshape(length, width)
+        flat = lambda a: a.reshape(length, a.shape[-1])
+        h1, cot = flat(h1), flat(cot)
         w_qkv, w_proj = w_qkv.reshape(width, 3 * hw), w_proj.reshape(hw, width)
-        g1, b1, qb, vb, pb, g2, b2, ob = [small[i] for i in range(8)]
-        fb = small[8].reshape(nz, wz)[:, :uw].reshape(-1)
+        fb = small[8].reshape(nz, wz)[:, :uw].reshape(1, units)
         pad_cols = lambda v: take(jnp.pad(v, (0, n * hw - width)), ctx * hw, hw)
-        qkv_bias = jnp.concatenate([pad_cols(qb), jnp.zeros((hw,), F32), pad_cols(vb)])
-
-        cut = 2 if n == 8 else 1
-        pieces = lambda a: a.reshape(cut, a.shape[0] // cut, a.shape[1])
-        x = tokens.astype(F32)
-        unit1, rstd1 = norm(x)
+        qkv_bias = jnp.concatenate([pad_cols(small[2]), jnp.zeros((hw,), F32), pad_cols(small[3])])
+
         qkv = (dot(h1, w_qkv) + qkv_bias).astype(BF)
         o, p = attend(qkv, inv, blk)
-        mid = x + plane_scatter(n, 5, (o, w_proj, NN))[0] + pb
-        unit2, rstd2 = norm(mid)
-        h2, o_all = plane_gather(n, 2, pieces((unit2 * g2 + b2).astype(BF)), pieces(o))
-        h2 = h2.reshape(length, width)
-        hidden, slope = hidden_units(h2, w_fc, fb.reshape(1, units))
+        mid, h2 = middle(n, 2, o, w_proj, tok_own, small)
+        h2 = flat(h2)
+        hidden, slope = hidden_units(h2, w_fc, fb)
         part_out = dot(hidden, cot, TN).astype(BF)
+        in_parts = lambda a: a.reshape(nz, parts, a.shape[0] // nz // parts, a.shape[1])
+        o, part_out = lax.optimization_barrier((o, part_out))
+        o_all = spread(n, 3, o.reshape(4, length // 4, hw))
+        w_out, o_all = lax.optimization_barrier((w_out, o_all))
+        to_owner = lambda a: lax.psum_scatter(a, "fsdp", scatter_dimension=0, tiled=True)
+        sum_out = to_owner(part_out)
         du, dfb = hidden_back(cot, w_out, slope)
-        part_fc = dot(h2, du, TN).astype(BF)
-        du, hidden, part_out, part_fc = lax.optimization_barrier((du, hidden, part_out, part_fc))
-        to_owner = lambda a: lax.psum_scatter(a, "fsdp", scatter_dimension=0, tiled=True)
-        sum_out, sum_fc = to_owner(part_out), to_owner(part_fc)
-        dh2, summed = plane_scatter(n, 6, (du, w_fc, NT), (hidden, w_out, NN))
-        layer_out = (mid + summed + ob).astype(BF)
-        dmid = cotangent.astype(F32) + norm_back(dh2, unit2, rstd2, g2)
-        da_own = dmid.astype(BF)
-        (da,) = plane_gather(n, 3, pieces(da_own))
-        da = da.reshape(length, width)
+        part_fc = outer(h2, du)
+        du, part_fc = lax.optimization_barrier((du, part_fc))
+        sum_fc = to_owner(part_fc)
+        da, dmid, layer_out, sums = turn(n, 4, du, w_fc, hidden, w_out, mid, cot_own, small)
+        da = flat(da)
         do = dot(da, w_proj, NT).astype(BF)
-        dqkv = attend_back(qkv, do, o, p, inv, blk)
-        part_qkv = dot(h1, dqkv, TN).astype(BF)
+        dqkv, bias_cols = attend_back(qkv, do, o, p, inv, blk)
         pw = width // n
-        part_proj = jnp.einsum(
-            "ntk,td->nkd",
-            o_all.reshape(n, length, hw),
-            take(da, ctx * pw, pw, 1),
-            preferred_element_type=F32,
+        part_attn = attn_outer(h1, dqkv, o_all.reshape(n, length, hw), take(da, ctx * pw, pw, 1))
+
+        put = lambda v, size: lax.dynamic_update_slice_in_dim(
+            jnp.zeros((1, size), F32), v, ctx * v.shape[1], 1
         )
-        part_proj = part_proj.reshape(n * hw, pw)[:width].astype(BF)
-        spare = -(3 * hw + pw) % 128
-        part_attn = jnp.concatenate(
-            [part_qkv, part_proj, jnp.zeros((width, spare), BF)], axis=1
-        ).reshape(nz, parts, wz // parts, 3 * hw + pw + spare)
-        tail_parts = lambda a: a.reshape(parts, a.shape[0] // parts, a.shape[1])
-        all_fc, all_out, sum_attn, dh1 = reduce_all(
-            n, nz, 9, [tail_parts(sum_fc), tail_parts(sum_out)], part_attn, dqkv, w_qkv, NT
+        biases = jnp.concatenate(
+            [put(bias_cols[:, :hw], n * hw), put(bias_cols[:, 2 * hw :], n * hw)]
+        )[:, :width]
+        wide_fb = lax.dynamic_update_slice_in_dim(
+            jnp.zeros((nz, unit_z), F32), dfb.reshape(nz, uw), ctx * uw, 1
         )
-        grad_tokens = (dmid + norm_back(dh1, unit1, rstd1, g1)).astype(BF)
-
-        col_sum = lambda a: jnp.sum(a.astype(F32), axis=0)
-        put = lambda v, size: lax.dynamic_update_slice_in_dim(
-            jnp.zeros((size,), F32), v, ctx * v.shape[0], 0
+        vectors = jnp.concatenate(
+            [sums + jnp.pad(biases, ((2, 4), (0, 0))), jnp.pad(wide_fb, ((0, -nz % 8), (0, width - unit_z)))]
         )
-        bias_cols = col_sum(dqkv)
-        dfb = dfb.reshape(nz, uw)
-        rows_of = [
-            col_sum(dh1 * unit1),
-            col_sum(dh1),
-            put(bias_cols[:hw], n * hw)[:width],
-            put(bias_cols[2 * hw :], n * hw)[:width],
-            col_sum(da_own),
-            col_sum(dh2 * unit2),
-            col_sum(dh2),
-            col_sum(cotangent),
-        ]
-        wide_fb = lax.dynamic_update_slice_in_dim(jnp.zeros((nz, unit_z), F32), dfb, ctx * uw, 1)
-        wide_fb = jnp.pad(wide_fb, ((0, 8 - nz % 8 if nz % 8 else 0), (0, width - unit_z)))
-        vectors = jnp.concatenate([jnp.stack(rows_of), wide_fb])
-
-        all_attn, vectors = last_gather(n, nz, 4, sum_attn, vectors)
+        all_fc, all_out, all_attn, grad_tokens, vectors = tail(
+            n,
+            nz,
+            5,
+            sum_fc.reshape(parts, wz // parts, units),
+            sum_out.reshape(parts, uw // parts, width),
+            in_parts(part_attn),
+            dqkv,
+            w_qkv,
+            tok_own,
+            dmid,
+            small,
+            vectors,
+        )
         whole_rows = lambda a: a.reshape(n, a.shape[1] * a.shape[2], a.shape[3])
         grad_fc, grad_qkv, grad_proj, grad_out = join(
             n, nz, hw, whole_rows(all_fc), whole_rows(all_attn), all_out.reshape(unit_z, width)

time: 535 us -> 469 us (0.88)
  local copies, waits for them, and re-layouts: 38.1 us -> 17.3 us
  Pallas kernels: 413 us -> 396 us
  matrix products: 32.7 us -> 16 us
  other arithmetic: 17.3 us -> 4.19 us
  waiting for transfers between devices: 13 us -> 19.5 us
    dot_general x5 -> x3, matrix products: 28.6 us -> 16 us  [dot(): return lax.dot_general(a, b, dims, preferred_element_type=F32)]
    pallas_call x6, Pallas kernels: 270 us -> 257 us  [the longest x4 238 us: call(): pl.pallas_call(kernel, out_shape=[jax.ShapeDtypeStruct(*o) for o in outs]...]
    reduce_sum x7 -> x0, other arithmetic: 9.45 us -> none  [the longest x4 7.58 us: body(): col_sum = lambda a: jnp.sum(a.astype(F32), axis=0)]
    unnamed x20 -> x33, local copies, waits for them, and re-layouts: 11.6 us -> 4.04 us
    another operation x25 -> x3, local copies, waits for them, and re-layouts: 7.54 us -> 0.09 us  [the longest x1 0.08 us: body(): fb = small[8].reshape(nz, wz)[:, :uw].reshape(1, units)]
    reduce_scatter x1, waiting for transfers between devices: 3.41 us -> 9.67 us  [body(): lax.psum_scatter(a, 'fsdp', scatter_dimension=0, tiled=True)]
    reshape x2, local copies, waits for them, and re-layouts: 6.53 us -> 0.75 us  [the longest x1 0.67 us: body(): fb = small[8].reshape(nz, wz)[:, :uw].reshape(1, units)]
  transfers between devices with their start and end apart: 4 -> 4, of which waited for: 2 -> 2; matrix products, arithmetic and copies ran while one was open for 10% -> 6% of each run, Pallas kernels for 31% -> 40%
where the time goes in v3:
time: 469 us; the launch traced here: 467 us
  Pallas kernels  396 us (84%)
  waiting for transfers between devices  19.5 us (4%)
  local copies, waits for them, and re-layouts  17.3 us (4%)
  matrix products  16 us (3%)
  between operations  14.1 us (3%)
    pallas_call x4, Pallas kernels, call(): pl.pallas_call(kernel, out_shape=[jax.ShapeDtypeStruct(*o) for o in outs]...  238 us
    pallas_call x1, Pallas kernels, entry(): pl.pallas_call(functools.partial(entry_kernel, n, nz), out_shape=[shape((...  70.9 us
    pallas_call x1, Pallas kernels, join(): pl.pallas_call(functools.partial(join_kernel, n, nz, hw, width), grid=(ti...  25.1 us
    dot_general x3, matrix products, dot(): return lax.dot_general(a, b, dims, preferred_element_type=F32)  16 us
    pallas_call x1, Pallas kernels, attend_back(): pl.pallas_call(functools.partial(attend_back_kernel, blocks, blk, tile, p...  12.9 us
    pallas_call x1, Pallas kernels, attend(): pl.pallas_call(functools.partial(attend_kernel, blocks, blk, tile), out_s...  12.3 us
    pallas_call x1, Pallas kernels, attn_outer(): pl.pallas_call(attn_outer_kernel, grid=(pl.cdiv(m, tile),), out_shape=jax...  9.96 us
    all_gather x1, waiting for transfers between devices, body(): lax.all_gather(take(out_weight, ctx * uw, uw), 'fsdp', axis=0, tiled=True)  9.75 us
  transfers between devices with their start and end apart: 4, of which 2 were waited for; matrix products, arithmetic and copies ran while one was open for 6% of the time, Pallas kernels for 40%

profile of v3, /device:TPU:0, one launch (start us, length us, event | category | flops | bytes accessed | tf_op | source)
XLA Modules:
  0.0 467.4 jit_solution(3516253818146539051)
XLA Ops:
  7.3 0.0 all-gather.5.cloned.1.call-start
  7.4 0.8 dynamic_slice.42
  8.2 1.3 pad_dynamic-slice_fusion.2
  9.5 0.9 pad_maximum_fusion.1
  10.4 0.7 select_select_fusion.small
  11.1 70.9 %entry.1 = (bf16[8,2,64,1600]{3,2,1,0:T(8,128)(2,1)}, bf16[8,2,64,1600]{3,2,1,0:T(8,128)(2,1)}, f32[16,1600]{1,0:T(8,128)}, bf16[20,80,768]{2,1,0:T(8,128)(2,1)}...) custom-call(bf16[1600,128]{1,0:T(8,128)(2,1)} %bitcast.53, ...), custom_call_target="tpu_custom_call" | custom-call | tf_op jit(solution)/shard_map/entry/pallas_call | solution.py:327
  82.0 1.8 constant_dynamic-slice_fusion.5
  83.8 1.2 pad_maximum_fusion
  85.0 0.0 all-gather.5.cloned.1.call-update
  85.0 0.0 all-gather.3.cloned.1.call-start
  85.1 2.0 constant_dynamic-slice_fusion.6
  87.1 0.2 reduce-scatter.7.cloned.1.call-start
  87.4 0.1 copy.40
  87.4 0.1 eq.98
  87.5 0.9 slice_reduce_fusion
  88.5 0.1 reshape_squeeze.3
  88.6 0.7 reshape.99.b_ref
  89.2 0.1 pad_dynamic-slice_fusion.3
  89.3 0.1 pad_dynamic-slice_fusion.4
  89.4 0.6 iota_reduce_fusion
  90.0 5.8 %add_convert_fusion.q_ref.k_ref.v_ref = bf16[1024,768]{1,0:T(8,128)(2,1)} fusion(bf16[1024,1600]{1,0:T(8,128)(2,1)S(1)} %bitcast.44, bf16[1600,768]{1,0:T(8,128)(2,1)} %bitcast.45, f32[768]{0:T(1024)S(1)} %pad_maximum_fusion.2), kind=kOutput, calls=%fused_computation.4 | convolution fusion | flops 2518155264 | bytes 7310336 | tf_op jit(solution)/shard_map/dot_general | solution.py:23
  95.8 12.3 %attend.1 = (bf16[1024,256]{1,0:T(8,128)(2,1)}, bf16[4,1024,1024]{2,1,0:T(8,128)(2,1)}) custom-call(s32[16]{0:T(128)} %get-tuple-element.58.inv_ref, bf16[1024,768]{1,0:T(8,128)(2,1)} %add_convert_fusion.q_ref.k_ref.v_ref, bf16[1024,768]{1,0:T(8,128)(2,1)} %add_convert_fusion.q_ref.k_ref.v_ref, bf16[1024,768]{1,0:T(8,128)(2,1)} %add_convert_fusion.q_ref.k_ref.v_ref), custom_call_target="tpu_custom_call" | custom-call | tf_op jit(solution)/shard_map/attend/pallas_call | solution.py:1057
  108.2 44.8 %middle.1 = (f32[128,1600]{1,0:T(8,128)}, bf16[8,4,32,1600]{3,2,1,0:T(8,128)(2,1)}) custom-call(bf16[1024,256]{1,0:T(8,128)(2,1)} %get-tuple-element.68.o.o_ref, bf16[256,1600]{1,0:T(8,128)(2,1)} %bitcast.49, bf16[128,1600]{1,0:T(8,128)(2,1)} %get-tuple-element.64.tok, f32[16,1600]{1,0:T(8,128)} %get-tuple-element.61.vec), custom_call_target="tpu_custom_call" | custom-call | tf_op jit(solution)/shard_map/middle/pallas_call | solution.py:678
  153.0 0.0 all-gather.5.cloned.1.call-done.w_ref.w_fc
  153.0 9.3 %hidden.1 = (bf16[1024,800]{1,0:T(8,128)(2,1)}, bf16[1024,800]{1,0:T(8,128)(2,1)}) custom-call(bf16[1024,1600]{1,0:T(8,128)(2,1)} %bitcast.34, bf16[1600,800]{1,0:T(8,128)(2,1)} %all-gather.5.cloned.1.call-done.w_ref.w_fc, f32[1,800]{1,0:T(1,128)} %reshape.99.b_ref), custom_call_target="tpu_custom_call" | custom-call | tf_op jit(solution)/shard_map/hidden/pallas_call | solution.py:942
  162.3 6.2 %convolution_convert_fusion = bf16[800,1600]{1,0:T(8,128)(2,1)} fusion(bf16[1024,800]{1,0:T(8,128)(2,1)} %get-tuple-element.67.hid, bf16[1024,1600]{1,0:T(8,128)(2,1)S(1)} %bitcast.42), kind=kOutput, calls=%fused_computation.3 | convolution fusion | flops 2622720000 | bytes 7475200 | tf_op jit(solution)/shard_map/dot_general | solution.py:23
  168.6 0.0 reduce-scatter.5.cloned.1.call-start
  168.6 24.9 %spread.1 = bf16[8,4,256,256]{3,2,1,0:T(8,128)(2,1)} custom-call(bf16[4,256,256]{2,1,0:T(8,128)(2,1)} %bitcast.40), custom_call_target="tpu_custom_call" | custom-call | tf_op jit(solution)/shard_map/spread/pallas_call | solution.py:678
  193.5 9.7 %all-gather.3.cloned.1.call-done.w_ref.w_out = bf16[800,1600]{1,0:T(8,128)(2,1)} async-done(((bf16[200,1600]{1,0:T(8,128)(2,1)}), bf16[800,1600]{1,0:T(8,128)(2,1)}) %all-gather.3.cloned.1.call-update) | async-done | bytes 2560016 | tf_op jit(solution)/shard_map/all_gather | solution.py:1228
  203.3 7.9 %hidden_back.1 = (bf16[1024,800]{1,0:T(8,128)(2,1)}, f32[1,800]{1,0:T(1,128)}) custom-call(bf16[1024,1600]{1,0:T(8,128)(2,1)} %bitcast.41, bf16[800,1600]{1,0:T(8,128)(2,1)} %all-gather.3.cloned.1.call-done.w_ref.w_out, bf16[1024,800]{1,0:T(8,128)(2,1)} %get-tuple-element.70.s_ref), custom_call_target="tpu_custom_call" | custom-call | tf_op jit(solution)/shard_map/hidden_back/pallas_call | solution.py:956
  211.2 9.1 %outer.1 = bf16[1600,800]{1,0:T(8,128)(2,1)} custom-call(bf16[1024,1600]{1,0:T(8,128)(2,1)} %bitcast.35, bf16[1024,800]{1,0:T(8,128)(2,1)} %get-tuple-element.72.y_ref.du), custom_call_target="tpu_custom_call" | custom-call | tf_op jit(solution)/shard_map/outer/pallas_call | solution.py:871
  220.4 54.5 %turn.1 = (bf16[8,4,32,1600]{3,2,1,0:T(8,128)(2,1)}, f32[128,1600]{1,0:T(8,128)}, bf16[128,1600]{1,0:T(8,128)(2,1)}, f32[8,1600]{1,0:T(8,128)}) custom-call(bf16[1024,800]{1,0:T(8,128)(2,1)} %get-tuple-element.72.y_ref.du, bf16[1600,800]{1,0:T(8,128)(2,1)} %all-gather.5.cloned.1.call-done.w_ref.w_fc, bf16[1024,800]{1,0:T(8,128)(2,1)} %get-tuple-element.67.hid, ...), custom_call_target="tpu_custom_call" | custom-call | tf_op jit(solution)/shard_map/turn/pallas_call | solution.py:678
  274.9 1.9 copy.41
  276.8 0.1 reshape.106
  276.9 4.0 convolution_convert_fusion.1.g_ref
  280.9 12.9 %attend_back.1 = (bf16[1024,768]{1,0:T(8,128)(2,1)}, f32[1,768]{1,0:T(1,128)}) custom-call(s32[16]{0:T(128)} %get-tuple-element.58.inv_ref, bf16[1024,768]{1,0:T(8,128)(2,1)} %add_convert_fusion.q_ref.k_ref.v_ref, bf16[1024,768]{1,0:T(8,128)(2,1)} %add_convert_fusion.q_ref.k_ref.v_ref, bf16[1024,768]{1,0:T(8,128)(2,1)} %add_convert_fusion.q_ref.k_ref.v_ref, ...), custom_call_target="tpu_custom_call" | custom-call | tf_op jit(solution)/shard_map/attend_back/pallas_call | solution.py:1137
  293.8 0.2 dynamic_update_slice.11
  294.1 2.2 constant_dynamic-slice_fusion.1.a_ref
  296.3 10.0 %attn_outer.1 = bf16[1600,1024]{1,0:T(8,128)(2,1)} custom-call(bf16[1024,1600]{1,0:T(8,128)(2,1)} %bitcast.43, bf16[1024,768]{1,0:T(8,128)(2,1)} %get-tuple-element.80.y_ref.dqkv, bf16[8,1024,256]{2,1,0:T(8,128)(2,1)} %bitcast.33, bf16[1024,200]{1,0:T(8,128)(2,1)} %constant_dynamic-slice_fusion.1.a_ref), custom_call_target="tpu_custom_call" | custom-call | tf_op jit(solution)/shard_map/attn_outer/pallas_call | solution.py:893
  306.3 0.7 select_maximum_fusion.v_in
  307.0 9.7 %reduce-scatter.5.cloned.1.call-done = bf16[400,800]{1,0:T(8,128)(2,1)} async-done(((bf16[1600,800]{1,0:T(8,128)(2,1)}), bf16[400,800]{1,0:T(8,128)(2,1)}) %reduce-scatter.5.cloned.1.call-update) | async-done | bytes 640016 | tf_op jit(solution)/shard_map/reduce_scatter | solution.py:1247
  316.7 114.2 %tail.1 = (bf16[8,5,80,800]{3,2,1,0:T(8,128)(2,1)}, bf16[8,5,40,1600]{3,2,1,0:T(8,128)(2,1)}, bf16[8,5,80,1024]{3,2,1,0:T(8,128)(2,1)}, bf16[128,1600]{1,0:T(8,128)(2,1)}, f32[16,1600]{1,0:T(8,128)}) custom-call(bf16[5,80,800]{2,1,0:T(8,128)(2,1)} %bitcast.51, bf16[5,40,1600]{2,1,0:T(8,128)(2,1)} %bitcast.52, bf16[4,5,80,1024]{3,2,1,0:T(8,128)(2,1)} %bitcast.36, ...), custom_call_target="tpu_custom_call" | custom-call | tf_op jit(solution)/shard_map/tail/pallas_call | solution.py:678
  430.9 0.8 slice.66
  431.7 0.8 slice.58
  432.5 1.9 copy.42
  434.4 0.6 dynamic-slice_reduce_fusion
  435.1 25.1 %join.1 = (f32[400,6400]{1,0:T(8,128)}, f32[400,4800]{1,0:T(8,128)}, f32[400,1600]{1,0:T(8,128)}, f32[1600,1600]{1,0:T(8,128)}) custom-call(bf16[8,25,16,800]{3,2,1,0:T(8,128)(2,1)} %bitcast.38, bf16[8,25,16,1024]{3,2,1,0:T(8,128)(2,1)} %bitcast.37, bf16[1600,1600]{1,0:T(8,128)(2,1)} %bitcast.39), custom_call_target="tpu_custom_call" | custom-call | tf_op jit(solution)/shard_map/join/pallas_call | solution.py:995
  460.1 0.7 fusion.2
  (50 shorter events, 0.3 us)
Async XLA Ops:
  7.2 3.2 copy-start.14
  7.2 3.2 copy-start.13
  7.2 3.2 copy-start.12
  7.2 3.2 copy-start.11
  7.2 3.1 copy-start.10
  7.2 3.1 copy-start.9
  7.2 3.1 copy-start.8
  7.3 3.1 copy-start.7
  7.3 145.7 %all-gather.5.cloned.1.call-start = ((), (), s32[]{:S(2)}) async-start(), calls=%async_computation.3 | async-start | bytes 3584000 | tf_op jit(solution)/shard_map/all_gather | solution.py:1227
  82.0 5.4 %copy-start.6 = (s32[8,2]{0,1:T(2,128)S(1)}, s32[8,2]{0,1:T(2,128)}, u32[]{:S(2)}) copy-start(s32[8,2]{0,1:T(2,128)} %param.17) | copy-start | bytes 196
  82.0 8.0 %copy-start.1 = (bf16[8,2,64,1600]{3,2,1,0:T(8,128)(2,1)S(1)}, bf16[8,2,64,1600]{3,2,1,0:T(8,128)(2,1)}, u32[]{:S(2)}) copy-start(bf16[8,2,64,1600]{3,2,1,0:T(8,128)(2,1)} %get-tuple-element.59) | copy-start | bytes 9830404
  85.0 118.2 %all-gather.3.cloned.1.call-start = ((), (), s32[]{:S(2)}) async-start(), calls=%async_computation.2 | async-start | bytes 3328000 | tf_op jit(solution)/shard_map/all_gather | solution.py:1228
  87.1 219.9 %reduce-scatter.7.cloned.1.call-start = ((), (), s32[]{:S(2)}) async-start(), calls=%async_computation.5 | async-start | bytes 3328000
  153.0 9.4 %copy-start = (bf16[8,2,64,1600]{3,2,1,0:T(8,128)(2,1)S(1)}, bf16[8,2,64,1600]{3,2,1,0:T(8,128)(2,1)}, u32[]{:S(2)}) copy-start(bf16[8,2,64,1600]{3,2,1,0:T(8,128)(2,1)} %get-tuple-element.55) | copy-start | bytes 9830404
  168.6 148.1 %reduce-scatter.5.cloned.1.call-start = ((), (), s32[]{:S(2)}) async-start(), calls=%async_computation.4 | async-start | bytes 3584000 | tf_op jit(solution)/shard_map/reduce_scatter | solution.py:1247
  220.3 56.5 %copy-start.4 = (f32[1,800]{1,0:T(1,128)S(1)}, f32[1,800]{1,0:T(1,128)}, u32[]{:S(2)}) copy-start(f32[1,800]{1,0:T(1,128)} %get-tuple-element.85) | copy-start | bytes 9604
  220.3 56.6 %copy-start.2 = (bf16[16,16,1600]{2,1,0:T(8,128)(2,1)S(1)}, bf16[16,16,1600]{2,1,0:T(8,128)(2,1)}, u32[]{:S(2)}) copy-start(bf16[16,16,1600]{2,1,0:T(8,128)(2,1)} %get-tuple-element.63) | copy-start | bytes 2457604
  296.3 10.0 %copy-start.5 = (f32[1,768]{1,0:T(1,128)S(1)}, f32[1,768]{1,0:T(1,128)}, u32[]{:S(2)}) copy-start(f32[1,768]{1,0:T(1,128)} %get-tuple-element.84) | copy-start | bytes 9220
  296.3 10.0 %copy-start.3 = (f32[8,1600]{1,0:T(8,128)S(1)}, f32[8,1600]{1,0:T(8,128)}, u32[]{:S(2)}) copy-start(f32[8,1600]{1,0:T(8,128)} %get-tuple-element.83) | copy-start | bytes 153604
Sparse Core Ops, SparseCore 0:
  85.2 62.3 all-gather.4
  149.1 54.0 all-gather.2
  206.2 51.1 reduce-scatter.6
  260.1 56.4 reduce-scatter.4

commit v4 on v3

--- a/solution.py
+++ b/solution.py
@@ -77,6 +77,16 @@
         item[3]()
 
 
+def timed(*lists):
+    keyed = [(time, t, i, step) for t, steps in enumerate(lists) for i, (time, step) in enumerate(steps)]
+    for item in sorted(keyed, key=lambda k: k[:3]):
+        item[3]()
+
+
+def spaced(steps, start, stop):
+    return [(start + (stop - start) * (i + 0.5) / len(steps), step) for i, step in enumerate(steps)]
+
+
 class Gather:
     def __init__(self, n, src, out, sems):
         self.n, self.src, self.out = n, src, out
@@ -146,6 +156,14 @@
             todo.append(functools.partial(self.arrived, 2, self.parts - 1))
         return todo
 
+    def timed_steps(self, begin, wait, relay):
+        todo = []
+        for c in range(self.parts):
+            for d in range(len(self.others)):
+                late = relay if self.square and d == 2 else 0
+                todo.append((begin(c) + wait + late, functools.partial(self.arrived, d, c)))
+        return todo
+
     def finish(self):
         for c in range(self.parts):
             *far, own = self.own_sends(c)
@@ -249,11 +267,16 @@
 
 
 def entry_kernel(
-    n, nz, tok_t, cot_t, small, wq, wp, h1_all, cot_all, vec, wq_all, wp_all, tok, cot_own, *scratch
+    n, nz, tok_t, cot_t, small, wq, wp, fc_hbm, out_hbm, h1_all, cot_all, vec, wq_all, wp_all, tok, cot_own,
+    fc_own, out_own, *scratch
 ):
-    cot, h1, inbox, zeros, small_s, small_r, zero_s = scratch[:7]
-    g_h, g_c = scratch[7:12], scratch[12:17]
-    r_q, r_p = scratch[17:21], scratch[21:25]
+    cot, h1, inbox, zeros, fc_all, load_s, small_s, small_r, zero_s = scratch[:9]
+    g_h, g_c = scratch[9:14], scratch[14:19]
+    r_q, r_p = scratch[19:23], scratch[23:27]
+    loads = [
+        pltpu.make_async_copy(fc_hbm, fc_all, load_s.at[0]),
+        pltpu.make_async_copy(out_hbm.at[lax.axis_index("ctx")], out_own, load_s.at[1]),
+    ]
     me, core, chip, sib, others = places(n)
     z = lax.axis_index("fsdp")
     planes = others_of(z, nz)
@@ -298,8 +321,28 @@
         unit, _ = norm(tok[c * rows : (c + 1) * rows, :].astype(F32))
         h1[c] = (unit * gain + shift).astype(BF)
         gather_h.start_part(c)
+    for load in loads:
+        load.start()
+
+    def columns():
+        for load in loads:
+            load.wait()
+        uw = fc_own.shape[-1] // nz
+        for place in range(n):
+
+            @pl.when(me == place)
+            def _():
+                def tile(i, carry):
+                    for t in range(nz):
+                        at = (t * n + place) * uw
+                        fc_own[i, :, t * uw : (t + 1) * uw] = fc_all[i, :, at : at + uw]
+                    return carry
+
+                lax.fori_loop(0, fc_own.shape[0], tile, 0)
+
+    steps = gather_c.steps() + gather_h.steps()
     merge(
-        gather_c.steps() + gather_h.steps(),
+        steps[:4] + [columns] + steps[4:],
         relay_q.steps(nz * k - k) + relay_p.steps(blocks),
     )
     gather_c.finish()
@@ -316,7 +359,7 @@
         send(small, inbox.at[z], small_s.at[d], small_r.at[d], fsdp=plane).wait_send()
 
 
-def entry(n, nz, tokens, cot, small, wq, wp, hw):
+def entry(n, nz, tokens, cot, small, wq, wp, fc, out, hw):
     rows, width = tokens.shape
     parts = 2 if n == 8 else 1
     dma = pltpu.SemaphoreType.DMA
@@ -334,14 +377,18 @@
             shape((blocks, tile, width), BF),
             shape((rows, width), BF),
             shape((rows, width), BF),
+            shape(fc.shape[:2] + (fc.shape[2] // n,), BF),
+            shape(out.shape[1:], BF),
         ],
-        in_specs=[VMEM] * 5,
-        out_specs=[ANY, ANY, VMEM, ANY, ANY, VMEM, VMEM],
+        in_specs=[VMEM] * 5 + [ANY, ANY],
+        out_specs=[ANY, ANY, VMEM, ANY, ANY] + [VMEM] * 4,
         scratch_shapes=[
             pltpu.VMEM(piece, BF),
             pltpu.VMEM(piece, BF),
             pltpu.VMEM((nz,) + small.shape, BF),
             pltpu.VMEM((tile, width), BF),
+            pltpu.VMEM(fc.shape, BF),
+            dma((2,)),
             dma((nz - 1,)),
             dma((nz - 1,)),
             dma((blocks,)),
@@ -350,9 +397,11 @@
         + Gather.sems(n, parts)
         + Relay.sems(nz * k)
         + Relay.sems(blocks),
-        compiler_params=pltpu.CompilerParams(collective_id=1, has_side_effects=True),
+        compiler_params=pltpu.CompilerParams(
+            collective_id=1, has_side_effects=True, vmem_limit_bytes=60 * 1024 * 1024
+        ),
         name="entry",
-    )(tokens.T, cot.T, small, wq, wp)
+    )(tokens.T, cot.T, small, wq, wp, fc, out)
 
 
 class Scatter:
@@ -508,17 +557,19 @@
         )
 
     def start(self):
-        for d in range(self.nz - 1, 0, -1):
-
-            @pl.when(self.z == 0)
-            def _():
-                for c in range(self.parts):
-                    self.up(self.src, d, c).start()
-
-            @pl.when(self.z == self.nz - 1)
-            def _():
-                for c in range(self.parts):
-                    self.down(self.src, self.nz - 1 - d, c).start()
+        top = self.nz - 1
+
+        @pl.when(self.z == 0)
+        def _():
+            for c in range(self.parts):
+                for k in range(top):
+                    self.up(self.src, top - k, c).start()
+
+        @pl.when(self.z == top)
+        def _():
+            for c in range(self.parts):
+                for k in range(top):
+                    self.down(self.src, k, c).start()
 
         self.load = pltpu.make_async_copy(self.src, self.mine, self.load_s.at[0])
         self.load.start()
@@ -549,27 +600,23 @@
             total = total + self.below[z, c].astype(F32)
         self.out[c] = total.astype(BF)
 
-    def steps(self, after=None):
-        top, parts = self.nz - 1, self.parts
+    def timed_steps(self, after):
+        top = self.nz - 1
         slots = {}
 
         def put(time, place, fn):
             slots.setdefault(time, {}).setdefault(place, []).append(fn)
 
-        for place in range(self.nz):
-            for k in range(1, self.nz):
-                for c in range(parts):
-                    at = (k - 1) * parts + c
-                    if 0 < place < top - k + 1:
-                        put(at + place, place, functools.partial(self.pass_up, top - k + 1, c))
-                    if k - 1 < place < top:
-                        put(at + top - place, place, functools.partial(self.pass_down, k - 1, c))
-            for c in range(parts):
-                up = (top - place) * parts + c + place if place > 0 else 0
-                down = place * parts + c + top - place if place < top else 0
-                put(max(up, down), place, functools.partial(self.settle, place, c))
-                if after:
-                    put(max(up, down), place, functools.partial(after, c))
+        for c in range(self.parts):
+            for place in range(self.nz):
+                for k in range(top):
+                    at = c * top + k
+                    if 0 < place < top - k:
+                        put(at + place, place, functools.partial(self.pass_up, top - k, c))
+                    if k < place < top:
+                        put(at + top - place, place, functools.partial(self.pass_down, k, c))
+                put((c + 1) * top, place, functools.partial(self.settle, place, c))
+                put((c + 1) * top, place, functools.partial(after, c))
 
         def run(work):
             for place, fns in sorted(work.items()):
@@ -579,7 +626,7 @@
                     for fn in fns:
                         fn()
 
-        return [self.loaded] + [functools.partial(run, slots[t]) for t in sorted(slots)]
+        return [(0, self.loaded)] + [(t, functools.partial(run, slots[t])) for t in sorted(slots)]
 
     def finish(self):
         for d in range(self.nz):
@@ -598,8 +645,8 @@
 class Vectors:
     def __init__(self, n, nz, src, out, scratch):
         self.n, self.nz, self.src, self.out = n, nz, src, out
-        self.from_sib, self.chips, self.line = scratch[:3]
-        self.ss, self.sr, self.cs, self.cr, self.ls, self.lr = scratch[3:]
+        self.low, self.from_sib, self.chips, self.line = scratch[:4]
+        self.ss, self.sr, self.cs, self.cr, self.ls, self.lr = scratch[4:]
         self.me, self.core, self.chip, self.sib, self.others = places(n)
         self.z = lax.axis_index("fsdp")
         self.planes = others_of(self.z, nz)
@@ -609,9 +656,10 @@
         dma = pltpu.SemaphoreType.DMA
         half = n // 2
         return [
-            pltpu.VMEM(shape, F32),
-            pltpu.VMEM((half,) + shape, F32),
-            pltpu.VMEM((nz,) + shape, F32),
+            pltpu.VMEM(shape, BF),
+            pltpu.VMEM(shape, BF),
+            pltpu.VMEM((half,) + shape, BF),
+            pltpu.VMEM((nz,) + shape, BF),
             dma((1,)),
             dma((1,)),
             dma((half - 1,)),
@@ -621,7 +669,7 @@
         ]
 
     def to_sib(self):
-        return send(self.src, self.from_sib, self.ss.at[0], self.sr.at[0], ctx=self.sib)
+        return send(self.low, self.from_sib, self.ss.at[0], self.sr.at[0], ctx=self.sib)
 
     def to_chip(self, d):
         at = self.chips.at[self.chip]
@@ -632,30 +680,31 @@
         return send(at, at, self.ls.at[d], self.lr.at[d], fsdp=self.planes[d])
 
     def start(self):
+        self.low[...] = self.src[...].astype(BF)
         self.to_sib().start()
 
     def first(self):
         self.to_sib().wait_recv()
-        self.chips[self.chip] = self.src[...] + self.from_sib[...]
+        self.chips[self.chip] = self.low[...] + self.from_sib[...]
         for d in range(self.n // 2 - 1):
             self.to_chip(d).start()
 
     def second(self):
         for d in range(self.n // 2 - 1):
             self.to_chip(d).wait_recv()
-        total = self.chips[0]
+        total = self.chips[0].astype(F32)
         for k in range(1, self.n // 2):
-            total = total + self.chips[k]
-        self.line[self.z] = total
+            total = total + self.chips[k].astype(F32)
+        self.line[self.z] = total.astype(BF)
         for d in range(self.nz - 1):
             self.to_plane(d).start()
 
     def third(self):
         for d in range(self.nz - 1):
             self.to_plane(d).wait_recv()
-        total = self.line[0]
+        total = self.line[0].astype(F32)
         for k in range(1, self.nz):
-            total = total + self.line[k]
+            total = total + self.line[k].astype(F32)
         self.out[...] = total
 
     def steps(self):
@@ -799,25 +848,33 @@
 
 
 def tail_kernel(
-    n, nz, fc, out, part, dqkv, w_qkv, tok, dmid, vec, v_in, fc_all, out_all, attn_all, g_tok, v_out,
-    v_own, attn, *scratch,
+    n, nz, fc, part, dqkv, w_qkv, tok, dmid, vec, v_in, fc_all, attn_all, g_tok, v_out,
+    v_own, attn, fc_v, dqkv_v, w_v, load_s, *scratch,
 ):
     z = lax.axis_index("fsdp")
     me, core, chip, sib, others = places(n)
     greet([sib] + [2 * p + core for p in others], others_of(z, nz))
     line = Line(nz, z, part, attn, scratch[:7])
     line.start()
+    loads = [
+        pltpu.make_async_copy(src, dst, load_s.at[i])
+        for i, (src, dst) in enumerate([(dqkv, dqkv_v), (w_qkv, w_v), (fc, fc_v)])
+    ]
+    for load in loads:
+        load.start()
+    fc, dqkv, w_qkv = fc_v, dqkv_v, w_v
     scatter = Scatter(n, NT, dqkv, w_qkv, scratch[7:15])
-    vectors = Vectors(n, nz, v_own, v_out, scratch[15:24])
-    fc_g = Gather(n, fc, fc_all, scratch[24:29])
-    out_g = Gather(n, out, out_all, scratch[29:34])
-    attn_g = Gather(n, attn, attn_all, scratch[34:39])
+    vectors = Vectors(n, nz, v_own, v_out, scratch[15:25])
+    fc_g = Gather(n, fc, fc_all, scratch[25:30])
+    attn_g = Gather(n, attn, attn_all, scratch[30:35])
     v_own[...] = v_in[...]
+    for load in loads[:2]:
+        load.wait()
     scatter.products()
     todo = scatter.forwards()
     for step in todo[: scatter.parts]:
         step()
-    fc_g.start()
+    loads[2].wait()
 
     def rest(c):
         win = scatter.win(c)
@@ -827,36 +884,41 @@
         v_own[0:1, :] += jnp.sum(grad * unit, axis=0, keepdims=True)
         v_own[1:2, :] += jnp.sum(grad, axis=0, keepdims=True)
 
-    first = todo[scatter.parts :] + [functools.partial(rest, c) for c in range(scatter.parts)]
-    first += [vectors.start, vectors.first, vectors.second]
-    fc_steps = fc_g.steps()
-    half = len(fc_steps) // 2
-    second = fc_steps[:half] + [out_g.start] + fc_steps[half:] + out_g.steps()
-    third = line.steps(attn_g.start_part)
-    merge(first, second, third, scales=(0.6, 1.0, 0.9))
-    for step in attn_g.steps() + [vectors.third]:
-        step()
-    for job in (fc_g, out_g, attn_g, scatter, line, vectors):
+    top = nz - 1
+    last = attn_g.parts * top
+    part_at = functools.partial
+    fc_at = lambda c: 4.0 + 2.0 * c
+    timed(
+        spaced(todo[scatter.parts :], 1.0, 4.0),
+        spaced([part_at(rest, c) for c in range(scatter.parts)], 4.5, 7.0),
+        [(7.1, vectors.start), (7.8, vectors.first), (11.0, vectors.second), (last + 3.0, vectors.third)],
+        [(fc_at(c), part_at(fc_g.start_part, c)) for c in range(fc_g.parts)],
+        fc_g.timed_steps(fc_at, 2.2, 1.6),
+        line.timed_steps(attn_g.start_part),
+        attn_g.timed_steps(lambda c: (c + 1) * top, 2.2, 1.6),
+    )
+    for job in (fc_g, attn_g, scatter, line, vectors):
         job.finish()
 
 
-def tail(n, nz, cid, fc, out, part, dqkv, w_qkv, tok, dmid, vec, v_in):
+def tail(n, nz, cid, fc, part, dqkv, w_qkv, tok, dmid, vec, v_in):
     rows, width = tok.shape
     attn = part.shape[1:]
     return call(
         functools.partial(tail_kernel, n, nz),
         cid,
         "tail",
-        (fc, out, part, dqkv, w_qkv, tok, dmid, vec, v_in),
-        [VMEM, VMEM, ANY] + [VMEM] * 6,
-        [((n,) + fc.shape, BF), ((n,) + out.shape, BF), ((n,) + attn, BF), (tok.shape, BF), (v_in.shape, F32)],
-        [ANY, ANY, ANY, VMEM, VMEM],
+        (fc, part, dqkv, w_qkv, tok, dmid, vec, v_in),
+        [ANY] * 4 + [VMEM] * 4,
+        [((n,) + fc.shape, BF), ((n,) + attn, BF), (tok.shape, BF), (v_in.shape, F32)],
+        [ANY, ANY, VMEM, VMEM],
         [pltpu.VMEM(v_in.shape, F32), pltpu.VMEM(attn, BF)]
+        + [pltpu.VMEM(a.shape, BF) for a in (fc, dqkv, w_qkv)]
+        + [pltpu.SemaphoreType.DMA((3,))]
         + Line.scratch(part.shape)
         + Scatter.scratch(n, rows, width)
         + Vectors.scratch(n, nz, v_in.shape)
         + Gather.sems(n, fc.shape[0])
-        + Gather.sems(n, out.shape[0])
         + Gather.sems(n, attn[0]),
     )
 
@@ -876,33 +938,6 @@
         out_specs=tiled(tile, y.shape[1]),
         name="outer",
     )(x, y)
-
-
-def attn_outer_kernel(x_ref, y_ref, o_ref, a_ref, out_ref):
-    cols, pw = y_ref.shape[1], a_ref.shape[1]
-    out_ref[:, :cols] = dot(x_ref[...], y_ref[...], TN).astype(BF)
-    out_ref[:, cols : cols + pw] = dot(o_ref[0], a_ref[...], TN).astype(BF)
-    out_ref[:, cols + pw :] = jnp.zeros((out_ref.shape[0], out_ref.shape[1] - cols - pw), BF)
-
-
-def attn_outer(h1, dqkv, o_all, da_cols):
-    rows, m = h1.shape
-    tile = o_all.shape[2]
-    cols, pw = dqkv.shape[1], da_cols.shape[1]
-    total = -(-(cols + pw) // 128) * 128
-    return pl.pallas_call(
-        attn_outer_kernel,
-        grid=(pl.cdiv(m, tile),),
-        out_shape=jax.ShapeDtypeStruct((m, total), BF),
-        in_specs=[
-            pl.BlockSpec((rows, tile), lambda i: (0, i)),
-            fixed(rows, cols),
-            pl.BlockSpec((1, rows, tile), lambda i: (i, 0, 0)),
-            fixed(rows, pw),
-        ],
-        out_specs=tiled(tile, total),
-        name="attn_outer",
-    )(h1, dqkv, o_all, da_cols)
 
 
 def hidden_kernel(h_ref, w_ref, b_ref, z_ref, s_ref):
@@ -968,17 +1003,20 @@
 
 def join_kernel(n, nz, hw, width, fc, qp, out, fc_o, qkv_o, proj_o, out_o):
     uw = fc.shape[-1] // nz
-    pw = width // n
     for c in range(n):
         for b in range(nz):
             at = b * n * uw + c * uw
             fc_o[:, at : at + uw] = fc[c, 0, :, b * uw : (b + 1) * uw].astype(F32)
-        proj_o[:, c * pw : (c + 1) * pw] = qp[c, 0, :, 3 * hw : 3 * hw + pw].astype(F32)
+        size = min(128, width - c * 128)
+        if size > 0:
+            proj_o[:, c * 128 : c * 128 + size] = qp[c, 0, :, 3 * hw : 3 * hw + size].astype(F32)
         size = min(hw, width - c * hw)
         if size > 0:
             for t in range(3):
                 at = t * width + c * hw
                 qkv_o[:, at : at + size] = qp[c, 0, :, t * hw : t * hw + size].astype(F32)
+    if 128 * n < width:
+        proj_o[:, 128 * n :] = qp[n - 1, 0, :, : width - 128 * n].astype(F32)
     out_o[...] = out[...].astype(F32)
 
 
@@ -990,7 +1028,7 @@
     fc, qp = split(fc), split(qp)
     wide = lambda a: pl.BlockSpec((n, 1, wz // tiles, a.shape[-1]), lambda i: (0, i, 0, 0))
     t, ot = wz // tiles, out.shape[0] // tiles
-    cols = (nz * out.shape[0], 3 * width, width)
+    cols = (n * fc.shape[-1], 3 * width, width)
     shape = jax.ShapeDtypeStruct
     return pl.pallas_call(
         functools.partial(join_kernel, n, nz, hw, width),
@@ -1002,7 +1040,7 @@
     )(fc, qp, out)
 
 
-def attend_kernel(blocks, blk, tile, inv_ref, q_ref, k_ref, v_ref, o_ref, p_ref, qn, kn, vn, ot):
+def attend_kernel(blocks, blk, tile, inv_ref, q_ref, k_ref, v_ref, o_ref, p_ref, qn, kn, vn, on, ot):
     length = blocks * blk
     for i in range(blocks):
         src, dst = pl.ds(pl.multiple_of(inv_ref[i] * blk, blk), blk), pl.ds(i * blk, blk)
@@ -1040,11 +1078,9 @@
                 p_ref[h, pl.ds(0, i * tile), cols] = early
                 o = o + dot(v_turned[half, : i * tile], early)
             ot[half, cols] = o
-    o_nat = ot[...].T
+    on[...] = ot[...].T.astype(BF)
     for i in range(blocks):
-        o_ref[pl.ds(pl.multiple_of(inv_ref[i] * blk, blk), blk), :] = o_nat[
-            i * blk : (i + 1) * blk, :
-        ].astype(BF)
+        o_ref[pl.ds(pl.multiple_of(inv_ref[i] * blk, blk), blk), :] = on[i * blk : (i + 1) * blk, :]
 
 
 def attend(qkv, inv, blk):
@@ -1059,7 +1095,8 @@
         out_shape=[
             jax.ShapeDtypeStruct((length, cols), BF),
             jax.ShapeDtypeStruct((2 * pairs, length, length), BF),
-        ],
+        ]
+        + [jax.ShapeDtypeStruct((length, cols), BF)] * 4,
         grid_spec=pltpu.PrefetchScalarGridSpec(
             num_scalar_prefetch=1,
             grid=(pairs,),
@@ -1067,104 +1104,206 @@
             out_specs=[
                 pl.BlockSpec((length, 128), lambda p, s: (0, p)),
                 pl.BlockSpec((2, length, length), lambda p, s: (p, 0, 0)),
-            ],
-            scratch_shapes=[
-                pltpu.VMEM((length, 128), BF),
-                pltpu.VMEM((length, 128), BF),
-                pltpu.VMEM((length, 128), BF),
-                pltpu.VMEM((128, length), F32),
-            ],
+            ]
+            + [pl.BlockSpec((length, 128), lambda p, s: (0, p))] * 4,
+            scratch_shapes=[pltpu.VMEM((128, length), F32)],
         ),
         compiler_params=pltpu.CompilerParams(vmem_limit_bytes=60 * 1024 * 1024),
         name="attend",
     )(inv, qkv, qkv, qkv)
 
 
-def attend_back_kernel(
-    blocks, blk, tile, pairs, inv_ref, q_ref, k_ref, v_ref, g_ref, o_ref, p_ref, out_ref, sum_ref,
-    qn, kn, vn, gn, on, dqt, dk, dv,
+def order_kernel(blocks, blk, table, x, out):
+    for i in range(blocks):
+        src = pl.ds(pl.multiple_of(table[i] * blk, blk), blk)
+        out[i * blk : (i + 1) * blk, :] = x[src, :]
+
+
+def order(x, table, blk):
+    return pl.pallas_call(
+        functools.partial(order_kernel, table.shape[0], blk),
+        out_shape=jax.ShapeDtypeStruct(x.shape, x.dtype),
+        in_specs=[pl.BlockSpec(memory_space=pltpu.SMEM), VMEM],
+        out_specs=VMEM,
+        name="order",
+    )(table, x)
+
+
+def heads_kernel(blocks, blk, tile, table, da, w, out, rows):
+    step = pl.program_id(0)
+    rows[pl.ds(pl.multiple_of(step * tile, tile), tile), :] = dot(da[...], w[...], NT).astype(BF)
+
+    @pl.when(step == pl.num_programs(0) - 1)
+    def _():
+        for i in range(blocks):
+            src = pl.ds(pl.multiple_of(table[i] * blk, blk), blk)
+            out[i * blk : (i + 1) * blk, :] = rows[src, :]
+
+
+def heads_grad(da, w_proj, table, blk):
+    length, width = da.shape
+    cols = w_proj.shape[0]
+    tile = 256
+    return pl.pallas_call(
+        functools.partial(heads_kernel, table.shape[0], blk, tile),
+        out_shape=jax.ShapeDtypeStruct((length, cols), BF),
+        grid_spec=pltpu.PrefetchScalarGridSpec(
+            num_scalar_prefetch=1,
+            grid=(length // tile,),
+            in_specs=[
+                pl.BlockSpec((tile, width), lambda i, s: (i, 0)),
+                pl.BlockSpec((cols, width), lambda i, s: (0, 0)),
+            ],
+            out_specs=pl.BlockSpec((length, cols), lambda i, s: (0, 0)),
+            scratch_shapes=[pltpu.VMEM((length, cols), BF)],
+        ),
+        name="heads_grad",
+    )(table, da, w_proj)
+
+
+def back_kernel(
+    n, tile, hw, width, ready, q, k, v, o, do, da_hbm, p_hbm, h1_hbm, all_hbm,
+    ready_all, dqkv, sums, out,
+    da, p, h1, o_all, dqt, dk, dv, load_s, p_s, *sems,
 ):
-    length = blocks * blk
-    for i in range(blocks):
-        src, dst = pl.ds(pl.multiple_of(inv_ref[i] * blk, blk), blk), pl.ds(i * blk, blk)
-        qn[dst, :] = q_ref[src, :]
-        kn[dst, :] = k_ref[src, :]
-        vn[dst, :] = v_ref[src, :]
-        gn[dst, :] = g_ref[src, :]
-        on[dst, :] = o_ref[src, :]
-    k_turned = kn[...].astype(F32).T.astype(BF)
-    prod = (gn[...].astype(F32) * on[...].astype(F32)).T
-    deltas = [jnp.sum(prod[64 * h : 64 * h + 64, :], axis=0, keepdims=True) for h in range(2)]
+    me = lax.axis_index("ctx")
+    length, cols = q.shape
+    pairs = cols // 128
+    slots = p.shape[0]
+    greet(beside(n))
+    gather = Gather(n, ready, ready_all, sems)
+    gather.start()
+    loads = [
+        pltpu.make_async_copy(src, dst, load_s.at[i])
+        for i, (src, dst) in enumerate([(da_hbm, da), (h1_hbm, h1), (all_hbm, o_all)])
+    ]
+
+    def load_p(pair):
+        at = pair % slots
+        return pltpu.make_async_copy(p_hbm.at[pl.ds(2 * pair, 2)], p.at[at], p_s.at[at])
+
+    load_p(0).start()
+    for load in loads:
+        load.start()
     lane = lax.broadcasted_iota(jnp.int32, (1, 128), 1)
-    dk[...] = jnp.zeros_like(dk)
-    dv[...] = jnp.zeros_like(dv)
-    for i in range(length // tile):
-        cols = pl.ds(i * tile, tile)
+    held = {}
+
+    def begin(pair):
+        if pair + 1 < pairs and slots > 1:
+            load_p(pair + 1).start()
+        at = slice(pair * 128, pair * 128 + 128)
+        held["k"] = k[:, at].astype(F32).T.astype(BF)
+        prod = (do[:, at].astype(F32) * o[:, at].astype(F32)).T
+        held["d"] = [jnp.sum(prod[64 * h : 64 * h + 64, :], axis=0, keepdims=True) for h in range(2)]
+        dk[...] = jnp.zeros_like(dk)
+        dv[...] = jnp.zeros_like(dv)
+        load_p(pair).wait()
+
+    def block(pair, i):
+        win = pl.ds(i * tile, tile)
+        at = slice(pair * 128, pair * 128 + 128)
         keys = (i + 1) * tile
         for h in range(2):
             here = (lane // 64) == h
-            q = jnp.where(here, qn[cols, :].astype(F32), 0.0).astype(BF)
-            g = jnp.where(here, gn[cols, :].astype(F32), 0.0).astype(BF)
-            p = p_ref[h, pl.ds(0, keys), cols]
-            dp = dot(vn[pl.ds(0, keys), :], g, NT)
-            ds = (
-                p.astype(F32) * (dp - deltas[h][:, i * tile : (i + 1) * tile]) * 0.125
-            ).astype(BF)
+            query = jnp.where(here, q[win, at].astype(F32), 0.0).astype(BF)
+            grad = jnp.where(here, do[win, at].astype(F32), 0.0).astype(BF)
+            prob = p[pair % slots, h, pl.ds(0, keys), win]
+            dp = dot(v[pl.ds(0, keys), at], grad, NT)
+            ds = (prob.astype(F32) * (dp - held["d"][h][:, i * tile : (i + 1) * tile]) * 0.125).astype(BF)
             half = slice(64 * h, 64 * h + 64)
-            dqt[half, cols] = dot(k_turned[half, :keys], ds)
-            dk[pl.ds(0, keys), :] += dot(ds, q)
-            dv[pl.ds(0, keys), :] += dot(p, g)
-    dq = dqt[...].T
-    pair = pl.program_id(0)
-    for t, val in enumerate((dq, dk[...], dv[...])):
-        at = pl.ds(pl.multiple_of((t * pairs + pair) * 128, 128), 128)
-        sum_ref[:, at] = jnp.sum(val.astype(BF).astype(F32), axis=0, keepdims=True)
-    for i in range(blocks):
-        dst = pl.ds(pl.multiple_of(inv_ref[i] * blk, blk), blk)
-        src = slice(i * blk, (i + 1) * blk)
-        for t, val in enumerate((dq, dk, dv)):
-            at = pl.ds(pl.multiple_of((t * pairs + pair) * 128, 128), 128)
-            out_ref[dst, at] = val[src, :].astype(BF)
-
-
-def attend_back(qkv, grad, o, p, inv, blk):
-    length = qkv.shape[0]
-    cols = qkv.shape[1] // 3
-    pairs = cols // 128
-    blocks = inv.shape[0]
-    tile = 256
-    piece = lambda off: pl.BlockSpec((length, 128), lambda i, s: (0, off * pairs + i))
-    return pl.pallas_call(
-        functools.partial(attend_back_kernel, blocks, blk, tile, pairs),
-        out_shape=[
-            jax.ShapeDtypeStruct((length, 3 * cols), BF),
-            jax.ShapeDtypeStruct((1, 3 * cols), F32),
+            dqt[half, win] = dot(held["k"][half, :keys], ds)
+            dk[pl.ds(0, keys), :] += dot(ds, query)
+            dv[pl.ds(0, keys), :] += dot(prob, grad)
+
+    def end(pair):
+        for t, val in enumerate((dqt[...].T, dk[...], dv[...])):
+            at = slice((t * pairs + pair) * 128, (t * pairs + pair) * 128 + 128)
+            low = val.astype(BF)
+            sums[:, at] = jnp.sum(low.astype(F32), axis=0, keepdims=True)
+            dqkv[:, at] = low
+
+    spare = max(0, width - 128 * n)
+    whole_tiles = width // hw
+
+    def products(rows, x, y):
+        out[rows, 3 * cols :] = dot(y, da[:, pl.ds(pl.multiple_of(me * 128, 128), 128)], TN).astype(BF)
+
+        @pl.when(me < n - 1 if spare else me < n)
+        def _():
+            out[rows, : 3 * cols] = dot(x, dqkv[...], TN).astype(BF)
+
+        if spare:
+
+            @pl.when(me == n - 1)
+            def _():
+                out[rows, : 3 * cols] = jnp.zeros((x.shape[1], 3 * cols), BF)
+                out[rows, :spare] = dot(y, da[:, 128 * n :], TN).astype(BF)
+
+    def weights(lo, hi):
+        if lo == 0:
+            for load in loads:
+                load.wait()
+
+        def body(i, carry):
+            at = pl.ds(pl.multiple_of(i * hw, hw), hw)
+            products(at, h1[:, at], o_all[i])
+            return carry
+
+        lax.fori_loop(lo, hi, body, 0)
+        if hi == whole_tiles and width % hw:
+            rest = width % hw
+            at = pl.ds(hi * hw, rest)
+            products(at, h1[:, at], o_all[hi, :, :rest])
+
+    part = functools.partial
+    steps = []
+    for pair in range(pairs):
+        steps.append((1.0, part(begin, pair)))
+        steps += [(0.6 + 0.5 * i, part(block, pair, i)) for i in range(length // tile)]
+        steps.append((1.0, part(end, pair)))
+    steps += [(3.8, part(weights, lo, min(lo + 2, whole_tiles))) for lo in range(0, whole_tiles, 2)]
+    clock, work = 0.0, []
+    for size, step in steps:
+        work.append((clock, step))
+        clock += size
+    timed(work, gather.timed_steps(lambda c: 3.5 * c, 6.0, 5.0))
+    gather.finish()
+
+
+def back(n, cid, ready, q, k, v, o, do, da, p, h1, o_all):
+    length, hw = q.shape
+    width = da.shape[1]
+    if 128 * n > width:
+        da = jnp.pad(da, ((0, 0), (0, 128 * n - width)))
+    assert width <= 128 * n or (n - 1) * hw >= width and width - 128 * n <= 3 * hw
+    dma = pltpu.SemaphoreType.DMA
+    slots = min(2, hw // 128)
+    return call(
+        functools.partial(back_kernel, n, 256, hw, width),
+        cid,
+        "back",
+        (ready, q, k, v, o, do, da, p, h1, o_all),
+        [VMEM] * 6 + [ANY] * 4,
+        [
+            ((n,) + ready.shape, BF),
+            ((length, 3 * hw), BF),
+            ((1, 3 * hw), F32),
+            ((width, 3 * hw + 128), BF),
         ],
-        grid_spec=pltpu.PrefetchScalarGridSpec(
-            num_scalar_prefetch=1,
-            grid=(pairs,),
-            in_specs=[
-                piece(0),
-                piece(1),
-                piece(2),
-                piece(0),
-                piece(0),
-                pl.BlockSpec((2, length, length), lambda i, s: (i, 0, 0)),
-            ],
-            out_specs=[
-                pl.BlockSpec((length, 3 * cols), lambda i, s: (0, 0)),
-                pl.BlockSpec((1, 3 * cols), lambda i, s: (0, 0)),
-            ],
-            scratch_shapes=[pltpu.VMEM((length, 128), BF)] * 5
-            + [
-                pltpu.VMEM((128, length), F32),
-                pltpu.VMEM((length, 128), F32),
-                pltpu.VMEM((length, 128), F32),
-            ],
-        ),
-        compiler_params=pltpu.CompilerParams(vmem_limit_bytes=60 * 1024 * 1024),
-        name="attend_back",
-    )(inv, qkv, qkv, qkv, grad, o, p)
+        [ANY, VMEM, VMEM, VMEM],
+        [
+            pltpu.VMEM(da.shape, BF),
+            pltpu.VMEM((slots, 2, length, length), BF),
+            pltpu.VMEM(h1.shape, BF),
+            pltpu.VMEM(o_all.shape, BF),
+            pltpu.VMEM((128, length), F32),
+            pltpu.VMEM((length, 128), F32),
+            pltpu.VMEM((length, 128), F32),
+            dma((3,)),
+            dma((slots,)),
+        ]
+        + Gather.sems(n, ready.shape[0]),
+    )
 
 
 def norm(values):
@@ -1217,15 +1356,20 @@
         ):
             small = jnp.where(row == i, v[None, :], small)
         tile = math.gcd(wz, hw)
-        h1, cot, small, w_qkv, w_proj, tok_own, cot_own = entry(
-            n, nz, tokens, cotangent, small, wq_own, proj_weight.reshape(wz // tile, tile, width), hw
+        h1, cot, small, w_qkv, w_proj, tok_own, cot_own, wfc_own, wout_own = entry(
+            n,
+            nz,
+            tokens,
+            cotangent,
+            small,
+            wq_own,
+            proj_weight.reshape(wz // tile, tile, width),
+            fc_weight.reshape(25, wz // 25, fc_weight.shape[1]),
+            out_weight.reshape(n, uw, width),
+            hw,
         )
-        small, fc_weight, out_weight = lax.optimization_barrier((small, fc_weight, out_weight))
-        wfc_own = jnp.concatenate(
-            [take(fc_weight, t * unit_z + ctx * uw, uw, 1) for t in range(nz)], axis=1
-        )
-        w_fc = lax.all_gather(wfc_own, "fsdp", axis=0, tiled=True)
-        w_out = lax.all_gather(take(out_weight, ctx * uw, uw), "fsdp", axis=0, tiled=True)
+        w_fc = lax.all_gather(wfc_own.reshape(wz, units), "fsdp", axis=0, tiled=True)
+        w_out = lax.all_gather(wout_own, "fsdp", axis=0, tiled=True)
         length = n * rows
         flat = lambda a: a.reshape(length, a.shape[-1])
         h1, cot = flat(h1), flat(cot)
@@ -1235,7 +1379,7 @@
         qkv_bias = jnp.concatenate([pad_cols(small[2]), jnp.zeros((hw,), F32), pad_cols(small[3])])
 
         qkv = (dot(h1, w_qkv) + qkv_bias).astype(BF)
-        o, p = attend(qkv, inv, blk)
+        o, p, q_pos, k_pos, v_pos, o_pos = attend(qkv, inv, blk)
         mid, h2 = middle(n, 2, o, w_proj, tok_own, small)
         h2 = flat(h2)
         hidden, slope = hidden_units(h2, w_fc, fb)
@@ -1243,7 +1387,8 @@
         in_parts = lambda a: a.reshape(nz, parts, a.shape[0] // nz // parts, a.shape[1])
         o, part_out = lax.optimization_barrier((o, part_out))
         o_all = spread(n, 3, o.reshape(4, length // 4, hw))
-        w_out, o_all = lax.optimization_barrier((w_out, o_all))
+        h1_pos = order(h1, inv, blk)
+        w_out, o_all, h1_pos = lax.optimization_barrier((w_out, o_all, h1_pos))
         to_owner = lambda a: lax.psum_scatter(a, "fsdp", scatter_dimension=0, tiled=True)
         sum_out = to_owner(part_out)
         du, dfb = hidden_back(cot, w_out, slope)
@@ -1252,10 +1397,21 @@
         sum_fc = to_owner(part_fc)
         da, dmid, layer_out, sums = turn(n, 4, du, w_fc, hidden, w_out, mid, cot_own, small)
         da = flat(da)
-        do = dot(da, w_proj, NT).astype(BF)
-        dqkv, bias_cols = attend_back(qkv, do, o, p, inv, blk)
-        pw = width // n
-        part_attn = attn_outer(h1, dqkv, o_all.reshape(n, length, hw), take(da, ctx * pw, pw, 1))
+        all_out, dqkv, bias_cols, part_attn = back(
+            n,
+            6,
+            sum_out.reshape(parts, uw // parts, width),
+            q_pos,
+            k_pos,
+            v_pos,
+            o_pos,
+            heads_grad(da, w_proj, inv, blk),
+            da,
+            p,
+            h1_pos,
+            o_all.reshape(n, length, hw),
+        )
+        dqkv = order(dqkv, table, blk)
 
         put = lambda v, size: lax.dynamic_update_slice_in_dim(
             jnp.zeros((1, size), F32), v, ctx * v.shape[1], 1
@@ -1269,12 +1425,11 @@
         vectors = jnp.concatenate(
             [sums + jnp.pad(biases, ((2, 4), (0, 0))), jnp.pad(wide_fb, ((0, -nz % 8), (0, width - unit_z)))]
         )
-        all_fc, all_out, all_attn, grad_tokens, vectors = tail(
+        all_fc, all_attn, grad_tokens, vectors = tail(
             n,
             nz,
             5,
             sum_fc.reshape(parts, wz // parts, units),
-            sum_out.reshape(parts, uw // parts, width),
             in_parts(part_attn),
             dqkv,
             w_qkv,

time: 469 us -> 449 us (0.957)
  waiting for transfers between devices: 19.5 us -> 5.57 us
  local copies, waits for them, and re-layouts: 17.3 us -> 11.6 us
    pallas_call x2 -> x3, Pallas kernels: 22.9 us -> 12.2 us  [the longest x2 6.65 us: order(): pl.pallas_call(functools.partial(order_kernel, table.shape[0], blk), out_...]
    reduce_scatter x1, waiting for transfers between devices: 9.67 us -> 0.01 us  [body(): lax.psum_scatter(a, 'fsdp', scatter_dimension=0, tiled=True)]
    pallas_call x4 -> x5, Pallas kernels: 238 us -> 247 us  [call(): pl.pallas_call(kernel, out_shape=[jax.ShapeDtypeStruct(*o) for o in outs]...]
    dynamic_slice x8 -> x5, local copies, waits for them, and re-layouts: 8.82 us -> 2.88 us  [body(): lax.dynamic_slice_in_dim(a, at, size, axis)]
    all_gather x2, waiting for transfers between devices: 9.77 us -> 4.81 us  [the longest x1 4.78 us: body(): w_out = lax.all_gather(wout_own, 'fsdp', axis=0, tiled=True)]
    dot_general x3 -> x2, matrix products: 16 us -> 13.1 us  [dot(): return lax.dot_general(a, b, dims, preferred_element_type=F32)]
  transfers between devices with their start and end apart: 4 -> 4, of which waited for: 2 -> 1; matrix products, arithmetic and copies ran while one was open for 6% -> 4% of each run, Pallas kernels for 40% -> 48%
where the time goes in v4:
time: 449 us; the launch traced here: 444 us
  Pallas kernels  396 us (88%)
  between operations  14.4 us (3%)
  matrix products  13.1 us (3%)
  local copies, waits for them, and re-layouts  11.6 us (3%)
  waiting for transfers between devices  5.57 us (1%)
    pallas_call x5, Pallas kernels, call(): pl.pallas_call(kernel, out_shape=[jax.ShapeDtypeStruct(*o) for o in outs]...  247 us
    pallas_call x1, Pallas kernels, entry(): pl.pallas_call(functools.partial(entry_kernel, n, nz), out_shape=[shape((...  72.5 us
    pallas_call x1, Pallas kernels, join(): pl.pallas_call(functools.partial(join_kernel, n, nz, hw, width), grid=(ti...  24.5 us
    dot_general x2, matrix products, dot(): return lax.dot_general(a, b, dims, preferred_element_type=F32)  13.1 us
    pallas_call x1, Pallas kernels, attend(): pl.pallas_call(functools.partial(attend_kernel, blocks, blk, tile), out_s...  12.7 us
    pallas_call x1, Pallas kernels, hidden_units(): pl.pallas_call(hidden_kernel, grid=(rows // tile,), out_shape=[shape, sha...  9.39 us
    pallas_call x1, Pallas kernels, outer(): pl.pallas_call(outer_kernel, grid=(pl.cdiv(m, tile),), out_shape=jax.Shap...  9.08 us
  transfers between devices with their start and end apart: 4, of which 1 were waited for; matrix products, arithmetic and copies ran while one was open for 4% of the time, Pallas kernels for 48%

profile of v4, /device:TPU:0, one launch (start us, length us, event | category | flops | bytes accessed | tf_op | source)
XLA Modules:
  0.0 444.1 jit_solution(9270262249582225272)
XLA Ops:
  7.3 0.0 all-gather.5.cloned.1.call-start
  7.4 0.8 dynamic_slice.24
  8.2 1.3 pad_dynamic-slice_fusion.2
  9.5 0.9 pad_maximum_fusion
  10.4 0.7 select_select_fusion.small
  11.1 72.5 %entry.1 = (bf16[8,2,64,1600]{3,2,1,0:T(8,128)(2,1)}, bf16[8,2,64,1600]{3,2,1,0:T(8,128)(2,1)}, f32[16,1600]{1,0:T(8,128)}, bf16[20,80,768]{2,1,0:T(8,128)(2,1)}...) custom-call(bf16[1600,128]{1,0:T(8,128)(2,1)} %bitcast.59, ...), custom_call_target="tpu_custom_call" | custom-call | tf_op jit(solution)/shard_map/entry/pallas_call | solution.py:370
  83.7 0.0 all-gather.5.cloned.1.call-update
  83.7 0.0 all-gather.3.cloned.1.call-start
  83.7 0.7 all-gather.3.cloned.1.call-update
  84.4 0.0 reduce-scatter.7.cloned.1.call-start
  84.5 0.1 copy.40
  84.6 0.1 eq.98.table
  84.7 0.9 slice_reduce_fusion
  85.6 0.1 reshape_squeeze.3
  85.7 0.7 reshape.112.b_ref
  86.4 0.1 pad_dynamic-slice_fusion.3
  86.4 0.1 pad_dynamic-slice_fusion.4
  86.5 1.2 iota_reduce_fusion
  87.7 6.9 %add_convert_fusion.q_ref.k_ref.v_ref = bf16[1024,768]{1,0:T(8,128)(2,1)} fusion(bf16[1024,1600]{1,0:T(8,128)(2,1)} %bitcast.48, bf16[1600,768]{1,0:T(8,128)(2,1)} %bitcast.51, f32[768]{0:T(1024)S(1)} %pad_maximum_fusion.1), kind=kOutput, calls=%fused_computation.4 | convolution fusion | flops 2518155264 | bytes 7310336 | tf_op jit(solution)/shard_map/dot_general | solution.py:23
  94.6 12.7 %attend.1 = (bf16[1024,256]{1,0:T(8,128)(2,1)}, bf16[4,1024,1024]{2,1,0:T(8,128)(2,1)}, bf16[1024,256]{1,0:T(8,128)(2,1)}, bf16[1024,256]{1,0:T(8,128)(2,1)}, bf...) custom-call(s32[16]{0:T(128)} %get-tuple-element.62.inv_ref.table, ...), custom_call_target="tpu_custom_call" | custom-call | tf_op jit(solution)/shard_map/attend/pallas_call | solution.py:1093
  107.3 43.9 %middle.1 = (f32[128,1600]{1,0:T(8,128)}, bf16[8,4,32,1600]{3,2,1,0:T(8,128)(2,1)}) custom-call(bf16[1024,256]{1,0:T(8,128)(2,1)} %get-tuple-element.72.o, bf16[256,1600]{1,0:T(8,128)(2,1)} %bitcast.44, bf16[128,1600]{1,0:T(8,128)(2,1)} %get-tuple-element.68.tok, f32[16,1600]{1,0:T(8,128)} %get-tuple-element.65.vec), custom_call_target="tpu_custom_call" | custom-call | tf_op jit(solution)/shard_map/middle/pallas_call | solution.py:727
  151.2 0.0 all-gather.5.cloned.1.call-done.w_ref.w_fc
  151.2 9.4 %hidden.1 = (bf16[1024,800]{1,0:T(8,128)(2,1)}, bf16[1024,800]{1,0:T(8,128)(2,1)}) custom-call(bf16[1024,1600]{1,0:T(8,128)(2,1)} %bitcast.37, bf16[1600,800]{1,0:T(8,128)(2,1)} %all-gather.5.cloned.1.call-done.w_ref.w_fc, f32[1,800]{1,0:T(1,128)} %reshape.112.b_ref), custom_call_target="tpu_custom_call" | custom-call | tf_op jit(solution)/shard_map/hidden/pallas_call | solution.py:977
  160.6 6.2 %convolution_convert_fusion = bf16[800,1600]{1,0:T(8,128)(2,1)} fusion(bf16[1024,800]{1,0:T(8,128)(2,1)} %get-tuple-element.71.hid, bf16[1024,1600]{1,0:T(8,128)(2,1)S(1)} %bitcast.47), kind=kOutput, calls=%fused_computation.3 | convolution fusion | flops 2622720000 | bytes 7475200 | tf_op jit(solution)/shard_map/dot_general | solution.py:23
  166.8 0.0 reduce-scatter.7.cloned.1.call-update
  166.8 0.2 reduce-scatter.5.cloned.1.call-start
  167.1 4.0 order.2.h1_hbm
  171.0 25.0 %spread.1 = bf16[8,4,256,256]{3,2,1,0:T(8,128)(2,1)} custom-call(bf16[4,256,256]{2,1,0:T(8,128)(2,1)} %bitcast.54), custom_call_target="tpu_custom_call" | custom-call | tf_op jit(solution)/shard_map/spread/pallas_call | solution.py:727
  196.0 4.8 %all-gather.3.cloned.1.call-done.w_ref.w_out = bf16[800,1600]{1,0:T(8,128)(2,1)} async-done(((bf16[200,1600]{1,0:T(8,128)(2,1)}), bf16[800,1600]{1,0:T(8,128)(2,1)}) %all-gather.3.cloned.1.call-update) | async-done | bytes 2560016 | tf_op jit(solution)/shard_map/all_gather | solution.py:1372
  200.8 7.9 %hidden_back.1 = (bf16[1024,800]{1,0:T(8,128)(2,1)}, f32[1,800]{1,0:T(1,128)}) custom-call(bf16[1024,1600]{1,0:T(8,128)(2,1)} %bitcast.46, bf16[800,1600]{1,0:T(8,128)(2,1)} %all-gather.3.cloned.1.call-done.w_ref.w_out, bf16[1024,800]{1,0:T(8,128)(2,1)} %get-tuple-element.74.s_ref), custom_call_target="tpu_custom_call" | custom-call | tf_op jit(solution)/shard_map/hidden_back/pallas_call | solution.py:991
  208.7 9.1 %outer.1 = bf16[1600,800]{1,0:T(8,128)(2,1)} custom-call(bf16[1024,1600]{1,0:T(8,128)(2,1)} %bitcast.38, bf16[1024,800]{1,0:T(8,128)(2,1)} %get-tuple-element.76.y_ref.du), custom_call_target="tpu_custom_call" | custom-call | tf_op jit(solution)/shard_map/outer/pallas_call | solution.py:933
  217.8 0.0 reduce-scatter.5.cloned.1.call-update
  217.8 54.5 %turn.1 = (bf16[8,4,32,1600]{3,2,1,0:T(8,128)(2,1)}, f32[128,1600]{1,0:T(8,128)}, bf16[128,1600]{1,0:T(8,128)(2,1)}, f32[8,1600]{1,0:T(8,128)}) custom-call(bf16[1024,800]{1,0:T(8,128)(2,1)} %get-tuple-element.76.y_ref.du, bf16[1600,800]{1,0:T(8,128)(2,1)} %all-gather.5.cloned.1.call-done.w_ref.w_fc, bf16[1024,800]{1,0:T(8,128)(2,1)} %get-tuple-element.71.hid, ...), custom_call_target="tpu_custom_call" | custom-call | tf_op jit(solution)/shard_map/turn/pallas_call | solution.py:727
  272.3 2.0 copy.41
  274.3 5.6 %heads_grad.1.do = bf16[1024,256]{1,0:T(8,128)(2,1)} custom-call(s32[16]{0:T(128)} %get-tuple-element.62.inv_ref.table, bf16[1024,1600]{1,0:T(8,128)(2,1)} %bitcast.35, bf16[256,1600]{1,0:T(8,128)(2,1)} %bitcast.45), custom_call_target="tpu_custom_call" | custom-call | tf_op jit(solution)/shard_map/heads_grad/pallas_call | solution.py:1147
  279.8 0.1 reshape.119
  279.9 0.5 dynamic_update_slice.11
  280.4 0.0 reduce-scatter.7.cloned.1.call-done
  280.4 37.4 %back.1 = (bf16[8,5,40,1600]{3,2,1,0:T(8,128)(2,1)}, bf16[1024,768]{1,0:T(8,128)(2,1)}, f32[1,768]{1,0:T(1,128)}, bf16[1600,896]{1,0:T(8,128)(2,1)}) custom-call(bf16[5,40,1600]{2,1,0:T(8,128)(2,1)} %bitcast.58, bf16[1024,256]{1,0:T(8,128)(2,1)} %get-tuple-element.82.q, bf16[1024,256]{1,0:T(8,128)(2,1)} %get-tuple-element.83.k, ...), custom_call_target="tpu_custom_call" | custom-call | tf_op jit(solution)/shard_map/back/pallas_call | solution.py:727
  317.8 2.7 order.3.dqkv
  320.6 0.7 select_maximum_fusion.v_in
  321.3 86.6 %tail.1 = (bf16[8,5,80,800]{3,2,1,0:T(8,128)(2,1)}, bf16[8,5,80,896]{3,2,1,0:T(8,128)(2,1)}, bf16[128,1600]{1,0:T(8,128)(2,1)}, f32[16,1600]{1,0:T(8,128)}) custom-call(bf16[5,80,800]{2,1,0:T(8,128)(2,1)} %bitcast.56, bf16[4,5,80,896]{3,2,1,0:T(8,128)(2,1)} %bitcast.50, bf16[1024,768]{1,0:T(8,128)(2,1)} %order.3.dqkv, bf16[1600,768]{1,0:T(8,128)(2,1)} %bitcast.52, ...), custom_call_target="tpu_custom_call" | custom-call | tf_op jit(solution)/shard_map/tail/pallas_call | solution.py:727
  407.9 0.8 slice.66
  408.7 0.8 slice.58
  409.5 1.9 copy.42
  411.5 0.6 dynamic-slice_reduce_fusion
  412.1 24.5 %join.1 = (f32[400,6400]{1,0:T(8,128)}, f32[400,4800]{1,0:T(8,128)}, f32[400,1600]{1,0:T(8,128)}, f32[1600,1600]{1,0:T(8,128)}) custom-call(bf16[8,25,16,800]{3,2,1,0:T(8,128)(2,1)} %bitcast.39, bf16[8,25,16,896]{3,2,1,0:T(8,128)(2,1)} %bitcast.40, bf16[1600,1600]{1,0:T(8,128)(2,1)} %bitcast.41), custom_call_target="tpu_custom_call" | custom-call | tf_op jit(solution)/shard_map/join/pallas_call | solution.py:1033
  436.5 0.7 fusion.2
  (45 shorter events, 0.2 us)
Async XLA Ops:
  7.2 3.2 copy-start.13
  7.2 3.2 copy-start.12
  7.2 3.2 copy-start.11
  7.2 3.2 copy-start.10
  7.2 3.1 copy-start.9
  7.2 3.1 copy-start.8
  7.2 3.1 copy-start.7
  7.3 3.1 copy-start.6
  7.3 144.0 %all-gather.5.cloned.1.call-start = ((), (), s32[]{:S(2)}) async-start(), calls=%async_computation.3 | async-start | bytes 3584000 | tf_op jit(solution)/shard_map/all_gather | solution.py:1371
  11.1 73.4 %copy-start.5 = (s32[8,2]{0,1:T(2,128)S(1)}, s32[8,2]{0,1:T(2,128)}, u32[]{:S(2)}) copy-start(s32[8,2]{0,1:T(2,128)} %param.17) | copy-start | bytes 196
  83.7 117.1 %all-gather.3.cloned.1.call-start = ((), (), s32[]{:S(2)}) async-start(), calls=%async_computation.2 | async-start | bytes 3328000 | tf_op jit(solution)/shard_map/all_gather | solution.py:1372
  84.4 196.0 %reduce-scatter.7.cloned.1.call-start = ((), (), s32[]{:S(2)}) async-start(), calls=%async_computation.5 | async-start | bytes 3328000
  84.7 9.9 %copy-start.3 = (s32[16]{0:T(128)}, s32[16]{0:T(128)S(1)}, u32[]{:S(2)}) copy-start(s32[16]{0:T(128)S(1)} %eq.98.table) | copy-start | bytes 196
  151.2 9.4 %copy-start = (bf16[8,2,64,1600]{3,2,1,0:T(8,128)(2,1)S(1)}, bf16[8,2,64,1600]{3,2,1,0:T(8,128)(2,1)}, u32[]{:S(2)}) copy-start(bf16[8,2,64,1600]{3,2,1,0:T(8,128)(2,1)} %get-tuple-element.60) | copy-start | bytes 9830404
  166.8 154.5 %reduce-scatter.5.cloned.1.call-start = ((), (), s32[]{:S(2)}) async-start(), calls=%async_computation.4 | async-start | bytes 3584000 | tf_op jit(solution)/shard_map/reduce_scatter | solution.py:1392
  272.3 7.5 %copy-start.2 = (f32[1,800]{1,0:T(1,128)S(1)}, f32[1,800]{1,0:T(1,128)}, u32[]{:S(2)}) copy-start(f32[1,800]{1,0:T(1,128)} %get-tuple-element.95) | copy-start | bytes 9604
  317.8 2.7 copy-start.4
  317.8 2.8 copy-start.1
Sparse Core Ops, SparseCore 0:
  83.8 61.2 all-gather.4
  146.7 54.0 all-gather.2
  203.7 51.1 reduce-scatter.6
  257.6 56.5 reduce-scatter.4

commit v5 on v4

--- a/solution.py
+++ b/solution.py
@@ -12,11 +12,18 @@
 BF = jnp.bfloat16
 F32 = jnp.float32
 MESH = pl.DeviceIdType.MESH
+ENTRY, ATTEND, MIDDLE, SPREAD, TURN, BACK, TAIL = 60, 60, 60, 60, 60, 60, 30
+HIDDEN, HIDDEN_BACK, OUTER, ORDER, HEADS_GRAD, JOIN = 60, 60, 60, 60, 60, 8
 ANY = pl.BlockSpec(memory_space=pl.ANY)
 VMEM = pl.BlockSpec(memory_space=pltpu.VMEM)
+HBM = pl.BlockSpec(memory_space=pltpu.HBM)
 NN = (((1,), (0,)), ((), ()))
 NT = (((1,), (1,)), ((), ()))
 TN = (((0,), (0,)), ((), ()))
+
+
+def room(length, mib):
+    return pltpu.CompilerParams(vmem_limit_bytes=(mib if length <= 1024 else 60) * 1024 * 1024)
 
 
 def dot(a, b, dims=NN):
@@ -380,7 +387,7 @@
             shape(fc.shape[:2] + (fc.shape[2] // n,), BF),
             shape(out.shape[1:], BF),
         ],
-        in_specs=[VMEM] * 5 + [ANY, ANY],
+        in_specs=[VMEM] * 5 + [HBM, HBM],
         out_specs=[ANY, ANY, VMEM, ANY, ANY] + [VMEM] * 4,
         scratch_shapes=[
             pltpu.VMEM(piece, BF),
@@ -398,7 +405,7 @@
         + Relay.sems(nz * k)
         + Relay.sems(blocks),
         compiler_params=pltpu.CompilerParams(
-            collective_id=1, has_side_effects=True, vmem_limit_bytes=60 * 1024 * 1024
+            collective_id=1, has_side_effects=True, vmem_limit_bytes=(ENTRY if n == 8 else 60) * 1024 * 1024
         ),
         name="entry",
     )(tokens.T, cot.T, small, wq, wp, fc, out)
@@ -723,7 +730,7 @@
     return [sib] + [2 * p + core for p in (others[:2] if n == 8 else others)]
 
 
-def call(kernel, cid, name, ins, in_specs, outs, out_specs, scratch):
+def call(kernel, cid, name, ins, in_specs, outs, out_specs, scratch, mib=60):
     return pl.pallas_call(
         kernel,
         out_shape=[jax.ShapeDtypeStruct(*o) for o in outs],
@@ -731,7 +738,7 @@
         out_specs=out_specs,
         scratch_shapes=scratch,
         compiler_params=pltpu.CompilerParams(
-            collective_id=cid, has_side_effects=True, vmem_limit_bytes=60 * 1024 * 1024
+            collective_id=cid, has_side_effects=True, vmem_limit_bytes=mib * 1024 * 1024
         ),
         name=name,
     )(*ins)
@@ -769,6 +776,7 @@
         [((rows, width), F32), ((n,) + piece, BF)],
         [VMEM, ANY],
         [pltpu.VMEM(piece, BF)] + Scatter.scratch(n, rows, width) + Gather.sems(n, parts),
+        MIDDLE if n == 8 else 60,
     )
 
 
@@ -791,6 +799,7 @@
         [((n,) + array.shape, BF)],
         [ANY],
         Gather.sems(n, array.shape[0]),
+        SPREAD if n == 8 else 60,
     )[0]
 
 
@@ -844,6 +853,7 @@
         + Scatter.scratch(n, rows, width)
         + Scatter.scratch(n, rows, width)
         + Gather.sems(n, parts),
+        TURN if n == 8 else 60,
     )
 
 
@@ -909,7 +919,7 @@
         cid,
         "tail",
         (fc, part, dqkv, w_qkv, tok, dmid, vec, v_in),
-        [ANY] * 4 + [VMEM] * 4,
+        [HBM] * 4 + [VMEM] * 4,
         [((n,) + fc.shape, BF), ((n,) + attn, BF), (tok.shape, BF), (v_in.shape, F32)],
         [ANY, ANY, VMEM, VMEM],
         [pltpu.VMEM(v_in.shape, F32), pltpu.VMEM(attn, BF)]
@@ -920,6 +930,7 @@
         + Vectors.scratch(n, nz, v_in.shape)
         + Gather.sems(n, fc.shape[0])
         + Gather.sems(n, attn[0]),
+        TAIL if n == 8 else 60,
     )
 
 
@@ -936,6 +947,7 @@
         out_shape=jax.ShapeDtypeStruct((m, y.shape[1]), BF),
         in_specs=[pl.BlockSpec((rows, tile), lambda i: (0, i)), fixed(*y.shape)],
         out_specs=tiled(tile, y.shape[1]),
+        compiler_params=room(rows, OUTER),
         name="outer",
     )(x, y)
 
@@ -980,6 +992,7 @@
         out_shape=[shape, shape],
         in_specs=[tiled(tile, width), fixed(width, units), fixed(1, units)],
         out_specs=[tiled(tile, units), tiled(tile, units)],
+        compiler_params=room(rows, HIDDEN),
         name="hidden",
     )(h2, w_fc, bias)
 
@@ -997,6 +1010,7 @@
         ],
         in_specs=[tiled(tile, width), fixed(units, width), tiled(tile, units)],
         out_specs=[tiled(tile, units), fixed(1, units)],
+        compiler_params=room(rows, HIDDEN_BACK),
         name="hidden_back",
     )(cot, w_out, slope)
 
@@ -1036,6 +1050,7 @@
         out_shape=[shape((wz, c), F32) for c in cols] + [shape(out.shape, F32)],
         in_specs=[wide(fc), wide(qp), tiled(ot, width)],
         out_specs=[tiled(t, c) for c in cols] + [tiled(ot, width)],
+        compiler_params=room(1024, JOIN),
         name="join",
     )(fc, qp, out)
 
@@ -1108,7 +1123,7 @@
             + [pl.BlockSpec((length, 128), lambda p, s: (0, p))] * 4,
             scratch_shapes=[pltpu.VMEM((128, length), F32)],
         ),
-        compiler_params=pltpu.CompilerParams(vmem_limit_bytes=60 * 1024 * 1024),
+        compiler_params=room(length, ATTEND),
         name="attend",
     )(inv, qkv, qkv, qkv)
 
@@ -1125,6 +1140,7 @@
         out_shape=jax.ShapeDtypeStruct(x.shape, x.dtype),
         in_specs=[pl.BlockSpec(memory_space=pltpu.SMEM), VMEM],
         out_specs=VMEM,
+        compiler_params=room(x.shape[0], ORDER),
         name="order",
     )(table, x)
 
@@ -1157,6 +1173,7 @@
             out_specs=pl.BlockSpec((length, cols), lambda i, s: (0, 0)),
             scratch_shapes=[pltpu.VMEM((length, cols), BF)],
         ),
+        compiler_params=room(length, HEADS_GRAD),
         name="heads_grad",
     )(table, da, w_proj)
 
@@ -1261,7 +1278,8 @@
         steps.append((1.0, part(begin, pair)))
         steps += [(0.6 + 0.5 * i, part(block, pair, i)) for i in range(length // tile)]
         steps.append((1.0, part(end, pair)))
-    steps += [(3.8, part(weights, lo, min(lo + 2, whole_tiles))) for lo in range(0, whole_tiles, 2)]
+    cut = whole_tiles // 2
+    steps += [(5.5, part(weights, 0, cut)), (5.5, part(weights, cut, whole_tiles))]
     clock, work = 0.0, []
     for size, step in steps:
         work.append((clock, step))
@@ -1303,6 +1321,7 @@
             dma((slots,)),
         ]
         + Gather.sems(n, ready.shape[0]),
+        BACK if n == 8 else 60,
     )
 
 
@@ -1442,6 +1461,9 @@
         grad_fc, grad_qkv, grad_proj, grad_out = join(
             n, nz, hw, whole_rows(all_fc), whole_rows(all_attn), all_out.reshape(unit_z, width)
         )
+        vectors, grad_tokens, layer_out, grad_fc = lax.optimization_barrier(
+            (vectors, grad_tokens, layer_out, grad_fc)
+        )
         mine = take(vectors[:8], z * wz, wz, 1)
         gfb = take(vectors[8 : 8 + nz], z, 1).reshape(-1)[:unit_z]
         return (

time: 449 us -> 436 us (0.971)
  Pallas kernels: 396 us -> 381 us
    pallas_call x1, Pallas kernels: 24.5 us -> 15.8 us  [join(): pl.pallas_call(functools.partial(join_kernel, n, nz, hw, width), grid=(ti...]
    pallas_call x5, Pallas kernels: 247 us -> 241 us  [call(): pl.pallas_call(kernel, out_shape=[jax.ShapeDtypeStruct(*o) for o in outs]...]
  transfers between devices with their start and end apart: 4 -> 4, of which waited for: 1 -> 1; matrix products, arithmetic and copies ran while one was open for 4% -> 4% of each run, Pallas kernels for 48% -> 49%
where the time goes in v5:
time: 436 us; the launch traced here: 432 us
  Pallas kernels  381 us (87%)
  between operations  14.5 us (3%)
  local copies, waits for them, and re-layouts  14 us (3%)
  matrix products  13.1 us (3%)
  waiting for transfers between devices  5.69 us (1%)
    pallas_call x5, Pallas kernels, call(): pl.pallas_call(kernel, out_shape=[jax.ShapeDtypeStruct(*o) for o in outs]...  241 us
    pallas_call x1, Pallas kernels, entry(): pl.pallas_call(functools.partial(entry_kernel, n, nz), out_shape=[shape((...  72.5 us
    pallas_call x1, Pallas kernels, join(): pl.pallas_call(functools.partial(join_kernel, n, nz, hw, width), grid=(ti...  15.8 us
    dot_general x2, matrix products, dot(): return lax.dot_general(a, b, dims, preferred_element_type=F32)  13.1 us
    pallas_call x1, Pallas kernels, attend(): pl.pallas_call(functools.partial(attend_kernel, blocks, blk, tile), out_s...  12.7 us
    pallas_call x1, Pallas kernels, hidden_units(): pl.pallas_call(hidden_kernel, grid=(rows // tile,), out_shape=[shape, sha...  9.41 us
    pallas_call x1, Pallas kernels, outer(): pl.pallas_call(outer_kernel, grid=(pl.cdiv(m, tile),), out_shape=jax.Shap...  9.08 us
  transfers between devices with their start and end apart: 4, of which 1 were waited for; matrix products, arithmetic and copies ran while one was open for 4% of the time, Pallas kernels for 49%

profile of v5, /device:TPU:0, one launch (start us, length us, event | category | flops | bytes accessed | tf_op | source)
XLA Modules:
  0.0 431.5 jit_solution(10202089394529433746)
XLA Ops:
  7.3 0.0 all-gather.5.cloned.1.call-start
  7.4 0.8 dynamic_slice.24
  8.2 1.3 pad_dynamic-slice_fusion.2
  9.5 0.9 pad_maximum_fusion
  10.4 0.7 select_select_fusion.small
  11.1 72.5 %entry.1 = (bf16[8,2,64,1600]{3,2,1,0:T(8,128)(2,1)}, bf16[8,2,64,1600]{3,2,1,0:T(8,128)(2,1)}, f32[16,1600]{1,0:T(8,128)}, bf16[20,80,768]{2,1,0:T(8,128)(2,1)}...) custom-call(bf16[1600,128]{1,0:T(8,128)(2,1)} %bitcast.61, ...), custom_call_target="tpu_custom_call" | custom-call | tf_op jit(solution)/shard_map/entry/pallas_call | solution.py:377
  83.6 0.0 all-gather.5.cloned.1.call-update
  83.6 0.0 all-gather.3.cloned.1.call-start
  83.7 0.7 all-gather.3.cloned.1.call-update
  84.4 0.0 reduce-scatter.7.cloned.1.call-start
  84.5 0.1 copy.40
  84.5 0.1 eq.98.table
  84.6 0.9 slice_reduce_fusion
  85.6 0.1 reshape_squeeze.3
  85.7 0.7 reshape.112.b_ref
  86.3 0.1 pad_dynamic-slice_fusion.3
  86.4 0.1 pad_dynamic-slice_fusion.4
  86.5 1.2 iota_reduce_fusion
  87.7 6.9 %add_convert_fusion.q_ref.k_ref.v_ref = bf16[1024,768]{1,0:T(8,128)(2,1)} fusion(bf16[1024,1600]{1,0:T(8,128)(2,1)} %bitcast.54, bf16[1600,768]{1,0:T(8,128)(2,1)} %bitcast.40, f32[768]{0:T(1024)S(1)} %pad_maximum_fusion.1), kind=kOutput, calls=%fused_computation.4 | convolution fusion | flops 2518155264 | bytes 7310336 | tf_op jit(solution)/shard_map/dot_general | solution.py:30
  94.5 12.7 %attend.1 = (bf16[1024,256]{1,0:T(8,128)(2,1)}, bf16[4,1024,1024]{2,1,0:T(8,128)(2,1)}, bf16[1024,256]{1,0:T(8,128)(2,1)}, bf16[1024,256]{1,0:T(8,128)(2,1)}, bf...) custom-call(s32[16]{0:T(128)} %get-tuple-element.66.inv_ref.table, ...), custom_call_target="tpu_custom_call" | custom-call | tf_op jit(solution)/shard_map/attend/pallas_call | solution.py:1108
  107.2 43.8 %middle.1 = (f32[128,1600]{1,0:T(8,128)}, bf16[8,4,32,1600]{3,2,1,0:T(8,128)(2,1)}) custom-call(bf16[1024,256]{1,0:T(8,128)(2,1)} %get-tuple-element.76.o, bf16[256,1600]{1,0:T(8,128)(2,1)} %bitcast.50, bf16[128,1600]{1,0:T(8,128)(2,1)} %get-tuple-element.72.tok, f32[16,1600]{1,0:T(8,128)} %get-tuple-element.69.vec), custom_call_target="tpu_custom_call" | custom-call | tf_op jit(solution)/shard_map/middle/pallas_call | solution.py:734
  151.1 0.0 all-gather.5.cloned.1.call-done.w_ref.w_fc
  151.1 9.4 %hidden.1 = (bf16[1024,800]{1,0:T(8,128)(2,1)}, bf16[1024,800]{1,0:T(8,128)(2,1)}) custom-call(bf16[1024,1600]{1,0:T(8,128)(2,1)} %bitcast.46, bf16[1600,800]{1,0:T(8,128)(2,1)} %all-gather.5.cloned.1.call-done.w_ref.w_fc, f32[1,800]{1,0:T(1,128)} %reshape.112.b_ref), custom_call_target="tpu_custom_call" | custom-call | tf_op jit(solution)/shard_map/hidden/pallas_call | solution.py:989
  160.5 6.2 %convolution_convert_fusion = bf16[800,1600]{1,0:T(8,128)(2,1)} fusion(bf16[1024,800]{1,0:T(8,128)(2,1)} %get-tuple-element.75.hid, bf16[1024,1600]{1,0:T(8,128)(2,1)S(1)} %bitcast.53), kind=kOutput, calls=%fused_computation.3 | convolution fusion | flops 2622720000 | bytes 7475200 | tf_op jit(solution)/shard_map/dot_general | solution.py:30
  166.7 0.2 reduce-scatter.5.cloned.1.call-start
  166.9 4.0 order.2.h1_hbm
  170.9 25.0 %spread.1 = bf16[8,4,256,256]{3,2,1,0:T(8,128)(2,1)} custom-call(bf16[4,256,256]{2,1,0:T(8,128)(2,1)} %bitcast.57), custom_call_target="tpu_custom_call" | custom-call | tf_op jit(solution)/shard_map/spread/pallas_call | solution.py:734
  195.9 4.9 %all-gather.3.cloned.1.call-done.w_ref.w_out = bf16[800,1600]{1,0:T(8,128)(2,1)} async-done(((bf16[200,1600]{1,0:T(8,128)(2,1)}), bf16[800,1600]{1,0:T(8,128)(2,1)}) %all-gather.3.cloned.1.call-update) | async-done | bytes 2560016 | tf_op jit(solution)/shard_map/all_gather | solution.py:1391
  200.8 7.9 %hidden_back.1 = (bf16[1024,800]{1,0:T(8,128)(2,1)}, f32[1,800]{1,0:T(1,128)}) custom-call(bf16[1024,1600]{1,0:T(8,128)(2,1)} %bitcast.52, bf16[800,1600]{1,0:T(8,128)(2,1)} %all-gather.3.cloned.1.call-done.w_ref.w_out, bf16[1024,800]{1,0:T(8,128)(2,1)} %get-tuple-element.78.s_ref), custom_call_target="tpu_custom_call" | custom-call | tf_op jit(solution)/shard_map/hidden_back/pallas_call | solution.py:1004
  208.7 9.1 %outer.1 = bf16[1600,800]{1,0:T(8,128)(2,1)} custom-call(bf16[1024,1600]{1,0:T(8,128)(2,1)} %bitcast.47, bf16[1024,800]{1,0:T(8,128)(2,1)} %get-tuple-element.86.y_ref.du), custom_call_target="tpu_custom_call" | custom-call | tf_op jit(solution)/shard_map/outer/pallas_call | solution.py:944
  217.8 54.5 %turn.1 = (bf16[8,4,32,1600]{3,2,1,0:T(8,128)(2,1)}, f32[128,1600]{1,0:T(8,128)}, bf16[128,1600]{1,0:T(8,128)(2,1)}, f32[8,1600]{1,0:T(8,128)}) custom-call(bf16[1024,800]{1,0:T(8,128)(2,1)} %get-tuple-element.86.y_ref.du, bf16[1600,800]{1,0:T(8,128)(2,1)} %all-gather.5.cloned.1.call-done.w_ref.w_fc, bf16[1024,800]{1,0:T(8,128)(2,1)} %get-tuple-element.75.hid, ...), custom_call_target="tpu_custom_call" | custom-call | tf_op jit(solution)/shard_map/turn/pallas_call | solution.py:734
  272.3 5.7 %heads_grad.1.do = bf16[1024,256]{1,0:T(8,128)(2,1)} custom-call(s32[16]{0:T(128)} %get-tuple-element.66.inv_ref.table, bf16[1024,1600]{1,0:T(8,128)(2,1)} %bitcast.44, bf16[256,1600]{1,0:T(8,128)(2,1)} %bitcast.51), custom_call_target="tpu_custom_call" | custom-call | tf_op jit(solution)/shard_map/heads_grad/pallas_call | solution.py:1163
  278.0 0.1 reshape.119
  278.1 0.5 dynamic_update_slice.11
  278.5 0.0 reduce-scatter.7.cloned.1.call-done
  278.6 35.4 %back.1 = (bf16[8,5,40,1600]{3,2,1,0:T(8,128)(2,1)}, bf16[1024,768]{1,0:T(8,128)(2,1)}, f32[1,768]{1,0:T(1,128)}, bf16[1600,896]{1,0:T(8,128)(2,1)}) custom-call(bf16[5,40,1600]{2,1,0:T(8,128)(2,1)} %bitcast.60, bf16[1024,256]{1,0:T(8,128)(2,1)} %get-tuple-element.82.q, bf16[1024,256]{1,0:T(8,128)(2,1)} %get-tuple-element.83.k, ...), custom_call_target="tpu_custom_call" | custom-call | tf_op jit(solution)/shard_map/back/pallas_call | solution.py:734
  314.1 2.8 order.3.dqkv
  317.0 0.0 reduce-scatter.5.cloned.1.call-done
  317.1 1.4 copy-done
  318.5 1.8 copy-done.1
  320.3 1.7 copy-done.2
  322.0 1.1 copy-done.6
  323.1 82.6 %tail.1 = (bf16[8,5,80,800]{3,2,1,0:T(8,128)(2,1)S(1)}, bf16[8,5,80,896]{3,2,1,0:T(8,128)(2,1)S(1)}, bf16[128,1600]{1,0:T(8,128)(2,1)S(1)}, f32[16,1600]{1,0:T(8,128)S(1)}) custom-call(bf16[5,80,800]{2,1,0:T(8,128)(2,1)S(1)} %bitcast.42, bf16[4,5,80,896]{3,2,1,0:T(8,128)(2,1)S(1)} %bitcast.39, bf16[1024,768]{1,0:T(8,128)(2,1)S(1)} %copy-done, ...), custom_call_target="tpu_custom_call" | custom-call | tf_op jit(solution)/shard_map/tail/pallas_call | solution.py:734
  405.7 15.8 %join.1 = (f32[400,6400]{1,0:T(8,128)}, f32[400,4800]{1,0:T(8,128)}, f32[400,1600]{1,0:T(8,128)}, f32[1600,1600]{1,0:T(8,128)}) custom-call(bf16[8,25,16,800]{3,2,1,0:T(8,128)(2,1)S(1)} %bitcast.34, bf16[8,25,16,896]{3,2,1,0:T(8,128)(2,1)S(1)} %bitcast.35, bf16[1600,1600]{1,0:T(8,128)(2,1)S(1)} %bitcast.38), custom_call_target="tpu_custom_call" | custom-call | tf_op jit(solution)/shard_map/join/pallas_call | solution.py:1047
  421.5 0.9 copy.41
  422.5 0.9 copy.42
  423.4 0.6 dynamic-slice_reduce_fusion
  424.1 0.7 fusion.2
  (66 shorter events, 0.3 us)
Async XLA Ops:
  7.2 3.2 copy-start.14
  7.2 3.2 copy-start.15
  7.2 3.2 copy-start.16
  7.2 3.1 copy-start.17
  7.2 3.1 copy-start.18
  7.2 3.1 copy-start.19
  7.2 3.1 copy-start.20
  7.3 3.1 copy-start.21
  7.3 143.8 %all-gather.5.cloned.1.call-start = ((), (), s32[]{:S(2)}) async-start(), calls=%async_computation.3 | async-start | bytes 3584000 | tf_op jit(solution)/shard_map/all_gather | solution.py:1390
  11.1 73.3 %copy-start.13 = (s32[8,2]{0,1:T(2,128)S(1)}, s32[8,2]{0,1:T(2,128)}, u32[]{:S(2)}) copy-start(s32[8,2]{0,1:T(2,128)} %param.17) | copy-start | bytes 196
  83.6 117.1 %all-gather.3.cloned.1.call-start = ((), (), s32[]{:S(2)}) async-start(), calls=%async_computation.2 | async-start | bytes 3328000 | tf_op jit(solution)/shard_map/all_gather | solution.py:1391
  84.4 194.2 %reduce-scatter.7.cloned.1.call-start = ((), (), s32[]{:S(2)}) async-start(), calls=%async_computation.5 | async-start | bytes 3328000
  84.6 9.9 %copy-start.11 = (s32[16]{0:T(128)}, s32[16]{0:T(128)S(1)}, u32[]{:S(2)}) copy-start(s32[16]{0:T(128)S(1)} %eq.98.table) | copy-start | bytes 196
  151.1 9.4 %copy-start.7 = (bf16[8,2,64,1600]{3,2,1,0:T(8,128)(2,1)S(1)}, bf16[8,2,64,1600]{3,2,1,0:T(8,128)(2,1)}, u32[]{:S(2)}) copy-start(bf16[8,2,64,1600]{3,2,1,0:T(8,128)(2,1)} %get-tuple-element.64) | copy-start | bytes 9830404
  166.7 150.3 %reduce-scatter.5.cloned.1.call-start = ((), (), s32[]{:S(2)}) async-start(), calls=%async_computation.4 | async-start | bytes 3584000 | tf_op jit(solution)/shard_map/reduce_scatter | solution.py:1411
  272.3 5.7 %copy-start.10 = (f32[1,800]{1,0:T(1,128)S(1)}, f32[1,800]{1,0:T(1,128)}, u32[]{:S(2)}) copy-start(f32[1,800]{1,0:T(1,128)} %get-tuple-element.98) | copy-start | bytes 9604
  314.0 2.9 copy-start.12
  314.0 2.9 copy-start.9
  314.0 3.0 copy-start.3
  314.0 3.0 copy-start.4
  314.1 3.0 copy-start.5
  314.1 91.6 %slice-start = ((s8[5324800]{0:T(1024)(128)(4,1)}), s8[1130496]{0:T(1024)(128)(4,1)S(1)}, s32[]{:S(2)}) async-start(s8[5324800]{0:T(1024)(128)(4,1)} %bitcast.36), calls=%async_computation.6 | async-start | bytes 2260992
  317.1 1.4 copy-start
  318.5 1.8 copy-start.1
  320.3 1.7 copy-start.2
  322.0 1.1 copy-start.6
  323.1 82.6 %slice-start.1 = ((s8[5324800]{0:T(1024)(128)(4,1)}), s8[4194304]{0:T(1024)(128)(4,1)S(1)}, s32[]{:S(2)}) async-start(s8[5324800]{0:T(1024)(128)(4,1)} %bitcast.36), calls=%async_computation.7 | async-start | bytes 8388608
  405.7 15.8 %copy-start.8 = (bf16[128,1600]{1,0:T(8,128)(2,1)S(1)}, bf16[128,1600]{1,0:T(8,128)(2,1)}, u32[]{:S(2)}) copy-start(bf16[128,1600]{1,0:T(8,128)(2,1)} %get-tuple-element.158) | copy-start | bytes 1228804
Sparse Core Ops, SparseCore 0:
  83.8 61.2 all-gather.4
  146.6 54.0 all-gather.2
  203.7 51.1 reduce-scatter.6
  257.6 56.5 reduce-scatter.4

commit v6 on v5

--- a/solution.py
+++ b/solution.py
@@ -13,7 +13,7 @@
 F32 = jnp.float32
 MESH = pl.DeviceIdType.MESH
 ENTRY, ATTEND, MIDDLE, SPREAD, TURN, BACK, TAIL = 60, 60, 60, 60, 60, 60, 30
-HIDDEN, HIDDEN_BACK, OUTER, ORDER, HEADS_GRAD, JOIN = 60, 60, 60, 60, 60, 8
+HIDDEN, HIDDEN_BACK, OUTER, ORDER, HEADS_GRAD, JOIN = 60, 60, 60, 9, 60, 8
 ANY = pl.BlockSpec(memory_space=pl.ANY)
 VMEM = pl.BlockSpec(memory_space=pltpu.VMEM)
 HBM = pl.BlockSpec(memory_space=pltpu.HBM)
@@ -803,7 +803,16 @@
     )[0]
 
 
-def turn_kernel(n, du, w_fc, hid, w_out, mid, cot, vec, da_all, dmid, layer, sums, da, *scratch):
+def turn_kernel(
+    n, du, w_fc, hid_in, w_out_in, mid_in, cot_in, vec, da_all, dmid, layer, sums,
+    da, hid, w_out, mid, cot, load_s, *scratch,
+):
+    loads = [
+        pltpu.make_async_copy(src, dst, load_s.at[i])
+        for i, (src, dst) in enumerate([(hid_in, hid), (w_out_in, w_out), (mid_in, mid), (cot_in, cot)])
+    ]
+    for load in loads:
+        load.start()
     greet(beside(n))
     back = Scatter(n, NT, du, w_fc, scratch[:8])
     ahead = Scatter(n, NN, hid, w_out, scratch[8:16])
@@ -812,6 +821,8 @@
     todo = back.forwards()
     for step in todo[: back.parts]:
         step()
+    for load in loads:
+        load.wait()
     ahead.products()
     for step in todo[back.parts :]:
         step()
@@ -846,10 +857,12 @@
         cid,
         "turn",
         (du, w_fc, hidden, w_out, mid, cot, vec),
-        [VMEM] * 7,
+        [VMEM] * 2 + [ANY] * 4 + [VMEM],
         [((n,) + piece, BF), ((rows, width), F32), ((rows, width), BF), ((8, width), F32)],
         [ANY, VMEM, VMEM, VMEM],
         [pltpu.VMEM(piece, BF)]
+        + [pltpu.VMEM(a.shape, a.dtype) for a in (hidden, w_out, mid, cot)]
+        + [pltpu.SemaphoreType.DMA((4,))]
         + Scatter.scratch(n, rows, width)
         + Scatter.scratch(n, rows, width)
         + Gather.sems(n, parts),

time: 436 us -> 433 us (level)
  Pallas kernels: 381 us -> 374 us
    pallas_call x2, Pallas kernels: 6.79 us -> 1.43 us  [order(): pl.pallas_call(functools.partial(order_kernel, table.shape[0], blk), out_...]
  transfers between devices with their start and end apart: 4 -> 4, of which waited for: 1 -> 1; matrix products, arithmetic and copies ran while one was open for 4% -> 4% of each run, Pallas kernels for 49% -> 47%
where the time goes in v6:
time: 433 us; the launch traced here: 428 us
  Pallas kernels  374 us (86%)
  local copies, waits for them, and re-layouts  16.2 us (4%)
  between operations  14.5 us (3%)
  matrix products  14.2 us (3%)
  waiting for transfers between devices  6.11 us (1%)
    pallas_call x5, Pallas kernels, call(): pl.pallas_call(kernel, out_shape=[jax.ShapeDtypeStruct(*o) for o in outs]...  239 us
    pallas_call x1, Pallas kernels, entry(): pl.pallas_call(functools.partial(entry_kernel, n, nz), out_shape=[shape((...  72.5 us
    pallas_call x1, Pallas kernels, join(): pl.pallas_call(functools.partial(join_kernel, n, nz, hw, width), grid=(ti...  15.8 us
    dot_general x2, matrix products, dot(): return lax.dot_general(a, b, dims, preferred_element_type=F32)  14.2 us
    pallas_call x1, Pallas kernels, attend(): pl.pallas_call(functools.partial(attend_kernel, blocks, blk, tile), out_s...  12.7 us
    unnamed x51, local copies, waits for them, and re-layouts  10.3 us
    pallas_call x1, Pallas kernels, hidden_units(): pl.pallas_call(hidden_kernel, grid=(rows // tile,), out_shape=[shape, sha...  9.25 us
    pallas_call x1, Pallas kernels, outer(): pl.pallas_call(outer_kernel, grid=(pl.cdiv(m, tile),), out_shape=jax.Shap...  9.08 us
  transfers between devices with their start and end apart: 4, of which 1 were waited for; matrix products, arithmetic and copies ran while one was open for 4% of the time, Pallas kernels for 47%

profile of v6, /device:TPU:0, one launch (start us, length us, event | category | flops | bytes accessed | tf_op | source)
XLA Modules:
  0.0 427.9 jit_solution(13060608691236990871)
XLA Ops:
  7.3 0.0 all-gather.5.cloned.1.call-start
  7.4 0.8 dynamic_slice.24
  8.2 1.3 pad_dynamic-slice_fusion.2
  9.5 0.9 pad_maximum_fusion
  10.4 0.7 select_select_fusion.small
  11.1 72.5 %entry.1 = (bf16[8,2,64,1600]{3,2,1,0:T(8,128)(2,1)}, bf16[8,2,64,1600]{3,2,1,0:T(8,128)(2,1)}, f32[16,1600]{1,0:T(8,128)}, bf16[20,80,768]{2,1,0:T(8,128)(2,1)}...) custom-call(bf16[1600,128]{1,0:T(8,128)(2,1)} %bitcast.59, ...), custom_call_target="tpu_custom_call" | custom-call | tf_op jit(solution)/shard_map/entry/pallas_call | solution.py:377
  83.7 0.0 all-gather.3.cloned.1.call-start
  83.7 0.7 all-gather.3.cloned.1.call-update
  84.4 0.0 reduce-scatter.7.cloned.1.call-start
  84.5 0.1 copy.40
  84.5 0.1 eq.98.table
  84.6 0.9 slice_reduce_fusion
  85.6 0.1 reshape_squeeze.3
  85.7 0.7 reshape.112.b_ref
  86.3 0.1 pad_dynamic-slice_fusion.3
  86.4 0.1 pad_dynamic-slice_fusion.4
  86.5 1.2 iota_reduce_fusion
  87.7 6.9 %add_convert_fusion.q_ref.k_ref.v_ref = bf16[1024,768]{1,0:T(8,128)(2,1)} fusion(bf16[1024,1600]{1,0:T(8,128)(2,1)} %bitcast.37, bf16[1600,768]{1,0:T(8,128)(2,1)} %bitcast.40, f32[768]{0:T(1024)S(1)} %pad_maximum_fusion.1), kind=kOutput, calls=%fused_computation.4 | convolution fusion | flops 2518155264 | bytes 7310336 | tf_op jit(solution)/shard_map/dot_general | solution.py:30
  94.5 12.7 %attend.1 = (bf16[1024,256]{1,0:T(8,128)(2,1)}, bf16[4,1024,1024]{2,1,0:T(8,128)(2,1)}, bf16[1024,256]{1,0:T(8,128)(2,1)}, bf16[1024,256]{1,0:T(8,128)(2,1)}, bf...) custom-call(s32[16]{0:T(128)} %get-tuple-element.66.inv_ref.table, ...), custom_call_target="tpu_custom_call" | custom-call | tf_op jit(solution)/shard_map/attend/pallas_call | solution.py:1121
  107.2 43.8 %middle.1 = (f32[128,1600]{1,0:T(8,128)}, bf16[8,4,32,1600]{3,2,1,0:T(8,128)(2,1)}) custom-call(bf16[1024,256]{1,0:T(8,128)(2,1)} %get-tuple-element.76.o, bf16[256,1600]{1,0:T(8,128)(2,1)} %bitcast.50, bf16[128,1600]{1,0:T(8,128)(2,1)} %get-tuple-element.72.tok, f32[16,1600]{1,0:T(8,128)} %get-tuple-element.69.vec), custom_call_target="tpu_custom_call" | custom-call | tf_op jit(solution)/shard_map/middle/pallas_call | solution.py:734
  151.1 9.2 %hidden.1 = (bf16[1024,800]{1,0:T(8,128)(2,1)}, bf16[1024,800]{1,0:T(8,128)(2,1)}) custom-call(bf16[1024,1600]{1,0:T(8,128)(2,1)} %bitcast.46, bf16[1600,800]{1,0:T(8,128)(2,1)} %all-gather.5.cloned.1.call-done.w_ref.w_fc, f32[1,800]{1,0:T(1,128)} %reshape.112.b_ref), custom_call_target="tpu_custom_call" | custom-call | tf_op jit(solution)/shard_map/hidden/pallas_call | solution.py:1002
  160.4 7.4 %convolution_convert_fusion = bf16[800,1600]{1,0:T(8,128)(2,1)} fusion(bf16[1024,800]{1,0:T(8,128)(2,1)} %get-tuple-element.75.hid_in, bf16[1024,1600]{1,0:T(8,128)(2,1)} %bitcast.52), kind=kOutput, calls=%fused_computation.3 | convolution fusion | flops 2622720000 | bytes 7475200 | tf_op jit(solution)/shard_map/dot_general | solution.py:30
  167.7 0.2 reduce-scatter.5.cloned.1.call-start
  168.0 0.8 order.2.h1_hbm
  168.8 1.7 copy-done
  170.5 24.9 %spread.1 = bf16[8,4,256,256]{3,2,1,0:T(8,128)(2,1)} custom-call(bf16[4,256,256]{2,1,0:T(8,128)(2,1)} %bitcast.55), custom_call_target="tpu_custom_call" | custom-call | tf_op jit(solution)/shard_map/spread/pallas_call | solution.py:734
  195.5 5.3 %all-gather.3.cloned.1.call-done.w_ref.w_out_in = bf16[800,1600]{1,0:T(8,128)(2,1)} async-done(((bf16[200,1600]{1,0:T(8,128)(2,1)}), bf16[800,1600]{1,0:T(8,128)(2,1)}) %all-gather.3.cloned.1.call-update) | async-done | bytes 2560016 | tf_op jit(solution)/shard_map/all_gather | solution.py:1404
  200.8 7.9 %hidden_back.1 = (bf16[1024,800]{1,0:T(8,128)(2,1)}, f32[1,800]{1,0:T(1,128)}) custom-call(bf16[1024,1600]{1,0:T(8,128)(2,1)} %bitcast.53, bf16[800,1600]{1,0:T(8,128)(2,1)} %all-gather.3.cloned.1.call-done.w_ref.w_out_in, bf16[1024,800]{1,0:T(8,128)(2,1)} %get-tuple-element.78.s_ref), custom_call_target="tpu_custom_call" | custom-call | tf_op jit(solution)/shard_map/hidden_back/pallas_call | solution.py:1017
  208.7 9.1 %outer.1 = bf16[1600,800]{1,0:T(8,128)(2,1)} custom-call(bf16[1024,1600]{1,0:T(8,128)(2,1)} %bitcast.47, bf16[1024,800]{1,0:T(8,128)(2,1)} %get-tuple-element.86.y_ref.du), custom_call_target="tpu_custom_call" | custom-call | tf_op jit(solution)/shard_map/outer/pallas_call | solution.py:957
  217.8 52.9 %turn.1 = (bf16[8,4,32,1600]{3,2,1,0:T(8,128)(2,1)}, f32[128,1600]{1,0:T(8,128)}, bf16[128,1600]{1,0:T(8,128)(2,1)}, f32[8,1600]{1,0:T(8,128)}) custom-call(bf16[1024,800]{1,0:T(8,128)(2,1)} %get-tuple-element.86.y_ref.du, bf16[1600,800]{1,0:T(8,128)(2,1)} %all-gather.5.cloned.1.call-done.w_ref.w_fc, bf16[1024,800]{1,0:T(8,128)(2,1)} %get-tuple-element.75.hid_in, ...), custom_call_target="tpu_custom_call" | custom-call | tf_op jit(solution)/shard_map/turn/pallas_call | solution.py:734
  270.7 5.7 %heads_grad.1.do = bf16[1024,256]{1,0:T(8,128)(2,1)} custom-call(s32[16]{0:T(128)} %get-tuple-element.66.inv_ref.table, bf16[1024,1600]{1,0:T(8,128)(2,1)} %bitcast.44, bf16[256,1600]{1,0:T(8,128)(2,1)} %bitcast.51), custom_call_target="tpu_custom_call" | custom-call | tf_op jit(solution)/shard_map/heads_grad/pallas_call | solution.py:1176
  276.4 0.1 reshape.119
  276.5 0.5 dynamic_update_slice.11
  277.0 35.5 %back.1 = (bf16[8,5,40,1600]{3,2,1,0:T(8,128)(2,1)}, bf16[1024,768]{1,0:T(8,128)(2,1)}, f32[1,768]{1,0:T(1,128)}, bf16[1600,896]{1,0:T(8,128)(2,1)}) custom-call(bf16[5,40,1600]{2,1,0:T(8,128)(2,1)} %bitcast.58, bf16[1024,256]{1,0:T(8,128)(2,1)} %get-tuple-element.82.q, bf16[1024,256]{1,0:T(8,128)(2,1)} %get-tuple-element.83.k, ...), custom_call_target="tpu_custom_call" | custom-call | tf_op jit(solution)/shard_map/back/pallas_call | solution.py:734
  312.6 1.5 copy-done.6
  314.0 0.6 order.3.dqkv
  314.8 0.1 copy-done.12
  314.9 0.0 copy-done.7
  314.9 0.3 copy-done.8
  315.3 1.8 copy-done.3
  317.1 1.7 copy-done.4
  318.8 1.1 copy-done.9
  319.9 82.1 %tail.1 = (bf16[8,5,80,800]{3,2,1,0:T(8,128)(2,1)S(1)}, bf16[8,5,80,896]{3,2,1,0:T(8,128)(2,1)S(1)}, bf16[128,1600]{1,0:T(8,128)(2,1)S(1)}, f32[16,1600]{1,0:T(8,128)S(1)}) custom-call(bf16[5,80,800]{2,1,0:T(8,128)(2,1)S(1)} %bitcast.42, bf16[4,5,80,896]{3,2,1,0:T(8,128)(2,1)S(1)} %bitcast.39, bf16[1024,768]{1,0:T(8,128)(2,1)S(1)} %order.3.dqkv, ...), custom_call_target="tpu_custom_call" | custom-call | tf_op jit(solution)/shard_map/tail/pallas_call | solution.py:734
  402.0 15.8 %join.1 = (f32[400,6400]{1,0:T(8,128)}, f32[400,4800]{1,0:T(8,128)}, f32[400,1600]{1,0:T(8,128)}, f32[1600,1600]{1,0:T(8,128)}) custom-call(bf16[8,25,16,800]{3,2,1,0:T(8,128)(2,1)S(1)} %bitcast.34, bf16[8,25,16,896]{3,2,1,0:T(8,128)(2,1)S(1)} %bitcast.35, bf16[1600,1600]{1,0:T(8,128)(2,1)S(1)} %bitcast.36), custom_call_target="tpu_custom_call" | custom-call | tf_op jit(solution)/shard_map/join/pallas_call | solution.py:1060
  417.9 0.9 copy.41
  418.8 0.9 copy.42
  419.8 0.6 dynamic-slice_reduce_fusion
  420.4 0.7 fusion.2
  (65 shorter events, 0.4 us)
Async XLA Ops:
  7.2 3.2 copy-start.16
  7.2 3.2 copy-start.17
  7.2 3.2 copy-start.18
  7.2 3.1 copy-start.19
  7.2 3.1 copy-start.20
  7.2 3.1 copy-start.21
  7.2 3.1 copy-start.22
  7.3 3.1 copy-start.23
  7.3 143.8 %all-gather.5.cloned.1.call-start = ((), (), s32[]{:S(2)}) async-start(), calls=%async_computation.3 | async-start | bytes 3584000 | tf_op jit(solution)/shard_map/all_gather | solution.py:1403
  11.1 73.4 %copy-start.15 = (s32[8,2]{0,1:T(2,128)S(1)}, s32[8,2]{0,1:T(2,128)}, u32[]{:S(2)}) copy-start(s32[8,2]{0,1:T(2,128)} %param.17) | copy-start | bytes 196
  83.7 117.1 %all-gather.3.cloned.1.call-start = ((), (), s32[]{:S(2)}) async-start(), calls=%async_computation.2 | async-start | bytes 3328000 | tf_op jit(solution)/shard_map/all_gather | solution.py:1404
  84.4 192.6 %reduce-scatter.7.cloned.1.call-start = ((), (), s32[]{:S(2)}) async-start(), calls=%async_computation.5 | async-start | bytes 3328000
  160.3 7.6 %copy-start.2 = (bf16[8,2,64,1600]{3,2,1,0:T(8,128)(2,1)S(1)}, bf16[8,2,64,1600]{3,2,1,0:T(8,128)(2,1)}, u32[]{:S(2)}) copy-start(bf16[8,2,64,1600]{3,2,1,0:T(8,128)(2,1)} %get-tuple-element.67) | copy-start | bytes 9830404
  160.3 7.6 %copy-start.10 = (s32[16]{0:T(128)S(1)}, s32[16]{0:T(128)}, u32[]{:S(2)}) copy-start(s32[16]{0:T(128)} %get-tuple-element.66.inv_ref.table) | copy-start | bytes 196
  167.7 147.2 %reduce-scatter.5.cloned.1.call-start = ((), (), s32[]{:S(2)}) async-start(), calls=%async_computation.4 | async-start | bytes 3584000 | tf_op jit(solution)/shard_map/reduce_scatter | solution.py:1424
  168.8 1.8 copy-start
  270.7 5.7 %copy-start.13 = (f32[1,800]{1,0:T(1,128)S(1)}, f32[1,800]{1,0:T(1,128)}, u32[]{:S(2)}) copy-start(f32[1,800]{1,0:T(1,128)} %get-tuple-element.98) | copy-start | bytes 9604
  312.6 2.4 copy-start.5
  312.6 1.5 copy-start.6
  314.0 0.7 copy-start.14
  314.0 0.8 copy-start.12
  314.0 0.9 copy-start.7
  314.0 1.2 copy-start.8
  315.3 1.8 copy-start.3
  317.1 1.7 copy-start.4
  318.8 1.1 copy-start.9
  319.9 82.1 %copy-start.1 = (bf16[8,5,40,1600]{3,2,1,0:T(8,128)(2,1)S(1)}, bf16[8,5,40,1600]{3,2,1,0:T(8,128)(2,1)}, u32[]{:S(2)}) copy-start(bf16[8,5,40,1600]{3,2,1,0:T(8,128)(2,1)} %get-tuple-element.104) | copy-start | bytes 15360004
  402.0 15.8 %copy-start.11 = (bf16[128,1600]{1,0:T(8,128)(2,1)S(1)}, bf16[128,1600]{1,0:T(8,128)(2,1)}, u32[]{:S(2)}) copy-start(bf16[128,1600]{1,0:T(8,128)(2,1)} %get-tuple-element.158) | copy-start | bytes 1228804
Sparse Core Ops, SparseCore 0:
  83.8 61.2 all-gather.4
  146.6 54.0 all-gather.2
  203.7 51.1 reduce-scatter.6
  257.6 56.5 reduce-scatter.4

commit v7 on v6

--- a/solution.py
+++ b/solution.py
@@ -1013,7 +1013,7 @@
 def hidden_back(cot, w_out, slope):
     rows, width = cot.shape
     units = w_out.shape[0]
-    tile = 256
+    tile = 512
     return pl.pallas_call(
         hidden_back_kernel,
         grid=(rows // tile,),
@@ -1172,7 +1172,7 @@
 def heads_grad(da, w_proj, table, blk):
     length, width = da.shape
     cols = w_proj.shape[0]
-    tile = 256
+    tile = 512
     return pl.pallas_call(
         functools.partial(heads_kernel, table.shape[0], blk, tile),
         out_shape=jax.ShapeDtypeStruct((length, cols), BF),

time: 433 us -> 432 us (level)
  no operation moved by 1% of the time
where the time goes in v7:
time: 432 us; the launch traced here: 427 us
  Pallas kernels  373 us (86%)
  local copies, waits for them, and re-layouts  16.3 us (4%)
  between operations  14.5 us (3%)
  matrix products  14.2 us (3%)
  waiting for transfers between devices  6.11 us (1%)
    pallas_call x5, Pallas kernels, call(): pl.pallas_call(kernel, out_shape=[jax.ShapeDtypeStruct(*o) for o in outs]...  239 us
    pallas_call x1, Pallas kernels, entry(): pl.pallas_call(functools.partial(entry_kernel, n, nz), out_shape=[shape((...  72.5 us
    pallas_call x1, Pallas kernels, join(): pl.pallas_call(functools.partial(join_kernel, n, nz, hw, width), grid=(ti...  15.8 us
    dot_general x2, matrix products, dot(): return lax.dot_general(a, b, dims, preferred_element_type=F32)  14.2 us
    pallas_call x1, Pallas kernels, attend(): pl.pallas_call(functools.partial(attend_kernel, blocks, blk, tile), out_s...  12.7 us
    unnamed x51, local copies, waits for them, and re-layouts  10.3 us
    pallas_call x1, Pallas kernels, hidden_units(): pl.pallas_call(hidden_kernel, grid=(rows // tile,), out_shape=[shape, sha...  9.25 us
    pallas_call x1, Pallas kernels, outer(): pl.pallas_call(outer_kernel, grid=(pl.cdiv(m, tile),), out_shape=jax.Shap...  9 us
  transfers between devices with their start and end apart: 4, of which 1 were waited for; matrix products, arithmetic and copies ran while one was open for 4% of the time, Pallas kernels for 47%

profile of v7, /device:TPU:0, one launch (start us, length us, event | category | flops | bytes accessed | tf_op | source)
XLA Modules:
  0.0 427.3 jit_solution(10705008949232178835)
XLA Ops:
  7.3 0.0 all-gather.5.cloned.1.call-start
  7.4 0.8 dynamic_slice.24
  8.2 1.3 pad_dynamic-slice_fusion.2
  9.5 0.9 pad_maximum_fusion
  10.4 0.7 select_select_fusion.small
  11.1 72.5 %entry.1 = (bf16[8,2,64,1600]{3,2,1,0:T(8,128)(2,1)}, bf16[8,2,64,1600]{3,2,1,0:T(8,128)(2,1)}, f32[16,1600]{1,0:T(8,128)}, bf16[20,80,768]{2,1,0:T(8,128)(2,1)}...) custom-call(bf16[1600,128]{1,0:T(8,128)(2,1)} %bitcast.59, ...), custom_call_target="tpu_custom_call" | custom-call | tf_op jit(solution)/shard_map/entry/pallas_call | solution.py:377
  83.7 0.0 all-gather.3.cloned.1.call-start
  83.7 0.7 all-gather.3.cloned.1.call-update
  84.4 0.0 reduce-scatter.7.cloned.1.call-start
  84.5 0.1 copy.40
  84.5 0.1 eq.98.table
  84.6 0.9 slice_reduce_fusion
  85.6 0.1 reshape_squeeze.3
  85.7 0.7 reshape.112.b_ref
  86.3 0.1 pad_dynamic-slice_fusion.3
  86.4 0.1 pad_dynamic-slice_fusion.4
  86.5 1.2 iota_reduce_fusion
  87.7 6.9 %add_convert_fusion.q_ref.k_ref.v_ref = bf16[1024,768]{1,0:T(8,128)(2,1)} fusion(bf16[1024,1600]{1,0:T(8,128)(2,1)} %bitcast.37, bf16[1600,768]{1,0:T(8,128)(2,1)} %bitcast.40, f32[768]{0:T(1024)S(1)} %pad_maximum_fusion.1), kind=kOutput, calls=%fused_computation.4 | convolution fusion | flops 2518155264 | bytes 7310336 | tf_op jit(solution)/shard_map/dot_general | solution.py:30
  94.5 12.7 %attend.1 = (bf16[1024,256]{1,0:T(8,128)(2,1)}, bf16[4,1024,1024]{2,1,0:T(8,128)(2,1)}, bf16[1024,256]{1,0:T(8,128)(2,1)}, bf16[1024,256]{1,0:T(8,128)(2,1)}, bf...) custom-call(s32[16]{0:T(128)} %get-tuple-element.66.inv_ref.table, ...), custom_call_target="tpu_custom_call" | custom-call | tf_op jit(solution)/shard_map/attend/pallas_call | solution.py:1121
  107.2 43.8 %middle.1 = (f32[128,1600]{1,0:T(8,128)}, bf16[8,4,32,1600]{3,2,1,0:T(8,128)(2,1)}) custom-call(bf16[1024,256]{1,0:T(8,128)(2,1)} %get-tuple-element.76.o, bf16[256,1600]{1,0:T(8,128)(2,1)} %bitcast.50, bf16[128,1600]{1,0:T(8,128)(2,1)} %get-tuple-element.72.tok, f32[16,1600]{1,0:T(8,128)} %get-tuple-element.69.vec), custom_call_target="tpu_custom_call" | custom-call | tf_op jit(solution)/shard_map/middle/pallas_call | solution.py:734
  151.1 9.2 %hidden.1 = (bf16[1024,800]{1,0:T(8,128)(2,1)}, bf16[1024,800]{1,0:T(8,128)(2,1)}) custom-call(bf16[1024,1600]{1,0:T(8,128)(2,1)} %bitcast.46, bf16[1600,800]{1,0:T(8,128)(2,1)} %all-gather.5.cloned.1.call-done.w_ref.w_fc, f32[1,800]{1,0:T(1,128)} %reshape.112.b_ref), custom_call_target="tpu_custom_call" | custom-call | tf_op jit(solution)/shard_map/hidden/pallas_call | solution.py:1002
  160.4 7.4 %convolution_convert_fusion = bf16[800,1600]{1,0:T(8,128)(2,1)} fusion(bf16[1024,800]{1,0:T(8,128)(2,1)} %get-tuple-element.75.hid_in, bf16[1024,1600]{1,0:T(8,128)(2,1)} %bitcast.52), kind=kOutput, calls=%fused_computation.3 | convolution fusion | flops 2622720000 | bytes 7475200 | tf_op jit(solution)/shard_map/dot_general | solution.py:30
  167.7 0.2 reduce-scatter.5.cloned.1.call-start
  168.0 0.8 order.2.h1_hbm
  168.8 1.7 copy-done
  170.5 24.9 %spread.1 = bf16[8,4,256,256]{3,2,1,0:T(8,128)(2,1)} custom-call(bf16[4,256,256]{2,1,0:T(8,128)(2,1)} %bitcast.55), custom_call_target="tpu_custom_call" | custom-call | tf_op jit(solution)/shard_map/spread/pallas_call | solution.py:734
  195.5 5.3 %all-gather.3.cloned.1.call-done.w_ref.w_out_in = bf16[800,1600]{1,0:T(8,128)(2,1)} async-done(((bf16[200,1600]{1,0:T(8,128)(2,1)}), bf16[800,1600]{1,0:T(8,128)(2,1)}) %all-gather.3.cloned.1.call-update) | async-done | bytes 2560016 | tf_op jit(solution)/shard_map/all_gather | solution.py:1404
  200.8 8.2 %hidden_back.1 = (bf16[1024,800]{1,0:T(8,128)(2,1)}, f32[1,800]{1,0:T(1,128)}) custom-call(bf16[1024,1600]{1,0:T(8,128)(2,1)} %bitcast.53, bf16[800,1600]{1,0:T(8,128)(2,1)} %all-gather.3.cloned.1.call-done.w_ref.w_out_in, bf16[1024,800]{1,0:T(8,128)(2,1)} %get-tuple-element.78.s_ref), custom_call_target="tpu_custom_call" | custom-call | tf_op jit(solution)/shard_map/hidden_back/pallas_call | solution.py:1017
  209.0 9.0 %outer.1 = bf16[1600,800]{1,0:T(8,128)(2,1)} custom-call(bf16[1024,1600]{1,0:T(8,128)(2,1)} %bitcast.47, bf16[1024,800]{1,0:T(8,128)(2,1)} %get-tuple-element.86.y_ref.du), custom_call_target="tpu_custom_call" | custom-call | tf_op jit(solution)/shard_map/outer/pallas_call | solution.py:957
  218.0 52.9 %turn.1 = (bf16[8,4,32,1600]{3,2,1,0:T(8,128)(2,1)}, f32[128,1600]{1,0:T(8,128)}, bf16[128,1600]{1,0:T(8,128)(2,1)}, f32[8,1600]{1,0:T(8,128)}) custom-call(bf16[1024,800]{1,0:T(8,128)(2,1)} %get-tuple-element.86.y_ref.du, bf16[1600,800]{1,0:T(8,128)(2,1)} %all-gather.5.cloned.1.call-done.w_ref.w_fc, bf16[1024,800]{1,0:T(8,128)(2,1)} %get-tuple-element.75.hid_in, ...), custom_call_target="tpu_custom_call" | custom-call | tf_op jit(solution)/shard_map/turn/pallas_call | solution.py:734
  271.0 4.7 %heads_grad.1.do = bf16[1024,256]{1,0:T(8,128)(2,1)} custom-call(s32[16]{0:T(128)} %get-tuple-element.66.inv_ref.table, bf16[1024,1600]{1,0:T(8,128)(2,1)} %bitcast.44, bf16[256,1600]{1,0:T(8,128)(2,1)} %bitcast.51), custom_call_target="tpu_custom_call" | custom-call | tf_op jit(solution)/shard_map/heads_grad/pallas_call | solution.py:1176
  275.7 0.1 reshape.119
  275.8 0.5 dynamic_update_slice.11
  276.3 35.5 %back.1 = (bf16[8,5,40,1600]{3,2,1,0:T(8,128)(2,1)}, bf16[1024,768]{1,0:T(8,128)(2,1)}, f32[1,768]{1,0:T(1,128)}, bf16[1600,896]{1,0:T(8,128)(2,1)}) custom-call(bf16[5,40,1600]{2,1,0:T(8,128)(2,1)} %bitcast.58, bf16[1024,256]{1,0:T(8,128)(2,1)} %get-tuple-element.82.q, bf16[1024,256]{1,0:T(8,128)(2,1)} %get-tuple-element.83.k, ...), custom_call_target="tpu_custom_call" | custom-call | tf_op jit(solution)/shard_map/back/pallas_call | solution.py:734
  311.9 1.5 copy-done.6
  313.3 0.6 order.3.dqkv
  314.1 0.1 copy-done.12
  314.2 0.0 copy-done.7
  314.3 0.3 copy-done.8
  314.6 1.8 copy-done.3
  316.4 1.7 copy-done.4
  318.1 1.1 copy-done.9
  319.2 82.2 %tail.1 = (bf16[8,5,80,800]{3,2,1,0:T(8,128)(2,1)S(1)}, bf16[8,5,80,896]{3,2,1,0:T(8,128)(2,1)S(1)}, bf16[128,1600]{1,0:T(8,128)(2,1)S(1)}, f32[16,1600]{1,0:T(8,128)S(1)}) custom-call(bf16[5,80,800]{2,1,0:T(8,128)(2,1)S(1)} %bitcast.42, bf16[4,5,80,896]{3,2,1,0:T(8,128)(2,1)S(1)} %bitcast.39, bf16[1024,768]{1,0:T(8,128)(2,1)S(1)} %order.3.dqkv, ...), custom_call_target="tpu_custom_call" | custom-call | tf_op jit(solution)/shard_map/tail/pallas_call | solution.py:734
  401.5 15.8 %join.1 = (f32[400,6400]{1,0:T(8,128)}, f32[400,4800]{1,0:T(8,128)}, f32[400,1600]{1,0:T(8,128)}, f32[1600,1600]{1,0:T(8,128)}) custom-call(bf16[8,25,16,800]{3,2,1,0:T(8,128)(2,1)S(1)} %bitcast.34, bf16[8,25,16,896]{3,2,1,0:T(8,128)(2,1)S(1)} %bitcast.35, bf16[1600,1600]{1,0:T(8,128)(2,1)S(1)} %bitcast.36), custom_call_target="tpu_custom_call" | custom-call | tf_op jit(solution)/shard_map/join/pallas_call | solution.py:1060
  417.3 0.9 copy.41
  418.2 0.9 copy.42
  419.2 0.6 dynamic-slice_reduce_fusion
  419.8 0.7 fusion.2
  (65 shorter events, 0.4 us)
Async XLA Ops:
  7.2 3.2 copy-start.16
  7.2 3.2 copy-start.17
  7.2 3.2 copy-start.18
  7.2 3.1 copy-start.19
  7.2 3.1 copy-start.20
  7.2 3.1 copy-start.21
  7.2 3.1 copy-start.22
  7.3 3.1 copy-start.23
  7.3 143.8 %all-gather.5.cloned.1.call-start = ((), (), s32[]{:S(2)}) async-start(), calls=%async_computation.3 | async-start | bytes 3584000 | tf_op jit(solution)/shard_map/all_gather | solution.py:1403
  11.1 73.4 %copy-start.15 = (s32[8,2]{0,1:T(2,128)S(1)}, s32[8,2]{0,1:T(2,128)}, u32[]{:S(2)}) copy-start(s32[8,2]{0,1:T(2,128)} %param.17) | copy-start | bytes 196
  83.7 117.1 %all-gather.3.cloned.1.call-start = ((), (), s32[]{:S(2)}) async-start(), calls=%async_computation.2 | async-start | bytes 3328000 | tf_op jit(solution)/shard_map/all_gather | solution.py:1404
  84.4 191.9 %reduce-scatter.7.cloned.1.call-start = ((), (), s32[]{:S(2)}) async-start(), calls=%async_computation.5 | async-start | bytes 3328000
  160.3 7.6 %copy-start.2 = (bf16[8,2,64,1600]{3,2,1,0:T(8,128)(2,1)S(1)}, bf16[8,2,64,1600]{3,2,1,0:T(8,128)(2,1)}, u32[]{:S(2)}) copy-start(bf16[8,2,64,1600]{3,2,1,0:T(8,128)(2,1)} %get-tuple-element.67) | copy-start | bytes 9830404
  160.3 7.6 %copy-start.10 = (s32[16]{0:T(128)S(1)}, s32[16]{0:T(128)}, u32[]{:S(2)}) copy-start(s32[16]{0:T(128)} %get-tuple-element.66.inv_ref.table) | copy-start | bytes 196
  167.7 146.5 %reduce-scatter.5.cloned.1.call-start = ((), (), s32[]{:S(2)}) async-start(), calls=%async_computation.4 | async-start | bytes 3584000 | tf_op jit(solution)/shard_map/reduce_scatter | solution.py:1424
  168.8 1.8 copy-start
  271.0 4.7 %copy-start.13 = (f32[1,800]{1,0:T(1,128)S(1)}, f32[1,800]{1,0:T(1,128)}, u32[]{:S(2)}) copy-start(f32[1,800]{1,0:T(1,128)} %get-tuple-element.98) | copy-start | bytes 9604
  311.8 2.4 copy-start.5
  311.9 1.5 copy-start.6
  313.3 0.7 copy-start.14
  313.3 0.8 copy-start.12
  313.3 0.9 copy-start.7
  313.3 1.3 copy-start.8
  314.6 1.8 copy-start.3
  316.4 1.7 copy-start.4
  318.1 1.1 copy-start.9
  319.2 82.2 %copy-start.1 = (bf16[8,5,40,1600]{3,2,1,0:T(8,128)(2,1)S(1)}, bf16[8,5,40,1600]{3,2,1,0:T(8,128)(2,1)}, u32[]{:S(2)}) copy-start(bf16[8,5,40,1600]{3,2,1,0:T(8,128)(2,1)} %get-tuple-element.104) | copy-start | bytes 15360004
  401.5 15.8 %copy-start.11 = (bf16[128,1600]{1,0:T(8,128)(2,1)S(1)}, bf16[128,1600]{1,0:T(8,128)(2,1)}, u32[]{:S(2)}) copy-start(bf16[128,1600]{1,0:T(8,128)(2,1)} %get-tuple-element.158) | copy-start | bytes 1228804
Sparse Core Ops, SparseCore 0:
  83.8 61.2 all-gather.4
  146.6 54.0 all-gather.2
  203.7 51.1 reduce-scatter.6
  257.6 56.4 reduce-scatter.4
